TPU v7x, 32 devices: a whole 2x2x4 slice. The times are simulated.
32 devices in a mesh: rep: 8 (over y, x, core), shard: 4 (over z).
Axes of the slice: x: 2, y: 2, z: 4, core: 2. Of those that a mesh axis runs over, the one named last changes fastest.
Arguments:
- tokens: bfloat16 [8192, 1024], P(('rep', 'shard')), may hold values from -6 to 6
- in_proj: bfloat16 [1024, 3072], P('shard'), may hold values from -0.1875 to 0.1875
- in_bias: bfloat16 [3072], P('shard'), may hold values from -3 to 3
- out_proj: bfloat16 [1024, 1024], P('shard'), may hold values from -1.5 to 1.5
- out_bias: bfloat16 [1024], P('shard'), may hold values from -3 to 3
- up_proj: bfloat16 [1024, 4096], P('shard'), may hold values from -0.1875 to 0.1875
- up_bias: bfloat16 [4096], P('shard'), may hold values from -3 to 3
- down_proj: bfloat16 [4096, 1024], P('shard'), may hold values from -0.09375 to 0.09375
- down_bias: bfloat16 [1024], P('shard'), may hold values from -3 to 3
- first_gain: bfloat16 [1024], P('shard'), may hold values from 0.5 to 1.5
- first_shift: bfloat16 [1024], P('shard'), may hold values from -3 to 3
- second_gain: bfloat16 [1024], P('shard'), may hold values from 0.5 to 1.5
- second_shift: bfloat16 [1024], P('shard'), may hold values from -3 to 3
- cotangent: bfloat16 [8192, 1024], P(('rep', 'shard')), may hold values from -6 to 6
Outputs:
- mixed: bfloat16 [8192, 1024], P(('rep', 'shard'))
- tokens_grad: float32 [8192, 1024], P(('rep', 'shard'))
- in_proj_grad: float32 [1024, 3072], P('shard')
- in_bias_grad: float32 [3072], P('shard')
- out_proj_grad: float32 [1024, 1024], P('shard')
- out_bias_grad: float32 [1024], P('shard')
- up_proj_grad: float32 [1024, 4096], P('shard')
- up_bias_grad: float32 [4096], P('shard')
- down_proj_grad: float32 [4096, 1024], P('shard')
- down_bias_grad: float32 [1024], P('shard')
- first_gain_grad: float32 [1024], P('shard')
- first_shift_grad: float32 [1024], P('shard')
- second_gain_grad: float32 [1024], P('shard')
- second_shift_grad: float32 [1024], P('shard')
All inputs are finite; a program needn't handle non-finite values.
Results may differ from a plain program's by a relative error of at most 0.012.
Values may be sent and summed in bfloat16 or wider, within the bound.
A program may use at most 192 MiB of HBM per device.

v0:
```python
import jax
import jax.numpy as jnp
from jax import lax
from jax.sharding import PartitionSpec as P

D = 1024
FF = 4096
HEADS = 16
HEAD_DIM = 64
ROT = 16


epsilon = 1e-05
masked_value = -1e30


def layer_norm_apply(values, gain, shift):
    average = jnp.mean(values, axis=1, keepdims=True)
    centred = values - average
    inv_scale = lax.rsqrt(jnp.mean(centred * centred, axis=1, keepdims=True) + epsilon)
    normal = centred * inv_scale
    return (normal * gain + shift, normal, inv_scale)


def layer_norm_reverse(grad, normal, inv_scale, gain):
    scaled = grad * gain
    return inv_scale * (
        scaled
        - jnp.mean(scaled, axis=1, keepdims=True)
        - normal * jnp.mean(scaled * normal, axis=1, keepdims=True)
    )


def rotary_tables(length):
    half = ROT // 2
    inverse = jnp.exp(-jnp.log(10000.0) * (2.0 * jnp.arange(half, dtype=jnp.float32) / ROT))
    angles = jnp.arange(length, dtype=jnp.float32)[:, None] * inverse[None, :]
    return (jnp.cos(angles)[:, None, :], jnp.sin(angles)[:, None, :])


def rotate(values, cosine, sine, sign):
    half = ROT // 2
    first = values[..., :half]
    second = values[..., half:ROT]
    return jnp.concatenate(
        [
            first * cosine - sign * second * sine,
            second * cosine + sign * first * sine,
            values[..., ROT:],
        ],
        axis=-1,
    )


def matmul(left, right):
    return jnp.dot(left, right, preferred_element_type=jnp.float32)


def matmul_trans(left, right):
    return lax.dot_general(
        left, right, (((1,), (1,)), ((), ())), preferred_element_type=jnp.float32
    )


def matmul_left_trans(left, right):
    return lax.dot_general(
        left, right, (((0,), (0,)), ((), ())), preferred_element_type=jnp.float32
    )


def masked_scores(query, keys, causal, scale):
    scores = jnp.einsum("qhd,khd->hqk", query, keys, preferred_element_type=jnp.float32) * scale
    return jnp.where(causal[None], scores, masked_value)


def on_device(
    tokens,
    in_proj,
    in_bias,
    out_proj,
    out_bias,
    up_proj,
    up_bias,
    down_proj,
    down_bias,
    first_gain,
    first_shift,
    second_gain,
    second_shift,
    cotangent,
):
    length = tokens.shape[0]
    width = tokens.shape[1]
    ratio = FF // D
    scale = HEAD_DIM ** (-0.5)
    gathered = (
        lax.all_gather(in_bias, "shard", axis=0, tiled=True),
        lax.all_gather(out_bias, "shard", axis=0, tiled=True),
        lax.all_gather(up_bias, "shard", axis=0, tiled=True),
        lax.all_gather(down_bias, "shard", axis=0, tiled=True),
        lax.all_gather(first_gain, "shard", axis=0, tiled=True),
        lax.all_gather(first_shift, "shard", axis=0, tiled=True),
        lax.all_gather(second_gain, "shard", axis=0, tiled=True),
        lax.all_gather(second_shift, "shard", axis=0, tiled=True),
    )
    in_bias_all, out_bias_all, up_bias_all, down_bias_all = [
        v.astype(jnp.float32) for v in gathered[:4]
    ]
    first_norm_gain, first_norm_shift, second_norm_gain, second_norm_shift = [
        v.astype(jnp.float32) for v in gathered[4:]
    ]
    block_inputs = tokens.astype(jnp.float32)
    attention_function, first_normalized_input, first_inverse_deviation = layer_norm_apply(
        block_inputs, first_norm_gain, first_norm_shift
    )
    perceptron_function, second_normalized_input, second_inverse_deviation = layer_norm_apply(
        block_inputs, second_norm_gain, second_norm_shift
    )
    attn_in = attention_function.astype(jnp.bfloat16)
    mlp_in = perceptron_function.astype(jnp.bfloat16)
    down_rows = down_proj.reshape(out_proj.shape[0], ratio * width)
    pieces = (
        lax.all_gather(in_proj, "shard", axis=0, tiled=True),
        lax.all_gather(up_proj, "shard", axis=0, tiled=True),
    )
    left_attn = attn_in
    left_mlp = mlp_in
    projected = matmul(left_attn, pieces[0])
    hidden_pre = matmul(left_mlp, pieces[1])
    qkv = (projected + in_bias_all).reshape(length, 3, HEADS, HEAD_DIM)
    cosine, sine = rotary_tables(length)
    query = rotate(qkv[:, 0], cosine, sine, 1.0).astype(jnp.bfloat16)
    keys = rotate(qkv[:, 1], cosine, sine, 1.0).astype(jnp.bfloat16)
    values = qkv[:, 2].astype(jnp.bfloat16)
    causal = jnp.arange(length)[:, None] >= jnp.arange(length)[None, :]
    scores = masked_scores(query, keys, causal, scale)
    expo = jnp.exp(scores)
    total = jnp.sum(expo, axis=2, keepdims=True)
    probs = (expo / total).astype(jnp.bfloat16)
    log_total = jnp.log(total)
    attended = jnp.einsum("hqk,khd->qhd", probs, values, preferred_element_type=jnp.float32)
    attended = attended.reshape(length, width).astype(jnp.bfloat16)
    up_pre = hidden_pre + up_bias_all
    activated = jax.nn.gelu(up_pre, approximate=False).astype(jnp.bfloat16)
    pieces = (
        lax.all_gather(out_proj, "shard", axis=0, tiled=True),
        lax.all_gather(down_rows, "shard", axis=0, tiled=True),
    )
    count = pieces[0].shape[0]
    left_attn = attended
    left_mlp = activated
    branch_sum = matmul(left_attn, pieces[0]) + matmul(
        left_mlp, pieces[1].reshape(count * ratio, width)
    )
    mixed = (block_inputs + branch_sum + out_bias_all + down_bias_all).astype(jnp.bfloat16)
    pieces = (
        lax.all_gather(out_proj, "shard", axis=0, tiled=True),
        lax.all_gather(down_rows, "shard", axis=0, tiled=True),
    )
    count = pieces[0].shape[0]
    part_attn = matmul_trans(cotangent, pieces[0])
    part_mlp = matmul_trans(cotangent, pieces[1].reshape(count * ratio, width))
    grad_att = part_attn.astype(jnp.bfloat16).reshape(length, HEADS, HEAD_DIM)
    gelu_pull = jax.vjp(lambda t: jax.nn.gelu(t, approximate=False), up_pre)[1]
    grad_up = gelu_pull(part_mlp)[0].astype(jnp.bfloat16)
    scores_again = masked_scores(query, keys, causal, scale)
    probs_full = jnp.exp(scores_again - log_total)
    probs_low = probs_full.astype(jnp.bfloat16)
    grad_probs = jnp.einsum("qhd,khd->hqk", grad_att, values, preferred_element_type=jnp.float32)
    grad_values = jnp.einsum(
        "hqk,qhd->khd", probs_low, grad_att, preferred_element_type=jnp.float32
    )
    inner = jnp.sum(grad_probs * probs_full, axis=2, keepdims=True)
    grad_scores = (probs_full * (grad_probs - inner)).astype(jnp.bfloat16)
    grad_query = (
        jnp.einsum("hqk,khd->qhd", grad_scores, keys, preferred_element_type=jnp.float32) * scale
    )
    grad_keys = (
        jnp.einsum("hqk,qhd->khd", grad_scores, query, preferred_element_type=jnp.float32) * scale
    )
    grad_query = rotate(grad_query, cosine, sine, -1.0)
    grad_keys = rotate(grad_keys, cosine, sine, -1.0)
    grad_qkv = jnp.stack([grad_query, grad_keys, grad_values], axis=1).reshape(length, 3 * width)
    grad_qkv = grad_qkv.astype(jnp.bfloat16)
    pieces = (
        lax.all_gather(in_proj, "shard", axis=0, tiled=True),
        lax.all_gather(up_proj, "shard", axis=0, tiled=True),
    )
    attention_input_gradient = matmul_trans(grad_qkv, pieces[0])
    perceptron_input_gradient = matmul_trans(grad_up, pieces[1])
    cot_full = cotangent.astype(jnp.float32)
    tokens_grad = (
        cot_full
        + layer_norm_reverse(
            attention_input_gradient,
            first_normalized_input,
            first_inverse_deviation,
            first_norm_gain,
        )
        + layer_norm_reverse(
            perceptron_input_gradient,
            second_normalized_input,
            second_inverse_deviation,
            second_norm_gain,
        )
    )
    in_owned = lax.psum_scatter(
        matmul_left_trans(attn_in, grad_qkv), "shard", scatter_dimension=0, tiled=True
    )
    up_owned = lax.psum_scatter(
        matmul_left_trans(mlp_in, grad_up), "shard", scatter_dimension=0, tiled=True
    )
    out_owned = lax.psum_scatter(
        matmul_left_trans(attended, cotangent), "shard", scatter_dimension=0, tiled=True
    )
    down_owned = lax.psum_scatter(
        matmul_left_trans(activated, cotangent), "shard", scatter_dimension=0, tiled=True
    )
    vector_owned = (
        lax.psum_scatter(
            jnp.sum(grad_qkv, axis=0, dtype=jnp.float32), "shard", scatter_dimension=0, tiled=True
        ),
        lax.psum_scatter(jnp.sum(cot_full, axis=0), "shard", scatter_dimension=0, tiled=True),
        lax.psum_scatter(
            jnp.sum(grad_up, axis=0, dtype=jnp.float32), "shard", scatter_dimension=0, tiled=True
        ),
        lax.psum_scatter(
            jnp.sum(attention_input_gradient * first_normalized_input, axis=0),
            "shard",
            scatter_dimension=0,
            tiled=True,
        ),
        lax.psum_scatter(
            jnp.sum(attention_input_gradient, axis=0), "shard", scatter_dimension=0, tiled=True
        ),
        lax.psum_scatter(
            jnp.sum(perceptron_input_gradient * second_normalized_input, axis=0),
            "shard",
            scatter_dimension=0,
            tiled=True,
        ),
        lax.psum_scatter(
            jnp.sum(perceptron_input_gradient, axis=0), "shard", scatter_dimension=0, tiled=True
        ),
    )
    summed = lax.psum((in_owned, up_owned, out_owned, down_owned) + tuple(vector_owned), "rep")
    in_grad, up_grad, out_grad, down_grad = (summed[0], summed[1], summed[2], summed[3])
    in_bias_grad, bias_grad, up_bias_grad = (summed[4], summed[5], summed[6])
    first_gain_grad, first_shift_grad, second_gain_grad, second_shift_grad = (
        summed[7],
        summed[8],
        summed[9],
        summed[10],
    )
    return (
        mixed,
        tokens_grad,
        in_grad,
        in_bias_grad,
        out_grad,
        bias_grad,
        up_grad,
        up_bias_grad,
        down_grad,
        bias_grad,
        first_gain_grad,
        first_shift_grad,
        second_gain_grad,
        second_shift_grad,
    )


def solution(mesh):
    in_specs = (
        P(("rep", "shard"), None),
        P("shard", None),
        P("shard"),
        P("shard", None),
        P("shard"),
        P("shard", None),
        P("shard"),
        P("shard", None),
        P("shard"),
        P("shard"),
        P("shard"),
        P("shard"),
        P("shard"),
        P(("rep", "shard"), None),
    )
    out_specs = (
        P(("rep", "shard"), None),
        P(("rep", "shard"), None),
        P("shard", None),
        P("shard"),
        P("shard", None),
        P("shard"),
        P("shard", None),
        P("shard"),
        P("shard", None),
        P("shard"),
        P("shard"),
        P("shard"),
        P("shard"),
        P("shard"),
    )
    return jax.shard_map(
        on_device, mesh=mesh, in_specs=in_specs, out_specs=out_specs, check_vma=False
    )
```

profile of v0, /device:TPU:0, one launch (start us, length us, event | category | flops | bytes accessed | tf_op | source)
XLA Modules:
  0.0 1526.6 jit_solution(15201256800612758057)
XLA Ops:
  8.8 4.4 reshape.141
  13.8 15.0 all-gather.2
  28.9 11.4 all-gather.1
  40.3 13.4 all-gather
  54.3 73.6 %all-gather.12.cloned.1.call-done = bf16[1024,3072]{1,0:T(8,128)(2,1)} async-done(((bf16[256,3072]{1,0:T(8,128)(2,1)}), bf16[1024,3072]{1,0:T(8,128)(2,1)}) %all-gather.12.cloned.1.call-update) | async-done | bytes 6291472 | tf_op jit(solution)/shard_map/all_gather | solution.py:123
  127.8 6.4 convolution_add_fusion.1
  134.2 3.7 copy.43
  137.9 1.7 slice_bitcast_fusion.1
  139.7 1.1 exponential_reduce_fusion
  140.9 3.1 fusion.22
  144.8 2.8 fusion.70
  147.9 25.3 %all-gather.14.cloned.1.call-done = bf16[1024,1024]{1,0:T(8,128)(2,1)} async-done(((bf16[256,1024]{1,0:T(8,128)(2,1)}), bf16[1024,1024]{1,0:T(8,128)(2,1)}) %all-gather.14.cloned.1.call-update) | async-done | bytes 2097168 | tf_op jit(solution)/shard_map/all_gather | solution.py:146
  173.2 2.3 convolution_convert_fusion
  175.8 4.1 multiply_reduce_fusion
  179.9 1.2 multiply_convert_fusion
  182.7 1.1 fusion.14
  184.3 1.1 copy-done.4
  185.4 6.6 fusion.64
  192.6 19.8 %all_gather.48 = bf16[4096]{0:T(1024)(128)(2,1)S(1)} all-gather(bf16[1024]{0:T(1024)(128)(2,1)S(1)} %copy-done.15), channel_id=1, replica_groups=mesh['rep'=8,'shard'=4] {'shard'}, dimensions={0}, use_global_device_ids=true | all-gather | bytes 10240 | tf_op jit(solution)/shard_map/all_gather | solution.py:99
  212.5 11.1 all-gather.4
  223.6 11.7 all-gather.3
  235.3 88.2 %all-gather.18.cloned.1.call-done = bf16[1024,4096]{1,0:T(8,128)(2,1)} async-done(((bf16[256,4096]{1,0:T(8,128)(2,1)}), bf16[1024,4096]{1,0:T(8,128)(2,1)}) %all-gather.18.cloned.1.call-update) | async-done | bytes 8388624 | tf_op jit(solution)/shard_map/all_gather | solution.py:147
  323.5 14.2 reshape.142
  337.7 135.0 %all-gather.16.cloned.1.call-done = bf16[1024,4096]{1,0:T(8,128)(2,1)} async-done(((bf16[256,4096]{1,0:T(8,128)(2,1)}), bf16[1024,4096]{1,0:T(8,128)(2,1)}) %all-gather.16.cloned.1.call-update) | async-done | bytes 8388624 | tf_op jit(solution)/shard_map/all_gather | solution.py:124
  472.7 6.0 convolution_add_fusion
  478.8 13.8 convert_reduce_fusion
  492.6 1.3 copy-done.13
  493.9 8.3 fusion.61
  502.2 4.2 multiply_convert_fusion.1
  506.4 8.1 fusion.71
  514.6 35.3 %reduce-scatter.7.cloned.1.call-done = f32[256,1024]{1,0:T(8,128)} async-done(((f32[1024,1024]{1,0:T(8,128)}), f32[256,1024]{1,0:T(8,128)}) %reduce-scatter.7.cloned.1.call-update) | async-done | bytes 1048592 | tf_op jit(solution)/shard_map/reduce_scatter | solution.py:213
  549.9 214.6 %reduce-scatter.5.cloned.1.call-done = f32[256,3072]{1,0:T(8,128)} async-done(((f32[1024,3072]{1,0:T(8,128)}), f32[256,3072]{1,0:T(8,128)}) %reduce-scatter.5.cloned.1.call-update) | async-done | bytes 3145744 | tf_op jit(solution)/shard_map/reduce_scatter | solution.py:207
  764.5 283.9 %reduce-scatter.9.cloned.1.call-done = f32[256,4096]{1,0:T(8,128)} async-done(((f32[1024,4096]{1,0:T(8,128)}), f32[256,4096]{1,0:T(8,128)}) %reduce-scatter.9.cloned.1.call-update) | async-done | bytes 4194320 | tf_op jit(solution)/shard_map/reduce_scatter | solution.py:210
  1048.4 283.5 %reduce-scatter.11.cloned.1.call-done = f32[1024,1024]{1,0:T(8,128)} async-done(((f32[4096,1024]{1,0:T(8,128)}), f32[1024,1024]{1,0:T(8,128)}) %reduce-scatter.11.cloned.1.call-update) | async-done | bytes 4194320 | tf_op jit(solution)/shard_map/reduce_scatter | solution.py:216
  1332.5 10.3 all-gather.6
  1342.8 7.8 all-gather.5
  1353.3 6.8 fusion.69
  1360.1 5.3 fusion.44
  1365.4 1.7 convert_reduce_fusion.3
  1367.1 18.0 %all-reduce.9 = (f32[3072]{0:T(1024)S(1)}, f32[1024]{0:T(1024)S(1)}, f32[4096]{0:T(1024)S(1)}, f32[1024]{0:T(1024)S(1)}, f32[1024]{0:T(1024)S(1)}, /*index=5*/f32[1024]{0:T(1024)S(1)}, f32[1024]{0:T(1024)S(1)}) all-reduce(f32[3072]{0:T(1024)S(1)} %reduce_sum.154, ...), channel_id=3, replica_groups=mesh['rep'=8,'shard'=4] {'shard'}, use_global_device_ids=true, to_apply=%region_11.12.clone | all-reduce | flops 12288 | bytes 98304
  1385.6 23.8 %all-reduce.7 = (f32[768]{0:T(1024)}, f32[256]{0:T(256)S(1)}, f32[1024]{0:T(1024)}, f32[256]{0:T(256)}, f32[256]{0:T(256)}, /*index=5*/f32[256]{0:T(256)}, f32[256]{0:T(256)}) all-reduce(f32[768]{0:T(1024)S(1)} %dynamic-slice.1, f32[256]{0:T(256)S(1)} %dynamic-slice.3, ...), channel_id=1, replica_groups=mesh['rep'=8,'shard'=4] {'rep'}, use_global_device_ids=true, to_apply=%region_12.13 | all-reduce | flops 3072 | bytes 24576 | tf_op jit(solution)/shard_map/psum | solution.py:246
  1409.4 5.9 fusion.68
  1415.4 1.6 fusion.21
  1417.0 91.8 %all-reduce.12.cloned.1.call-done = (f32[256,3072]{1,0:T(8,128)}, f32[256,1024]{1,0:T(8,128)}, f32[256,4096]{1,0:T(8,128)}, f32[1024,1024]{1,0:T(8,128)}) async-done(((f32[256,3072]{1,0:T(8,128)}, f32[256,1024]{1,0:T(8,128)}, f32[256,4096]{1,0:T(8,128)}, f32[1024,1024]{1,0:T(8,128)}), (f32[256,3072]{1,0:T(8,128)}, f32[256,1024]{1,0:T(8,128)}, f32[256,4096]{1,0:T(8,128)}, ...) | async-done | bytes 12582928 | tf_op jit(solution)/shard_map/psum | solution.py:246
  1509.4 4.0 copy.59
  1514.4 2.1 copy.61
  1516.5 1.6 copy-done.7
  1518.1 2.0 copy.62
  (114 shorter events, 10.4 us)
Async XLA Ops:
  7.2 120.7 %all-gather.12.cloned.1.call-start = ((), (), s32[]{:S(2)}) async-start(), calls=%async_computation.4 | async-start | bytes 7864320 | tf_op jit(solution)/shard_map/all_gather | solution.py:123
  7.9 165.3 %all-gather.14.cloned.1.call-start = ((), (), s32[]{:S(2)}) async-start(), calls=%async_computation.5 | async-start | bytes 2621440 | tf_op jit(solution)/shard_map/all_gather | solution.py:146
  8.7 5.1 copy-start.16
  8.7 20.2 %copy-start.18 = (bf16[256]{0:T(256)(128)(2,1)S(1)}, bf16[256]{0:T(256)(128)(2,1)}, u32[]{:S(2)}) copy-start(bf16[256]{0:T(256)(128)(2,1)} %param.24) | copy-start | bytes 1540
  8.7 31.6 %copy-start.19 = (bf16[256]{0:T(256)(128)(2,1)S(1)}, bf16[256]{0:T(256)(128)(2,1)}, u32[]{:S(2)}) copy-start(bf16[256]{0:T(256)(128)(2,1)} %param.23) | copy-start | bytes 1540
  8.7 45.0 %copy-start = (bf16[256,1024]{1,0:T(8,128)(2,1)S(1)}, bf16[256,1024]{1,0:T(8,128)(2,1)}, u32[]{:S(2)}) copy-start(bf16[256,1024]{1,0:T(8,128)(2,1)} %param.14) | copy-start | bytes 1572868
  8.7 314.8 %all-gather.18.cloned.1.call-start = ((), (), s32[]{:S(2)}) async-start(), calls=%async_computation.7 | async-start | bytes 10485760 | tf_op jit(solution)/shard_map/all_gather | solution.py:147
  13.2 459.6 %all-gather.16.cloned.1.call-start = ((), (), s32[]{:S(2)}) async-start(), calls=%async_computation.6 | async-start | bytes 10485760 | tf_op jit(solution)/shard_map/all_gather | solution.py:124
  13.8 536.1 %reduce-scatter.7.cloned.1.call-start = ((), (), s32[]{:S(2)}) async-start(), calls=%async_computation.9 | async-start | bytes 5242880 | tf_op jit(solution)/shard_map/reduce_scatter | solution.py:213
  140.9 3.1 copy-start.1
  140.9 3.9 copy-start.6
  144.0 0.8 copy-start.10
  147.7 616.8 %reduce-scatter.5.cloned.1.call-start = ((), (), s32[]{:S(2)}) async-start(), calls=%async_computation.8 | async-start | bytes 15728640 | tf_op jit(solution)/shard_map/reduce_scatter | solution.py:207
  175.8 4.1 copy-start.2
  184.2 1.1 copy-start.4
  191.9 0.7 copy-start.15
  191.9 20.5 %copy-start.20 = (bf16[256]{0:T(256)(128)(2,1)S(1)}, bf16[256]{0:T(256)(128)(2,1)}, u32[]{:S(2)}) copy-start(bf16[256]{0:T(256)(128)(2,1)} %param.26) | copy-start | bytes 1540
  191.9 31.7 %copy-start.21 = (bf16[256]{0:T(256)(128)(2,1)S(1)}, bf16[256]{0:T(256)(128)(2,1)}, u32[]{:S(2)}) copy-start(bf16[256]{0:T(256)(128)(2,1)} %param.25) | copy-start | bytes 1540
  192.0 856.4 %reduce-scatter.9.cloned.1.call-start = ((), (), s32[]{:S(2)}) async-start(), calls=%async_computation.10 | async-start | bytes 20971520 | tf_op jit(solution)/shard_map/reduce_scatter | solution.py:210
  472.7 6.0 copy-start.3
  478.7 13.9 copy-start.9
  492.6 1.3 copy-start.13
  502.2 829.6 %reduce-scatter.11.cloned.1.call-start = ((), (), s32[]{:S(2)}) async-start(), calls=%async_computation.11 | async-start | bytes 20971520 | tf_op jit(solution)/shard_map/reduce_scatter | solution.py:216
  514.6 994.2 %all-reduce.12.cloned.1.call-start = ((), (), s32[]{:S(2)}) async-start(), calls=%async_computation.12 | async-start | bytes 25165824 | tf_op jit(solution)/shard_map/psum | solution.py:246
  1331.8 0.7 copy-start.22
  1331.8 11.0 copy-start.23
  1331.8 18.8 %copy-start.24 = (u32[32]{0:T(128)S(1)}, u32[32]{0:T(128)}, u32[]{:S(2)}) copy-start(u32[32]{0:T(128)} %constant.89) | copy-start | bytes 388
  1353.3 6.8 copy-start.5
  1409.4 99.4 %copy-start.17 = (f32[256]{0:T(256)}, f32[256]{0:T(256)S(1)}, u32[]{:S(2)}) copy-start(f32[256]{0:T(256)S(1)} %get-tuple-element.108) | copy-start | bytes 3076
  1409.4 5.9 copy-start.11
  1409.4 5.9 copy-start.12
  1508.8 4.6 copy-start.14
  1509.4 5.0 copy-start.8
  1514.4 3.7 copy-start.7
Sparse Core Ops, SparseCore 0:
  9.6 118.2 all-gather.11
  129.4 43.7 all-gather.13
  174.8 148.6 all-gather.17
  324.9 147.7 all-gather.15
  474.9 74.9 reduce-scatter.6
  552.1 212.3 reduce-scatter.4
  766.9 281.4 reduce-scatter.8
  1050.7 281.0 reduce-scatter.10
  1335.8 172.9 all-reduce.11
where the time goes:
time: 1530 us
  waiting for transfers between devices  1230 us (80%)
  blocking collectives  142 us (9%)
  matrix products  84.4 us (6%)
  local copies, waits for them, and re-layouts  41.3 us (3%)
  between operations  16.3 us (1%)
    reduce_scatter x1, waiting for transfers between devices, on_device(): lax.psum_scatter(matmul_left_trans(mlp_in, grad_up), 'shard', scatter_dim...  284 us
    reduce_scatter x1, waiting for transfers between devices, on_device(): lax.psum_scatter(matmul_left_trans(activated, cotangent), 'shard', scatte...  283 us
    reduce_scatter x1, waiting for transfers between devices, on_device(): lax.psum_scatter(matmul_left_trans(attn_in, grad_qkv), 'shard', scatter_d...  215 us
    all_gather x1, waiting for transfers between devices, on_device(): lax.all_gather(up_proj, 'shard', axis=0, tiled=True)  135 us
    psum x1, waiting for transfers between devices, on_device(): lax.psum((in_owned, up_owned, out_owned, down_owned) + tuple(vector_owned...  91.8 us
    all_gather x1, waiting for transfers between devices, on_device(): lax.all_gather(down_rows, 'shard', axis=0, tiled=True)  88.2 us
    all_gather x1, waiting for transfers between devices, on_device(): lax.all_gather(in_proj, 'shard', axis=0, tiled=True)  73.6 us
    reduce_scatter x1, waiting for transfers between devices, on_device(): lax.psum_scatter(matmul_left_trans(attended, cotangent), 'shard', scatter...  35.3 us
  transfers between devices with their start and end apart: 9, of which 9 were waited for; matrix products, arithmetic and copies ran while one was open for 8% of the time, Pallas kernels for 0%

commit v1 on v0

v1 whole, which is shorter than its diff:
```python
import jax
import jax.numpy as jnp
from jax import lax
from jax.sharding import PartitionSpec as P

HEAD_DIM = 64
ROT = 16
EPS = 1e-05
MASKED = -1e30


def rotary_tables(length):
    half = ROT // 2
    inverse = jnp.exp(-jnp.log(10000.0) * (2.0 * jnp.arange(half, dtype=jnp.float32) / ROT))
    angles = jnp.arange(length, dtype=jnp.float32)[:, None] * inverse[None, :]
    return (jnp.cos(angles)[:, None, :], jnp.sin(angles)[:, None, :])


def rotate(values, cosine, sine, sign):
    half = ROT // 2
    first = values[..., :half]
    second = values[..., half:ROT]
    return jnp.concatenate(
        [
            first * cosine - sign * second * sine,
            second * cosine + sign * first * sine,
            values[..., ROT:],
        ],
        axis=-1,
    )


def mm(left, right, dims=((1,), (0,))):
    return lax.dot_general(left, right, (dims, ((), ())), preferred_element_type=jnp.float32)


def make_body(parts):
    def body(
        tokens,
        in_proj,
        in_bias,
        out_proj,
        out_bias,
        up_proj,
        up_bias,
        down_proj,
        down_bias,
        first_gain,
        first_shift,
        second_gain,
        second_shift,
        cotangent,
    ):
        length, width = tokens.shape
        me = lax.axis_index("shard")
        heads = width // parts // HEAD_DIM
        span = width // parts
        rows = in_proj.shape[0]
        hidden = up_bias.shape[0]
        scale = HEAD_DIM ** (-0.5)
        vectors = jnp.concatenate(
            [in_bias, out_bias, down_bias, first_gain, first_shift, second_gain, second_shift]
        )
        vectors = lax.all_gather(vectors, "shard", axis=0).astype(jnp.float32)
        cuts = [in_bias.shape[0]] + [span] * 6
        offsets = [sum(cuts[:i]) for i in range(len(cuts))]
        whole = [vectors[:, o : o + c].reshape(-1) for o, c in zip(offsets, cuts)]
        in_b, out_b, down_b, gain1, shift1, gain2, shift2 = whole
        both = lax.all_gather(jnp.stack([tokens, cotangent]), "shard", axis=1, tiled=True)
        x_all, g_all = both[0], both[1]
        w_in = lax.all_to_all(
            in_proj.reshape(rows, 3, parts, span), "shard", 2, 0, tiled=True
        ).reshape(parts * rows, 3 * span)
        w_up = lax.all_to_all(up_proj, "shard", 1, 0, tiled=True)
        b_in = lax.dynamic_slice_in_dim(in_b.reshape(3, parts, span), me, 1, axis=1).reshape(-1)
        x = x_all.astype(jnp.float32)
        mean = jnp.mean(x, axis=1, keepdims=True)
        cen = x - mean
        inv = lax.rsqrt(jnp.mean(cen * cen, axis=1, keepdims=True) + EPS)
        xhat = cen * inv
        attn_in = (xhat * gain1 + shift1).astype(jnp.bfloat16)
        mlp_in = (xhat * gain2 + shift2).astype(jnp.bfloat16)
        total_rows = x.shape[0]
        qkv = (mm(attn_in, w_in) + b_in).reshape(parts, length, 3, heads, HEAD_DIM)
        cosine, sine = rotary_tables(length)
        query = rotate(qkv[:, :, 0], cosine, sine, 1.0).astype(jnp.bfloat16)
        keys = rotate(qkv[:, :, 1], cosine, sine, 1.0).astype(jnp.bfloat16)
        values = qkv[:, :, 2].astype(jnp.bfloat16)
        causal = jnp.arange(length)[:, None] >= jnp.arange(length)[None, :]

        def ein(eq, a, b):
            return jnp.einsum(eq, a, b, preferred_element_type=jnp.float32)

        scores = jnp.where(causal, ein("sqhd,skhd->shqk", query, keys) * scale, MASKED)
        expo = jnp.exp(scores)
        probs_full = expo / jnp.sum(expo, axis=-1, keepdims=True)
        probs = probs_full.astype(jnp.bfloat16)
        attended = ein("shqk,skhd->sqhd", probs, values).astype(jnp.bfloat16)
        attended = attended.reshape(total_rows, span)
        up = mm(mlp_in, w_up) + up_bias.astype(jnp.float32)
        activated, pull = jax.vjp(lambda t: jax.nn.gelu(t, approximate=False), up)
        activated = activated.astype(jnp.bfloat16)
        partial = mm(attended, out_proj) + mm(activated, down_proj)
        branch = lax.psum_scatter(
            partial.astype(jnp.bfloat16), "shard", scatter_dimension=0, tiled=True
        )
        mixed = (tokens.astype(jnp.float32) + branch.astype(jnp.float32) + out_b + down_b).astype(
            jnp.bfloat16
        )
        grad_att = mm(g_all, out_proj, ((1,), (1,))).astype(jnp.bfloat16)
        grad_att = grad_att.reshape(parts, length, heads, HEAD_DIM)
        grad_act = mm(g_all, down_proj, ((1,), (1,)))
        grad_up = pull(grad_act)[0].astype(jnp.bfloat16)
        d_probs = ein("sqhd,skhd->shqk", grad_att, values)
        d_values = ein("shqk,sqhd->skhd", probs, grad_att)
        inner = jnp.sum(d_probs * probs_full, axis=-1, keepdims=True)
        d_scores = (probs_full * (d_probs - inner)).astype(jnp.bfloat16)
        d_query = ein("shqk,skhd->sqhd", d_scores, keys) * scale
        d_keys = ein("shqk,sqhd->skhd", d_scores, query) * scale
        d_query = rotate(d_query, cosine, sine, -1.0)
        d_keys = rotate(d_keys, cosine, sine, -1.0)
        grad_qkv = jnp.stack([d_query, d_keys, d_values], axis=2).astype(jnp.bfloat16)
        grad_qkv = grad_qkv.reshape(total_rows, 3 * span)
        d1 = mm(grad_qkv, w_in, ((1,), (1,)))
        d2 = mm(grad_up, w_up, ((1,), (1,)))
        scaled = (d1 * gain1 + d2 * gain2).astype(jnp.bfloat16)
        e = lax.psum_scatter(scaled, "shard", scatter_dimension=0, tiled=True).astype(jnp.float32)
        own = lambda a: lax.dynamic_slice_in_dim(a, me * length, length, axis=0)
        xh, rv = own(xhat), own(inv)
        tokens_grad = cotangent.astype(jnp.float32) + rv * (
            e - jnp.mean(e, axis=1, keepdims=True) - xh * jnp.mean(e * xh, axis=1, keepdims=True)
        )
        left = ((0,), (0,))
        dw_in = mm(attn_in, grad_qkv, left).astype(jnp.bfloat16)
        dw_up = mm(mlp_in, grad_up, left).astype(jnp.bfloat16)
        dw_out = mm(attended, g_all, left).astype(jnp.bfloat16)
        dw_down = mm(activated, g_all, left).astype(jnp.bfloat16)
        dw_in, dw_up, dw_out, dw_down = lax.psum((dw_in, dw_up, dw_out, dw_down), "rep")
        dw_in = lax.all_to_all(
            dw_in.reshape(parts * rows, 3, 1, span), "shard", 0, 2, tiled=True
        ).reshape(rows, 3 * width)
        dw_up = lax.all_to_all(dw_up, "shard", 0, 1, tiled=True)
        f32 = jnp.float32
        place = lambda v: lax.dynamic_update_slice_in_dim(
            jnp.zeros((3, parts, span), f32), v.reshape(3, 1, span), me, axis=1
        ).reshape(-1)
        vec = [
            place(jnp.sum(grad_qkv, axis=0, dtype=f32)),
            jnp.sum(cotangent.astype(f32), axis=0),
            jnp.sum(d1 * xhat, axis=0),
            jnp.sum(d1, axis=0),
            jnp.sum(d2 * xhat, axis=0),
            jnp.sum(d2, axis=0),
        ]
        vec = jnp.concatenate([v.reshape(parts, -1) for v in vec], axis=1)
        vec = lax.psum_scatter(vec, "shard", scatter_dimension=0, tiled=True)[0]
        vec, up_vec = lax.psum((vec, jnp.sum(grad_up, axis=0, dtype=f32)), "rep")
        o = in_bias.shape[0]
        bias_grad = vec[o : o + span]
        rest = [vec[o + span * i : o + span * (i + 1)] for i in range(1, 5)]
        return (
            mixed,
            tokens_grad,
            dw_in.astype(f32),
            vec[:o],
            dw_out.astype(f32),
            bias_grad,
            dw_up.astype(f32),
            up_vec,
            dw_down.astype(f32),
            bias_grad,
            *rest,
        )

    return body


def solution(mesh):
    rows = P(("rep", "shard"), None)
    mat = P("shard", None)
    vec = P("shard")
    in_specs = (rows, mat, vec, mat, vec, mat, vec, mat, vec, vec, vec, vec, vec, rows)
    out_specs = (rows, rows, mat, vec, mat, vec, mat, vec, mat, vec, vec, vec, vec, vec)
    return jax.shard_map(
        make_body(mesh.shape["shard"]),
        mesh=mesh,
        in_specs=in_specs,
        out_specs=out_specs,
        check_vma=False,
    )
```

time: 1530 us -> 617 us (0.40)
  waiting for transfers between devices: 1230 us -> 251 us
  blocking collectives: 142 us -> 170 us
  local copies, waits for them, and re-layouts: 41.3 us -> 68.6 us
  matrix products: 84.4 us -> 60.1 us
  starting transfers between devices: 0.54 us -> 21.3 us
  other arithmetic: 8.49 us -> 27.3 us
    reduce_scatter x4 -> x2, waiting for transfers between devices: 817 us -> 0.01 us  [the longest x1 0.01 us: body(): lax.psum_scatter(scaled, 'shard', scatter_dimension=0, tiled=True)]
    all_gather x4 -> x1, waiting for transfers between devices: 322 us -> 0.01 us  [body(): lax.all_gather(jnp.stack([tokens, cotangent]), 'shard', axis=1, tiled=True)]
    all_to_all x0 -> x4, waiting for transfers between devices: none -> 151 us  [the longest x1 75.6 us: body(): lax.all_to_all(dw_in.reshape(parts * rows, 3, 1, span), 'shard', 0, 2, ti...]
    unnamed x1, blocking collectives: 18 us -> 79.7 us
    all_gather x8 -> x1, blocking collectives: 101 us -> 68.2 us  [body(): vectors = lax.all_gather(vectors, 'shard', axis=0).astype(jnp.float32)]
    dot_general x18, matrix products: 84.4 us -> 60.1 us  [the longest x12 53.3 us: mm(): lax.dot_general(left, right, (dims, ((), ())), preferred_element_type=jnp...]
    all_to_all x0 -> x4, starting transfers between devices: none -> 21 us  [the longest x1 6.35 us: body(): lax.all_to_all(in_proj.reshape(rows, 3, parts, span), 'shard', 2, 0, tile...]
  transfers between devices with their start and end apart: 9 -> 8, of which waited for: 9 -> 3; matrix products, arithmetic and copies ran while one was open for 8% -> 10% of each run, Pallas kernels for 0% -> 0%
where the time goes in v1:
time: 617 us; the launch traced here: 613 us
  waiting for transfers between devices  251 us (41%)
  blocking collectives  170 us (28%)
  local copies, waits for them, and re-layouts  68.6 us (11%)
  matrix products  60.1 us (10%)
  other arithmetic  27.3 us (4%)
  starting transfers between devices  21.3 us (3%)
  between operations  14.7 us (2%)
    psum x1, waiting for transfers between devices, body(): lax.psum((dw_in, dw_up, dw_out, dw_down), 'rep')  99.9 us
    unnamed x1, blocking collectives  79.7 us
    all_to_all x1, waiting for transfers between devices, body(): lax.all_to_all(dw_in.reshape(parts * rows, 3, 1, span), 'shard', 0, 2, ti...  75.6 us
    all_to_all x1, waiting for transfers between devices, body(): lax.all_to_all(in_proj.reshape(rows, 3, parts, span), 'shard', 2, 0, tile...  75 us
    all_gather x1, blocking collectives, body(): vectors = lax.all_gather(vectors, 'shard', axis=0).astype(jnp.float32)  68.2 us
    dot_general x12, matrix products, mm(): lax.dot_general(left, right, (dims, ((), ())), preferred_element_type=jnp...  53.3 us
    psum x1, blocking collectives, body(): vec, up_vec = lax.psum((vec, jnp.sum(grad_up, axis=0, dtype=f32)), 'rep')  22.3 us
    unnamed x115, local copies, waits for them, and re-layouts  22.3 us
  transfers between devices with their start and end apart: 8, of which 3 were waited for; matrix products, arithmetic and copies ran while one was open for 10% of the time, Pallas kernels for 0%

profile of v1, /device:TPU:0, one launch (start us, length us, event | category | flops | bytes accessed | tf_op | source)
XLA Modules:
  0.0 612.7 jit_solution(14846961381033771)
XLA Ops:
  7.2 2.4 pad_maximum_fusion.1
  9.7 2.6 copy.92
  12.2 2.7 copy.93
  14.9 6.3 %all-to-all-start = ((bf16[256,3,4,256]{0,3,1,2:T(8,128)(2,1)}), bf16[256,3,4,256]{0,3,1,2:T(8,128)(2,1)}, u32[]{:S(2)}, u32[]{:S(2)}) async-start(bf16[256,3,4,256]{0,3,1,2:T(8,128)(2,1)} %copy.93), calls=%async_computation | async-start | bytes 3145728 | tf_op jit(solution)/shard_map/all_to_all | solution.py:71
  21.3 4.2 copy.101
  25.5 75.0 %all-to-all-done = bf16[256,3,4,256]{0,3,1,2:T(8,128)(2,1)} async-done(((bf16[256,3,4,256]{0,3,1,2:T(8,128)(2,1)}), bf16[256,3,4,256]{0,3,1,2:T(8,128)(2,1)}, u32[]{:S(2)}, u32[]{:S(2)}) %all-to-all-start) | async-done | bytes 1572896 | tf_op jit(solution)/shard_map/all_to_all | solution.py:71
  100.4 5.6 all-to-all-start.1
  107.9 68.2 %all-gather.1 = bf16[4,1,2304]{2,1,0:T(2,128)(2,1)S(1)} all-gather(bf16[1,1,2304]{2,1,0:T(2,128)(2,1)S(1)} %reshape.284), channel_id=2, replica_groups=mesh['rep'=8,'shard'=4] {'shard'}, dimensions={0}, use_global_device_ids=true | all-gather | bytes 23040 | tf_op jit(solution)/shard_map/all_gather | solution.py:64
  179.4 2.6 copy.94
  183.5 3.9 copy.102
  187.5 2.1 convert_reduce_fusion
  189.6 2.3 fusion.10
  192.4 5.2 convolution_add_fusion
  197.7 6.3 %reshape.289 = f32[4,256,3,4,64]{4,3,2,1,0:T(4,128)} reshape(f32[1024,768]{1,0:T(8,128)} %convolution_add_fusion) | data formatting | bytes 6291456 | tf_op jit(solution)/shard_map/reshape | solution.py:84
  204.0 2.9 slice.129
  206.9 4.7 fusion.63
  211.6 1.5 fusion.36
  213.1 2.0 reshape.290
  216.4 2.2 copy.122
  218.6 1.9 copy.123
  220.5 3.2 copy.124
  226.0 2.0 fusion.18
  237.1 3.1 convolution_convert_fusion.1
  240.2 4.3 copy.110
  244.6 3.2 fusion.37
  247.8 12.6 %multiply_convert_fusion.1 = (bf16[1024,1024]{1,0:T(8,128)(2,1)S(1)}, f32[1024,1024]{1,0:T(8,128)S(1)}, f32[1024,1024]{1,0:T(8,128)S(1)}) fusion(f32[1024]{0:T(1024)S(1)} %copy-done.23, bf16[1024,1024]{1,0:T(8,128)(2,1)} %bitcast.153, f32[1024]{0:T(1024)S(1)} %bitcast.175, f32[1024]{0:T(1024)S(1)} %bitcast.169, f32[1024]{0:T(1024)S(1)} %copy-done.21, ...), kind=kOutput, calls=%fused_computation.27 | convolution fusion | flops 2222981120 | bytes 14700544 | tf_op jit(solution)/shard_map/dot_general | solution.py:34
  260.4 4.2 convert_reduce_fusion.1
  264.6 4.2 fusion.30
  268.8 3.8 convolution_convert_fusion
  272.7 3.9 fusion.66
  277.1 5.6 multiply_reduce_fusion
  282.7 99.9 %all-reduce.5.cloned.1.call-done = (bf16[1024,3,1,256]{3,1,2,0:T(4,128)(2,1)}, bf16[256,1024]{1,0:T(8,128)(2,1)}, bf16[4,256,1024]{2,1,0:T(8,128)(2,1)}, bf16[1024,1024]{1,0:T(8,128)(2,1)}) async-done(((bf16[1024,3,1,256]{3,1,2,0:T(4,128)(2,1)}, bf16[256,1024]{1,0:T(8,128)(2,1)}, bf16[4,256,1024]{2,1,0:T(8,128)(2,1)}, bf16[1024,1024]{1,0:T(8,128)(2,1)}), (bf16[1024,3,1,256]{3,1,2,0:T(4,128)(2,1)}, ...) | async-done | bytes 6291472 | tf_op jit(solution)/shard_map/psum | solution.py:138
  382.6 4.6 all-to-all-start.2
  387.5 3.9 fusion.65
  391.4 2.1 add_convert_fusion.3
  393.5 75.6 %all-to-all-done.2 = bf16[1024,3,1,256]{3,1,2,0:T(4,128)(2,1)} async-done(((bf16[1024,3,1,256]{3,1,2,0:T(4,128)(2,1)}), bf16[1024,3,1,256]{3,1,2,0:T(4,128)(2,1)}, u32[]{:S(2)}, u32[]{:S(2)}) %all-to-all-start.2) | async-done | bytes 1572896 | tf_op jit(solution)/shard_map/all_to_all | solution.py:139
  469.1 4.5 all-to-all-start.3
  475.6 4.2 convert_element_type.180
  479.8 1.6 convert_reduce_fusion.3
  481.4 2.7 convert_reduce_fusion.4
  484.2 79.7 %all-reduce = f32[4,2048]{1,0:T(4,128)S(1)} all-reduce(f32[4,2048]{1,0:T(4,128)S(1)} %constant_dynamic-update-slice_fusion), channel_id=5, replica_groups=mesh['rep'=8,'shard'=4] {'shard'}, use_global_device_ids=true, to_apply=%region_15.16.clone | all-reduce | flops 8192 | bytes 65536
  564.5 22.3 %all-reduce.1 = (f32[2048]{0:T(1024)S(1)}, f32[1024]{0:T(1024)}) all-reduce(f32[2048]{0:T(1024)S(1)} %bitcast.166, f32[1024]{0:T(1024)S(1)} %get-tuple-element.67), channel_id=1, replica_groups=mesh['rep'=8,'shard'=4] {'rep'}, use_global_device_ids=true, to_apply=%region_16.17 | all-reduce | flops 3072 | bytes 24576 | tf_op jit(solution)/shard_map/psum | solution.py:157
  588.0 2.0 add_convert_fusion.7
  590.1 2.1 convert_bitcast_fusion.1
  592.2 3.7 copy.111
  595.9 5.1 reshape.279
  601.0 2.0 convert_bitcast_fusion.2
  603.0 2.3 copy.125
  (168 shorter events, 25.0 us)
Async XLA Ops:
  7.2 253.2 %copy-start = (bf16[1024,1024]{1,0:T(8,128)(2,1)S(1)}, bf16[1024,1024]{1,0:T(8,128)(2,1)}, u32[]{:S(2)}) copy-start(bf16[1024,1024]{1,0:T(8,128)(2,1)} %param.21) | copy-start | bytes 6291460
  7.2 180.3 %all-gather.4.cloned.1.call-start = ((), (), s32[]{:S(2)}) async-start(), calls=%async_computation.6 | async-start | bytes 5242880 | tf_op jit(solution)/shard_map/all_gather | solution.py:69
  14.9 85.5 %all-to-all-start = ((bf16[256,3,4,256]{0,3,1,2:T(8,128)(2,1)}), bf16[256,3,4,256]{0,3,1,2:T(8,128)(2,1)}, u32[]{:S(2)}, u32[]{:S(2)}) async-start(bf16[256,3,4,256]{0,3,1,2:T(8,128)(2,1)} %copy.93), calls=%async_computation | async-start | bytes 3145728 | tf_op jit(solution)/shard_map/all_to_all | solution.py:71
  21.2 84.8 %copy-start.30 = (bf16[1024]{0:T(1024)(128)(2,1)S(1)}, bf16[1024]{0:T(1024)(128)(2,1)}, u32[]{:S(2)}) copy-start(bf16[1024]{0:T(1024)(128)(2,1)} %param.20) | copy-start | bytes 6148
  21.2 85.4 %copy-start.31 = (bf16[768]{0:T(1024)(128)(2,1)S(1)}, bf16[768]{0:T(1024)(128)(2,1)}, u32[]{:S(2)}) copy-start(bf16[768]{0:T(1024)(128)(2,1)} %param.16) | copy-start | bytes 4612
  21.3 85.5 %copy-start.32 = (bf16[256]{0:T(256)(128)(2,1)S(1)}, bf16[256]{0:T(256)(128)(2,1)}, u32[]{:S(2)}) copy-start(bf16[256]{0:T(256)(128)(2,1)} %param.18) | copy-start | bytes 1540
  21.3 85.8 %copy-start.33 = (bf16[256]{0:T(256)(128)(2,1)S(1)}, bf16[256]{0:T(256)(128)(2,1)}, u32[]{:S(2)}) copy-start(bf16[256]{0:T(256)(128)(2,1)} %param.22) | copy-start | bytes 1540
  21.3 86.0 %copy-start.34 = (bf16[256]{0:T(256)(128)(2,1)S(1)}, bf16[256]{0:T(256)(128)(2,1)}, u32[]{:S(2)}) copy-start(bf16[256]{0:T(256)(128)(2,1)} %param.23) | copy-start | bytes 1540
  21.3 86.2 %copy-start.35 = (bf16[256]{0:T(256)(128)(2,1)S(1)}, bf16[256]{0:T(256)(128)(2,1)}, u32[]{:S(2)}) copy-start(bf16[256]{0:T(256)(128)(2,1)} %param.24) | copy-start | bytes 1540
  21.3 86.4 %copy-start.36 = (bf16[256]{0:T(256)(128)(2,1)S(1)}, bf16[256]{0:T(256)(128)(2,1)}, u32[]{:S(2)}) copy-start(bf16[256]{0:T(256)(128)(2,1)} %param.25) | copy-start | bytes 1540
  21.3 86.6 %copy-start.37 = (bf16[256]{0:T(256)(128)(2,1)S(1)}, bf16[256]{0:T(256)(128)(2,1)}, u32[]{:S(2)}) copy-start(bf16[256]{0:T(256)(128)(2,1)} %param.26) | copy-start | bytes 1540
  100.4 83.1 %all-to-all-start.1 = ((bf16[256,4,1024]{0,2,1:T(8,128)(2,1)}), bf16[256,4,1024]{0,2,1:T(8,128)(2,1)}, u32[]{:S(2)}, u32[]{:S(2)}) async-start(bf16[256,4,1024]{0,2,1:T(8,128)(2,1)} %bitcast.142), calls=%async_computation.1 | async-start | bytes 4194304 | tf_op jit(solution)/shard_map/all_to_all | solution.py:74
  106.0 276.6 %all-reduce.5.cloned.1.call-start = ((), (), s32[]{:S(2)}) async-start(), calls=%async_computation.9 | async-start | bytes 13631488 | tf_op jit(solution)/shard_map/psum | solution.py:138
  178.0 13.9 %copy-start.28 = (f32[1,2,4,128]{3,1,2,0:T(2,128)}, f32[1,2,4,128]{3,1,2,0:T(2,128)S(1)}, u32[]{:S(2)}) copy-start(f32[1,2,4,128]{3,1,2,0:T(2,128)S(1)} %copy.127) | copy-start | bytes 12292
  178.0 13.9 %copy-start.25 = (f32[1,2,4,128]{3,1,2,0:T(2,128)}, f32[1,2,4,128]{3,1,2,0:T(2,128)S(1)}, u32[]{:S(2)}) copy-start(f32[1,2,4,128]{3,1,2,0:T(2,128)S(1)} %copy.126) | copy-start | bytes 12292
  187.4 5.0 copy-start.1
  189.5 2.3 copy-start.16
  206.9 4.7 copy-start.2
  206.9 4.7 copy-start.10
  224.9 3.1 copy-start.13
  224.9 3.1 copy-start.15
  234.9 2.2 copy-start.3
  234.9 2.2 copy-start.17
  234.9 2.2 copy-start.21
  234.9 2.2 copy-start.26
  234.9 2.2 copy-start.29
  236.8 3.4 copy-start.9
  240.2 7.6 %copy-start.23 = (f32[1024]{0:T(1024)S(1)}, f32[1024]{0:T(1024)}, u32[]{:S(2)}) copy-start(f32[1024]{0:T(1024)} %convert_element_type.153) | copy-start | bytes 12292
  240.2 7.6 %copy-start.24 = (f32[1,2,4,128]{3,1,2,0:T(2,128)S(1)}, f32[1,2,4,128]{3,1,2,0:T(2,128)}, u32[]{:S(2)}) copy-start(f32[1,2,4,128]{3,1,2,0:T(2,128)} %copy.130) | copy-start | bytes 12292
  240.2 7.6 %copy-start.27 = (f32[1,2,4,128]{3,1,2,0:T(2,128)S(1)}, f32[1,2,4,128]{3,1,2,0:T(2,128)}, u32[]{:S(2)}) copy-start(f32[1,2,4,128]{3,1,2,0:T(2,128)} %copy.131) | copy-start | bytes 12292
  244.6 3.3 copy-start.4
  260.4 8.4 %copy-start.41 = (bf16[1024,1024]{1,0:T(8,128)(2,1)}, bf16[1024,1024]{1,0:T(8,128)(2,1)S(1)}, u32[]{:S(2)}) copy-start(bf16[1024,1024]{1,0:T(8,128)(2,1)S(1)} %get-tuple-element.28) | copy-start | bytes 6291460
  264.6 4.2 copy-start.39
  272.6 207.2 %reduce-scatter.5.cloned.1.call-start = ((), (), s32[]{:S(2)}) async-start(), calls=%async_computation.8 | async-start | bytes 2621440 | tf_op jit(solution)/shard_map/reduce_scatter | solution.py:127
  272.7 3.9 copy-start.5
  272.7 3.9 copy-start.6
  272.7 4.4 copy-start.40
  382.6 86.5 %all-to-all-start.2 = ((bf16[1024,3,1,256]{3,1,2,0:T(4,128)(2,1)}), bf16[1024,3,1,256]{3,1,2,0:T(4,128)(2,1)}, u32[]{:S(2)}, u32[]{:S(2)}) async-start(bf16[1024,3,1,256]{3,1,2,0:T(4,128)(2,1)} %get-tuple-element.22), calls=%async_computation.4 | async-start | bytes 4194304 | tf_op jit(solution)/shard_map/all_to_all | solution.py:139
  387.2 4.2 copy-start.11
  387.2 200.8 %reduce-scatter.3.cloned.1.call-start = ((), (), s32[]{:S(2)}) async-start(), calls=%async_computation.7 | async-start | bytes 2621440 | tf_op jit(solution)/shard_map/reduce_scatter | solution.py:104
  393.5 80.1 %copy-start.19 = (f32[1,2,4,128]{3,2,1,0:T(4,128)S(1)}, f32[1,2,4,128]{3,2,1,0:T(4,128)}, u32[]{:S(2)}) copy-start(f32[1,2,4,128]{3,2,1,0:T(4,128)} %get-tuple-element.44) | copy-start | bytes 12292
  393.5 80.1 %copy-start.18 = (f32[1,2,4,128]{3,2,1,0:T(4,128)S(1)}, f32[1,2,4,128]{3,2,1,0:T(4,128)}, u32[]{:S(2)}) copy-start(f32[1,2,4,128]{3,2,1,0:T(4,128)} %get-tuple-element.45) | copy-start | bytes 12292
  393.5 80.1 %copy-start.38 = (u32[32]{0:T(128)S(1)}, u32[32]{0:T(128)}, u32[]{:S(2)}) copy-start(u32[32]{0:T(128)} %constant.101) | copy-start | bytes 388
  393.5 81.0 %copy-start.12 = (bf16[256,1024]{1,0:T(8,128)(2,1)S(1)}, bf16[256,1024]{1,0:T(8,128)(2,1)}, u32[]{:S(2)}) copy-start(bf16[256,1024]{1,0:T(8,128)(2,1)} %get-tuple-element.23) | copy-start | bytes 1572868
  469.1 131.9 %all-to-all-start.3 = ((bf16[4,256,1024]{2,1,0:T(8,128)(2,1)}), bf16[4,256,1024]{2,1,0:T(8,128)(2,1)}, u32[]{:S(2)}, u32[]{:S(2)}) async-start(bf16[4,256,1024]{2,1,0:T(8,128)(2,1)} %get-tuple-element.24), calls=%async_computation.5 | async-start | bytes 4194304 | tf_op jit(solution)/shard_map/all_to_all | solution.py:142
  475.6 5.8 copy-start.8
  475.6 112.4 %copy-start.7 = (bf16[256,1024]{1,0:T(8,128)(2,1)S(1)}, bf16[256,1024]{1,0:T(8,128)(2,1)}, u32[]{:S(2)}) copy-start(bf16[256,1024]{1,0:T(8,128)(2,1)} %param.14) | copy-start | bytes 1572868
  588.0 17.4 %copy-start.22 = (f32[256]{0:T(256)}, f32[256]{0:T(256)S(1)}, u32[]{:S(2)}) copy-start(f32[256]{0:T(256)S(1)} %get-tuple-element.94) | copy-start | bytes 3076
  (2 other events, 1.7 us)
Sparse Core Ops, SparseCore 0:
  10.1 152.0 all-gather.3
  272.7 109.8 all-reduce.4
  384.9 73.5 reduce-scatter.4
  461.2 82.8 reduce-scatter.2

commit v2 on v1

--- a/solution.py
+++ b/solution.py
@@ -1,6 +1,11 @@
+import functools
+
 import jax
 import jax.numpy as jnp
+import numpy as np
 from jax import lax
+from jax.experimental import pallas as pl
+from jax.experimental.pallas import tpu as pltpu
 from jax.sharding import PartitionSpec as P
 
 HEAD_DIM = 64
@@ -175,16 +180,764 @@
     return body
 
 
+BF = jnp.bfloat16
+F32 = jnp.float32
+MESH = pl.DeviceIdType.MESH
+VMEM_LIMIT = 67_000_000
+NN = ((1,), (0,))
+NT = ((1,), (1,))
+TN = ((0,), (0,))
+
+
+class Sizes:
+    def __init__(self, mesh_shape, length, width, hidden):
+        self.copies = mesh_shape["rep"]
+        self.n = self.copies // 2
+        self.s = mesh_shape["shard"]
+        self.l = length
+        self.d = width
+        self.ff = hidden
+        self.span = width // self.n
+        self.hid = hidden // self.n
+        self.rs = width // self.s
+        self.hb = hidden // self.s // self.n
+        self.rows = self.n * length
+
+    def fits(self):
+        return (
+            self.copies % 2 == 0
+            and self.n == self.s
+            and self.span % 256 == 0
+            and self.hb % 256 == 0
+            and self.rs == 256
+            and self.span == 256
+            and self.hb == 256
+        )
+
+
+def rotary_lanes(length):
+    half = ROT // 2
+    inverse = np.exp(-np.log(10000.0) * (2.0 * np.arange(half) / ROT))
+    angles = np.arange(length)[:, None] * inverse[None, :]
+    cosine, sine = np.cos(angles), np.sin(angles)
+    table = np.zeros((3, length, 128), np.float32)
+    table[0] = 1.0
+    for start in (0, HEAD_DIM):
+        table[0, :, start : start + half] = cosine
+        table[0, :, start + half : start + ROT] = cosine
+        table[1, :, start : start + half] = -sine
+        table[2, :, start + half : start + ROT] = sine
+    return table
+
+
+def dot(left, right, dims=NN):
+    return lax.dot_general(left, right, (dims, ((), ())), preferred_element_type=F32)
+
+
+def fused(z, *refs):
+    (tok, cot, inp, upp, outp, downp, vec, rot) = refs[:8]
+    (mixed_o, tgrad_o, gin_o, gup_o, gdown_o, gout_o, vec_o) = refs[8:15]
+    (
+        x_all, g_all, a1, a2, w1, wo, wd, qkv, pt, der, act, att, gatt, gup, gqkv,
+        msend, mrecv, mown, esend, erecv, eown,
+        dwi, dwu, dwd, dwo, xri, xru, xrd, xro, zri, zru, zrd, zro, fi, fu, fd, fo,
+        va, inb, vfull, vz, vu, vr, mean_r, inv_r, vacc, bin_r, bup_r,
+        loc, v_s, v_r, x_s, x_r, g_s, g_r, w_s, w_r, wc_s, wc_r, d_s, d_r, dc_s, dc_r,
+        o_s, o_r, oc_s, oc_r, m_s, m_r, e_s, e_r, xs_s, xs_r, zs_s, zs_r,
+        agx_s, agx_r, agc_s, agc_r, agl, v1_s, v1_r, v2_s, v2_r,
+    ) = refs[15:]
+    n, s_n, length, width = z.n, z.s, z.l, z.d
+    span, hid, rs, hb = z.span, z.hid, z.rs, z.hb
+    iw = 3 * span
+    heads = span // HEAD_DIM
+    scale = HEAD_DIM**-0.5
+    r = lax.axis_index("rep")
+    zz = lax.axis_index("shard")
+    p = lax.div(r, 2)
+    c = lax.rem(r, 2)
+    other = 1 - c
+    partner = (2 * p + other, zz)
+
+    def rc(src, dst, ss, rr, dev):
+        return pltpu.make_async_remote_copy(
+            src_ref=src, dst_ref=dst, send_sem=ss, recv_sem=rr, device_id=dev, device_id_type=MESH
+        )
+
+    def mo(value, m):
+        return pl.multiple_of(value, m)
+
+    def seq(ref, s):
+        return ref.at[pl.ds(mo(s * length, length), length)]
+
+    sends = []
+
+    def start(copy, cond=None):
+        if cond is None:
+            copy.start()
+        else:
+            pl.when(cond)(copy.start)
+        sends.append((cond, copy))
+
+    own_rows = pl.ds(mo(zz * rs, rs), rs)
+    own_hb = pl.ds(mo(zz * hb, hb), hb)
+    locals_w = []
+    for i in range(3):
+        locals_w.append(
+            pltpu.make_async_copy(
+                inp.at[:, pl.ds(mo(i * width + p * span, span), span)],
+                w1.at[own_rows, pl.ds(i * span, span)],
+                loc.at[i],
+            )
+        )
+    for i in range(s_n):
+        locals_w.append(
+            pltpu.make_async_copy(
+                upp.at[:, pl.ds(mo(i * (hb * n) + p * hb, hb), hb)],
+                w1.at[own_rows, pl.ds(iw + i * hb, hb)],
+                loc.at[3 + i],
+            )
+        )
+    local_d = pltpu.make_async_copy(
+        downp.at[pl.ds(mo(p * hb, hb), hb)], wd.at[own_hb], loc.at[3 + s_n]
+    )
+    local_x = pltpu.make_async_copy(tok, seq(x_all, p), loc.at[4 + s_n])
+    local_g = pltpu.make_async_copy(cot, seq(g_all, p), loc.at[5 + s_n])
+    local_v = pltpu.make_async_copy(vec, va.at[zz], loc.at[6 + s_n])
+    local_o = pltpu.make_async_copy(outp, wo, loc.at[7 + s_n])
+    for cp in [local_v, local_x] + locals_w + [local_g, local_d]:
+        cp.start()
+    pl.when(zz == p)(local_o.start)
+
+    barrier = pltpu.get_barrier_semaphore()
+    for i in range(1, 2 * n):
+        pl.semaphore_signal(
+            barrier, 1, device_id=(lax.rem(r + i, 2 * n), zz), device_id_type=MESH
+        )
+    for i in range(1, s_n):
+        pl.semaphore_signal(barrier, 1, device_id=(r, lax.rem(zz + i, s_n)), device_id_type=MESH)
+    pl.semaphore_wait(barrier, 2 * n - 1 + s_n - 1)
+
+    def plane(i):
+        q = lax.rem(p + i, n)
+        return q, (2 * q + c, zz)
+
+    def line(i):
+        q = lax.rem(zz + i, s_n)
+        return q, (r, q)
+
+    left, right = (r, zz - 1), (r, zz + 1)
+    has_left, has_right = zz > 0, zz < s_n - 1
+
+    for i in range(1, s_n):
+        q, dev = line(i)
+        start(rc(vec, va.at[zz], v_s.at[i], v_r.at[zz], dev))
+    for i in range(1, n):
+        q, dev = plane(i)
+        start(rc(tok, seq(x_all, p), x_s.at[i], x_r.at[p], dev))
+    half = rs // 2
+
+    def w_piece(q):
+        return w1.at[pl.ds(mo(q * rs + c * half, half), half)]
+
+    def w_other(q):
+        return w1.at[pl.ds(mo(q * rs + other * half, half), half)]
+
+    for cp in locals_w:
+        cp.wait()
+    start(rc(w_piece(zz), w_piece(zz), w_s.at[0], w_r.at[zz], left), has_left)
+    start(rc(w_piece(zz), w_piece(zz), w_s.at[1], w_r.at[zz], right), has_right)
+    for i in range(1, n):
+        q, dev = plane(i)
+        start(rc(cot, seq(g_all, p), g_s.at[i], g_r.at[p], dev))
+
+    def relay(piece, ss, rr, cs, cr, d):
+        def take(q, has, onward, more, slot):
+            @pl.when(has)
+            def _():
+                rc(piece(q), piece(q), ss.at[slot], rr.at[q], partner).wait_recv()
+
+            start(
+                rc(piece(q), piece(q), ss.at[slot], rr.at[q], onward),
+                jnp.logical_and(has, more),
+            )
+            start(rc(piece(q), piece(q), cs.at[slot], cr.at[q], partner), has)
+
+        take(zz - d, zz - d >= 0, right, has_right, 2 * d)
+        take(zz + d, zz + d <= s_n - 1, left, has_left, 2 * d + 1)
+
+    def relay_done(piece_other, cs, cr):
+        for i in range(1, s_n):
+            q, _ = line(i)
+            rc(piece_other(q), piece_other(q), cs.at[0], cr.at[q], partner).wait_recv()
+
+    local_v.wait()
+    for i in range(1, s_n):
+        q, dev = line(i)
+        rc(vec, va.at[q], v_s.at[i], v_r.at[q], dev).wait_recv()
+    n_in = 3 * width // s_n
+    n_up = hb * n
+    at_up = n_in
+    at_rest = n_in + n_up
+
+    def vector(i):
+        off = at_rest + i * rs
+        return jnp.concatenate([va[q, :, off : off + rs] for q in range(s_n)], axis=1)
+
+    out_b, down_b, gain1, shift1, gain2, shift2 = [vector(i) for i in range(6)]
+    for q in range(s_n):
+        inb[:, q * n_in : (q + 1) * n_in] = va[q, :, :n_in]
+
+    def norm(s):
+        step = 32
+
+        def body(i, carry):
+            row = pl.ds(mo(s * length + i * step, step), step)
+            xv = x_all[row, :].astype(F32)
+            mu = jnp.mean(xv, axis=1, keepdims=True)
+            cen = xv - mu
+            inv = lax.rsqrt(jnp.mean(cen * cen, axis=1, keepdims=True) + EPS)
+            xh = cen * inv
+            a1[row, :] = (xh * gain1 + shift1).astype(BF)
+            a2[row, :] = (xh * gain2 + shift2).astype(BF)
+            mean_r[row, :] = mu
+            inv_r[row, :] = inv
+            return carry
+
+        lax.fori_loop(0, length // step, body, 0)
+
+    local_x.wait()
+    norm(p)
+    relay(w_piece, w_s, w_r, wc_s, wc_r, 1)
+    for d in range(2, s_n):
+        if d == s_n - 1:
+            for i in range(1, n):
+                q, dev = plane(i)
+                rc(tok, seq(x_all, q), x_s.at[i], x_r.at[q], dev).wait_recv()
+                norm(q)
+        relay(w_piece, w_s, w_r, wc_s, wc_r, d)
+
+    hhalf = hb // 2
+
+    def d_piece(q):
+        return wd.at[pl.ds(mo(q * hb + c * hhalf, hhalf), hhalf)]
+
+    def d_other(q):
+        return wd.at[pl.ds(mo(q * hb + other * hhalf, hhalf), hhalf)]
+
+    ohalf = span // 2
+    o_piece = wo.at[pl.ds(mo(c * ohalf, ohalf), ohalf)]
+    o_other = wo.at[pl.ds(mo(other * ohalf, ohalf), ohalf)]
+    local_d.wait()
+    pl.when(zz == p)(local_o.wait)
+    start(rc(d_piece(zz), d_piece(zz), d_s.at[0], d_r.at[zz], left), has_left)
+    start(rc(d_piece(zz), d_piece(zz), d_s.at[1], d_r.at[zz], right), has_right)
+    at_home = zz == p
+    start(rc(o_piece, o_piece, o_s.at[0], o_r.at[0], left), jnp.logical_and(at_home, has_left))
+    start(rc(o_piece, o_piece, o_s.at[1], o_r.at[0], right), jnp.logical_and(at_home, has_right))
+    relay_done(w_other, wc_s, wc_r)
+
+    def up_block(s):
+        row = pl.ds(mo(s * length, length), length)
+        left_a = a2[row, :]
+        for j in range(s_n):
+            col = pl.ds(j * hb, hb)
+            bias = va[j, :, pl.ds(mo(at_up + p * hb, hb), hb)]
+            u = dot(left_a, w1[:, iw + j * hb : iw + (j + 1) * hb]) + bias
+            phi = 0.5 * (1.0 + lax.erf(u * 0.7071067811865476))
+            act[row, col] = (u * phi).astype(BF)
+            der[row, col] = phi + u * (0.3989422804014327 * jnp.exp(-0.5 * u * u))
+
+    lax.fori_loop(0, n, lambda s, _: (up_block(s), 0)[1], 0)
+    relay(d_piece, d_s, d_r, dc_s, dc_r, 1)
+
+    def exchange(t, dw, xr, block_half):
+        src = dw.at[:, pl.ds(mo(other * block_half, block_half), block_half)]
+        start(rc(src, xr, xs_s.at[t], xs_r.at[t], partner))
+
+    def pair_sum(t, dw, xr, zr, block_half, blocks):
+        mine = pl.ds(mo(c * block_half, block_half), block_half)
+        src = dw.at[:, mine]
+        rc(src, xr, xs_s.at[t], xs_r.at[t], partner).wait_recv()
+
+        def body(q, carry):
+            xr[q] = (dw[q, mine].astype(F32) + xr[q].astype(F32)).astype(BF)
+            return carry
+
+        lax.fori_loop(0, blocks, body, 0)
+        for i in range(1, s_n):
+            q, dev = line(i)
+            start(rc(xr.at[q], zr.at[zz], zs_s.at[t, i], zs_r.at[t, zz], dev))
+
+    def line_sum(t, xr, zr, fin):
+        total = xr[zz].astype(F32)
+        for i in range(1, s_n):
+            q, dev = line(i)
+            rc(xr.at[q], zr.at[q], zs_s.at[t, i], zs_r.at[t, q], dev).wait_recv()
+            total = total + zr[q].astype(F32)
+        fin[...] = total.astype(BF)
+
+    def areas(t, q, core):
+        if t == 0:
+            row = pl.ds(mo(core * half, half), half)
+            return [
+                (k, gin_o.at[row, pl.ds(mo(k * width + q * span, span), span)], fi.at[:, pl.ds(k * span, span)])
+                for k in range(3)
+            ]
+        if t == 1:
+            row = pl.ds(mo(core * half, half), half)
+            return [
+                (3 + k, gup_o.at[row, pl.ds(mo(k * (hb * n) + q * hb, hb), hb)], fu.at[:, pl.ds(k * hb, hb)])
+                for k in range(s_n)
+            ]
+        if t == 2:
+            row = pl.ds(mo(q * hb + core * hhalf, hhalf), hhalf)
+            return [(3 + s_n, gdown_o.at[row], fd)]
+        row = pl.ds(mo(core * ohalf, ohalf), ohalf)
+        return [(4 + s_n, gout_o.at[row], fo)]
+
+    local_out = []
+
+    def spread(t, cond=None):
+        for k, area, fin in areas(t, p, c):
+            for i in range(1, n):
+                q, dev = plane(i)
+                start(rc(fin, area, agx_s.at[k, i], agx_r.at[k, p], dev), cond)
+            start(rc(fin, area, agc_s.at[k, 0], agc_r.at[k, p], partner), cond)
+            cp = pltpu.make_async_copy(fin, area, agl.at[k])
+            if cond is None:
+                cp.start()
+            else:
+                pl.when(cond)(cp.start)
+            local_out.append((cond, cp))
+
+    def spread_on(t):
+        for i in range(1, n):
+            q, dev = plane(i)
+            for k, area, fin in areas(t, q, c):
+                rc(fin, area, agx_s.at[k, i], agx_r.at[k, q], dev).wait_recv()
+                start(rc(area, area, agc_s.at[k, i], agc_r.at[k, q], partner))
+
+    def spread_end(t):
+        for i in range(n):
+            q = lax.rem(p + i, n)
+            for k, area, fin in areas(t, q, other):
+                rc(fin, area, agc_s.at[k, 0], agc_r.at[k, q], partner).wait_recv()
+
+    local_g.wait()
+    for i in range(1, n):
+        q, dev = plane(i)
+        rc(cot, seq(g_all, q), g_s.at[i], g_r.at[q], dev).wait_recv()
+
+    for j in range(s_n):
+        dwd[j] = dot(act[:, j * hb : (j + 1) * hb], g_all[...], TN).astype(BF)
+    exchange(2, dwd, xrd, hhalf)
+
+    table = [rot[i] for i in range(3)]
+
+    def turn(t, sign):
+        fwd = pltpu.roll(t, 128 - ROT // 2, 1)
+        back = pltpu.roll(t, ROT // 2, 1)
+        return t * table[0] + (fwd * table[1] + back * table[2]) * sign
+
+    def qkv_block(s):
+        row = pl.ds(mo(s * length, length), length)
+        left_a = a1[row, :]
+        for i in range(3):
+            bias = inb[:, pl.ds(mo(i * width + p * span, span), span)]
+            v = dot(left_a, w1[:, i * span : (i + 1) * span]) + bias
+            for h in range(span // 128):
+                part = v[:, h * 128 : (h + 1) * 128]
+                if i < 2:
+                    part = turn(part, 1.0)
+                qkv[row, i * span + h * 128 : i * span + (h + 1) * 128] = part.astype(BF)
+
+    relay(d_piece, d_s, d_r, dc_s, dc_r, 2)
+    lax.fori_loop(0, n, lambda s, _: (qkv_block(s), 0)[1], 0)
+    pair_sum(2, dwd, xrd, zrd, hhalf, s_n)
+
+    lane = lax.broadcasted_iota(jnp.int32, (1, 128), 1)
+    first = lane < HEAD_DIM
+    masks = [first.astype(F32).astype(BF), (1.0 - first.astype(F32)).astype(BF)]
+    pairs = span // 128
+
+    def att_forward(idx, carry):
+        s = lax.div(idx, pairs)
+        pr = lax.rem(idx, pairs)
+        row = pl.ds(mo(s * length, length), length)
+        q2 = qkv[row, pl.ds(mo(pr * 128, 128), 128)]
+        k2 = qkv[row, pl.ds(mo(span + pr * 128, 128), 128)]
+        v2 = qkv[row, pl.ds(mo(2 * span + pr * 128, 128), 128)]
+        key_i = lax.broadcasted_iota(jnp.int32, (length, length), 0)
+        query_i = lax.broadcasted_iota(jnp.int32, (length, length), 1)
+        got = []
+        for h in range(2):
+            st = dot(k2, q2 * masks[h], NT) * scale
+            ex = jnp.exp(jnp.where(key_i <= query_i, st, MASKED))
+            pr_t = ex / jnp.sum(ex, axis=0, keepdims=True)
+            pt[idx * 2 + h] = pr_t
+            got.append(dot(pr_t.astype(BF), v2, TN))
+        att[row, pl.ds(mo(pr * 128, 128), 128)] = jnp.where(first, got[0], got[1]).astype(BF)
+        return carry
+
+    lax.fori_loop(0, n * pairs, att_forward, 0)
+    relay(d_piece, d_s, d_r, dc_s, dc_r, 3)
+    dwo[0] = dot(att[...], g_all[...], TN).astype(BF)
+    exchange(3, dwo, xro, ohalf)
+
+    def o_relay():
+        away_left = zz < p
+        away_right = zz > p
+
+        @pl.when(jnp.logical_not(at_home))
+        def _():
+            rc(o_piece, o_piece, o_s.at[0], o_r.at[0], partner).wait_recv()
+
+        start(
+            rc(o_piece, o_piece, o_s.at[2], o_r.at[0], left), jnp.logical_and(away_left, has_left)
+        )
+        start(
+            rc(o_piece, o_piece, o_s.at[3], o_r.at[0], right),
+            jnp.logical_and(away_right, has_right),
+        )
+        start(
+            rc(o_piece, o_piece, oc_s.at[0], oc_r.at[0], partner), jnp.logical_not(at_home)
+        )
+
+        @pl.when(jnp.logical_not(at_home))
+        def _():
+            rc(o_other, o_other, oc_s.at[0], oc_r.at[0], partner).wait_recv()
+
+    o_relay()
+    relay_done(d_other, dc_s, dc_r)
+
+    bup_r[...] = jnp.zeros_like(bup_r)
+    bin_r[...] = jnp.zeros_like(bin_r)
+
+    def grad_block(s):
+        row = pl.ds(mo(s * length, length), length)
+        gs = g_all[row, :]
+        gatt[row, :] = dot(gs, wo[...], NT).astype(BF)
+        for j in range(s_n):
+            col = pl.ds(j * hb, hb)
+            gu = (dot(gs, wd[j * hb : (j + 1) * hb, :], NT) * der[row, col]).astype(BF)
+            gup[row, col] = gu
+            bup_r[:, col] += jnp.sum(gu.astype(F32), axis=0, keepdims=True)
+
+    lax.fori_loop(0, n, lambda s, _: (grad_block(s), 0)[1], 0)
+
+    for j in range(s_n):
+        dwu[j] = dot(a2[:, j * rs : (j + 1) * rs], gup[...], TN).astype(BF)
+    exchange(1, dwu, xru, half)
+
+    own_half = pl.ds(mo(c * ohalf, ohalf), ohalf)
+    rc(dwo.at[:, own_half], xro, xs_s.at[3], xs_r.at[3], partner).wait_recv()
+    xro[0] = (dwo[0, own_half].astype(F32) + xro[0].astype(F32)).astype(BF)
+    start(
+        rc(xro.at[0], zro.at[zz], zs_s.at[3, 0], zs_r.at[3, zz], (r, p)), jnp.logical_not(at_home)
+    )
+
+    def out_block(k, carry):
+        s = lax.rem(p + 1 + k, n)
+        row = pl.ds(mo(s * length, length), length)
+        for j in range(width // 256):
+            col = slice(j * 256, (j + 1) * 256)
+            v = dot(att[row, :], wo[:, col]) + dot(act[row, :], wd[:, col])
+            msend[k, :, col] = v.astype(BF)
+            mown[:, col] = v
+
+        @pl.when(k < n - 1)
+        def _():
+            rc(msend.at[k], mrecv.at[p], m_s.at[k], m_r.at[p], (2 * s + c, zz)).start()
+
+        return carry
+
+    lax.fori_loop(0, n, out_block, 0)
+    pair_sum(1, dwu, xru, zru, half, s_n)
+    line_sum(2, xrd, zrd, fd)
+    spread(2)
+
+    def att_backward(idx, carry):
+        s = lax.div(idx, pairs)
+        pr = lax.rem(idx, pairs)
+        row = pl.ds(mo(s * length, length), length)
+        q_col = pl.ds(mo(pr * 128, 128), 128)
+        k_col = pl.ds(mo(span + pr * 128, 128), 128)
+        v_col = pl.ds(mo(2 * span + pr * 128, 128), 128)
+        q2, k2, v2 = qkv[row, q_col], qkv[row, k_col], qkv[row, v_col]
+        g2 = gatt[row, q_col]
+        dq, dk, dv = [], [], []
+        for h in range(2):
+            pr_t = pt[idx * 2 + h]
+            dp = dot(v2, g2 * masks[h], NT)
+            inner = jnp.sum(dp * pr_t, axis=0, keepdims=True)
+            ds = (pr_t * (dp - inner)).astype(BF)
+            dv.append(dot(pr_t.astype(BF), g2))
+            dk.append(dot(ds, q2))
+            dq.append(dot(ds, k2, TN))
+        dqv = turn(jnp.where(first, dq[0], dq[1]) * scale, -1.0).astype(BF)
+        dkv = turn(jnp.where(first, dk[0], dk[1]) * scale, -1.0).astype(BF)
+        dvv = jnp.where(first, dv[0], dv[1]).astype(BF)
+        for col, val in ((q_col, dqv), (k_col, dkv), (v_col, dvv)):
+            gqkv[row, col] = val
+            bin_r[:, col] += jnp.sum(val.astype(F32), axis=0, keepdims=True)
+        return carry
+
+    lax.fori_loop(0, n * pairs, att_backward, 0)
+    for j in range(s_n):
+        dwi[j] = dot(a1[:, j * rs : (j + 1) * rs], gqkv[...], TN).astype(BF)
+    exchange(0, dwi, xri, half)
+
+    @pl.when(at_home)
+    def _():
+        total = xro[0].astype(F32)
+        for i in range(1, s_n):
+            q, dev = line(i)
+            rc(xro.at[0], zro.at[q], zs_s.at[3, 0], zs_r.at[3, q], dev).wait_recv()
+            total = total + zro[q].astype(F32)
+        fo[...] = total.astype(BF)
+
+    spread(3, at_home)
+    spread_on(2)
+
+    vacc[...] = jnp.zeros_like(vacc)
+
+    def in_block(k, carry):
+        s = lax.rem(p + 1 + k, n)
+        row = pl.ds(mo(s * length, length), length)
+        gq = gqkv[row, :]
+        gu = gup[row, :]
+        mu = mean_r[row, :]
+        inv = inv_r[row, :]
+        for j in range(s_n):
+            col = slice(j * rs, (j + 1) * rs)
+            d1 = dot(gq, w1[col, :iw], NT)
+            d2 = dot(gu, w1[col, iw:], NT)
+            xh = (x_all[row, col].astype(F32) - mu) * inv
+            vacc[0, :, col] += jnp.sum(d1 * xh, axis=0, keepdims=True)
+            vacc[1, :, col] += jnp.sum(d1, axis=0, keepdims=True)
+            vacc[2, :, col] += jnp.sum(d2 * xh, axis=0, keepdims=True)
+            vacc[3, :, col] += jnp.sum(d2, axis=0, keepdims=True)
+            e = d1 * gain1[:, col] + d2 * gain2[:, col]
+            esend[k, :, col] = e.astype(BF)
+            eown[:, col] = e
+
+        @pl.when(k < n - 1)
+        def _():
+            rc(esend.at[k], erecv.at[p], e_s.at[k], e_r.at[p], (2 * s + c, zz)).start()
+
+        return carry
+
+    pair_sum(0, dwi, xri, zri, half, s_n)
+    lax.fori_loop(0, n, in_block, 0)
+
+    slots = vfull.shape[0] // s_n
+    vfull[...] = jnp.zeros_like(vfull)
+    per = n_in // span
+    for i in range(3):
+        b = i * n + p
+        vfull[lax.div(b, per) * slots + lax.rem(b, per)] = bin_r[:, i * span : (i + 1) * span]
+    for q in range(s_n):
+        vfull[q * slots + per + p] = bup_r[:, q * hb : (q + 1) * hb]
+        col = slice(q * rs, (q + 1) * rs)
+        g_own = g_all[pl.ds(mo(p * length, length), length), col].astype(F32)
+        vfull[q * slots + per + n] = jnp.sum(g_own, axis=0, keepdims=True)
+        for i in range(4):
+            vfull[q * slots + per + n + 1 + i] = vacc[i, :, col]
+    for i in range(1, s_n):
+        q, dev = line(i)
+        start(rc(vfull.at[pl.ds(q * slots, slots)], vz.at[zz], v1_s.at[i], v1_r.at[zz], dev))
+
+    line_sum(1, xru, zru, fu)
+    spread(1)
+
+    for i in range(1, n):
+        q, dev = plane(i)
+        rc(msend.at[0], mrecv.at[q], m_s.at[0], m_r.at[q], dev).wait_recv()
+
+    def mixed_rows(i, carry):
+        step = 32
+        row = pl.ds(mo(i * step, step), step)
+        xv = x_all[pl.ds(mo(p * length + i * step, step), step), :].astype(F32)
+        t = mown[row, :]
+        for k in range(1, n):
+            t = t + mrecv[lax.rem(p + k, n), row, :].astype(F32)
+        mixed_o[row, :] = (xv + t + out_b + down_b).astype(BF)
+        return carry
+
+    lax.fori_loop(0, length // 32, mixed_rows, 0)
+
+    line_sum(0, xri, zri, fi)
+    spread(0)
+
+    total = [vfull[zz * slots + k] for k in range(slots)]
+    for i in range(1, s_n):
+        q, dev = line(i)
+        rc(vfull.at[pl.ds(0, slots)], vz.at[q], v1_s.at[i], v1_r.at[q], dev).wait_recv()
+        total = [t + vz[q, k] for k, t in enumerate(total)]
+    for k in range(slots):
+        vu[k] = total[k]
+        vr[r, k] = total[k]
+    for i in range(1, 2 * n):
+        start(rc(vu, vr.at[r], v2_s.at[i], v2_r.at[r], (lax.rem(r + i, 2 * n), zz)))
+
+    spread_on(1)
+
+    @pl.when(jnp.logical_not(at_home))
+    def _():
+        k, area, fin = areas(3, zz, c)[0]
+        rc(fin, area, agx_s.at[k, 0], agx_r.at[k, zz], partner).wait_recv()
+
+    k_o, area_o, _ = areas(3, zz, c)[0]
+    start(
+        rc(area_o, area_o, agc_s.at[k_o, 1], agc_r.at[k_o, zz], partner),
+        jnp.logical_not(at_home),
+    )
+
+    for i in range(1, n):
+        q, dev = plane(i)
+        rc(esend.at[0], erecv.at[q], e_s.at[0], e_r.at[q], dev).wait_recv()
+
+    def tgrad_rows(i, carry):
+        step = 32
+        row = pl.ds(mo(i * step, step), step)
+        far = pl.ds(mo(p * length + i * step, step), step)
+        inv = inv_r[far, :]
+        xh = (x_all[far, :].astype(F32) - mean_r[far, :]) * inv
+        e = eown[row, :]
+        for k in range(1, n):
+            e = e + erecv[lax.rem(p + k, n), row, :].astype(F32)
+        m0 = jnp.mean(e, axis=1, keepdims=True)
+        m1 = jnp.mean(e * xh, axis=1, keepdims=True)
+        tgrad_o[row, :] = g_all[far, :].astype(F32) + inv * (e - m0 - xh * m1)
+        return carry
+
+    lax.fori_loop(0, length // 32, tgrad_rows, 0)
+
+    for i in range(1, 2 * n):
+        q = lax.rem(r + i, 2 * n)
+        rc(vu, vr.at[q], v2_s.at[i], v2_r.at[q], (q, zz)).wait_recv()
+    for k in range(slots):
+        t = vr[0, k]
+        for q in range(1, 2 * n):
+            t = t + vr[q, k]
+        vec_o[k] = t
+
+    spread_on(0)
+    for t in (2, 1, 0):
+        spread_end(t)
+    k, area, fin = areas(3, zz, other)[0]
+    rc(fin, area, agc_s.at[k, 0], agc_r.at[k, zz], partner).wait_recv()
+
+    for cond, cp in local_out:
+        if cond is None:
+            cp.wait()
+        else:
+            pl.when(cond)(cp.wait)
+    for k in range(n - 1):
+        rc(msend.at[k], mrecv.at[p], m_s.at[k], m_r.at[p], partner).wait_send()
+        rc(esend.at[k], erecv.at[p], e_s.at[k], e_r.at[p], partner).wait_send()
+    for cond, cp in sends:
+        if cond is None:
+            cp.wait_send()
+        else:
+            pl.when(cond)(cp.wait_send)
+
+
+def fused_call(z, tok, cot, inp, upp, outp, downp, vec):
+    n, s_n, length, width, span, hid = z.n, z.s, z.l, z.d, z.span, z.hid
+    rs, hb, rows = z.rs, z.hb, z.rows
+    iw = 3 * span
+    nv = vec.shape[-1]
+    slots = 3 * width // s_n // span + n + 5
+    kinds = 5 + s_n
+    V = pltpu.VMEM
+    dma = lambda *shape: pltpu.SemaphoreType.DMA(shape)
+    scratch = [
+        *[V((rows, width), BF)] * 4,
+        V((width, iw + hid), BF), V((span, width), BF), V((hid, width), BF),
+        V((rows, iw), BF), V((n * span // HEAD_DIM, length, length), F32),
+        V((rows, hid), F32), V((rows, hid), BF), V((rows, span), BF),
+        V((rows, span), BF), V((rows, hid), BF), V((rows, iw), BF),
+        *[V((n, length, width), BF), V((n, length, width), BF), V((length, width), F32)] * 2,
+        V((s_n, rs, iw), BF), V((s_n, rs, hid), BF), V((s_n, hb, width), BF), V((1, span, width), BF),
+        V((s_n, rs // 2, iw), BF), V((s_n, rs // 2, hid), BF), V((s_n, hb // 2, width), BF), V((1, span // 2, width), BF),
+        V((s_n, rs // 2, iw), BF), V((s_n, rs // 2, hid), BF), V((s_n, hb // 2, width), BF), V((s_n, span // 2, width), BF),
+        V((rs // 2, iw), BF), V((rs // 2, hid), BF), V((hb // 2, width), BF), V((span // 2, width), BF),
+        V((s_n, 1, nv), F32), V((1, 3 * width), F32), V((s_n * slots, 1, 256), F32),
+        V((s_n, slots, 1, 256), F32), V((slots, 1, 256), F32), V((2 * n, slots, 1, 256), F32),
+        V((rows, 1), F32), V((rows, 1), F32), V((4, 1, width), F32), V((1, iw), F32), V((1, hid), F32),
+        dma(8 + s_n), dma(s_n), dma(s_n), dma(n), dma(n), dma(n), dma(n),
+        dma(2 * s_n), dma(s_n), dma(2 * s_n), dma(s_n),
+        dma(2 * s_n), dma(s_n), dma(2 * s_n), dma(s_n),
+        dma(4), dma(1), dma(1), dma(1),
+        dma(n), dma(n), dma(n), dma(n), dma(4), dma(4), dma(4, s_n), dma(4, s_n),
+        dma(kinds, n), dma(kinds, n), dma(kinds, n), dma(kinds, n), dma(kinds),
+        dma(s_n), dma(s_n), dma(2 * n), dma(2 * n),
+    ]
+    any_ = pl.BlockSpec(memory_space=pl.ANY)
+    vm = pl.BlockSpec(memory_space=pltpu.VMEM)
+    outs = [
+        jax.ShapeDtypeStruct((length, width), BF),
+        jax.ShapeDtypeStruct((length, width), F32),
+        jax.ShapeDtypeStruct((rs, 3 * width), BF),
+        jax.ShapeDtypeStruct((rs, z.ff), BF),
+        jax.ShapeDtypeStruct((hb * n, width), BF),
+        jax.ShapeDtypeStruct((span, width), BF),
+        jax.ShapeDtypeStruct((slots, 1, 256), F32),
+    ]
+    return pl.pallas_call(
+        functools.partial(fused, z),
+        out_shape=outs,
+        in_specs=[any_] * 7 + [vm],
+        out_specs=[vm, vm, any_, any_, any_, any_, vm],
+        scratch_shapes=scratch,
+        compiler_params=pltpu.CompilerParams(
+            collective_id=0, has_side_effects=True, vmem_limit_bytes=VMEM_LIMIT
+        ),
+        name="block_step",
+    )(tok, cot, inp, upp, outp, downp, vec, jnp.asarray(rotary_lanes(length)))
+
+
+def make_fused_body(z):
+    def body(
+        tokens, in_proj, in_bias, out_proj, out_bias, up_proj, up_bias, down_proj, down_bias,
+        first_gain, first_shift, second_gain, second_shift, cotangent,
+    ):
+        vec = jnp.concatenate(
+            [in_bias, up_bias, out_bias, down_bias, first_gain, first_shift, second_gain, second_shift]
+        ).astype(F32)[None]
+        mixed, tgrad, g_in, g_up, g_down, g_out, vg = fused_call(
+            z, tokens, cotangent, in_proj, up_proj, out_proj, down_proj, vec
+        )
+        per = in_bias.shape[0] // z.span
+        flat = vg.reshape(-1)
+        cut = lambda a, b: flat[a * 256 : b * 256]
+        at = per + z.n
+        bias = cut(at, at + 1)
+        return (
+            mixed, tgrad, g_in.astype(F32), cut(0, per), g_out.astype(F32), bias, g_up.astype(F32),
+            cut(per, at), g_down.astype(F32), bias,
+            cut(at + 1, at + 2), cut(at + 2, at + 3), cut(at + 3, at + 4), cut(at + 4, at + 5),
+        )
+
+    return body
+
+
 def solution(mesh):
     rows = P(("rep", "shard"), None)
     mat = P("shard", None)
     vec = P("shard")
     in_specs = (rows, mat, vec, mat, vec, mat, vec, mat, vec, vec, vec, vec, vec, rows)
     out_specs = (rows, rows, mat, vec, mat, vec, mat, vec, mat, vec, vec, vec, vec, vec)
-    return jax.shard_map(
-        make_body(mesh.shape["shard"]),
-        mesh=mesh,
-        in_specs=in_specs,
-        out_specs=out_specs,
-        check_vma=False,
-    )
+    shape = dict(mesh.shape)
+
+    def step(*args):
+        tokens, up_proj = args[0], args[5]
+        devices = shape["rep"] * shape["shard"]
+        z = Sizes(shape, tokens.shape[0] // devices, tokens.shape[1], up_proj.shape[1])
+        body = make_fused_body(z) if z.fits() else make_body(shape["shard"])
+        return jax.shard_map(
+            body, mesh=mesh, in_specs=in_specs, out_specs=out_specs, check_vma=False
+        )(*args)
+
+    return step

time: 617 us -> 231 us (0.37)
  waiting for transfers between devices: 251 us -> 0 us
  Pallas kernels: 0 us -> 205 us
  blocking collectives: 170 us -> 0 us
  matrix products: 60.1 us -> 0 us
  local copies, waits for them, and re-layouts: 68.6 us -> 11.5 us
  starting transfers between devices: 21.3 us -> 0 us
  other arithmetic: 27.3 us -> 10.4 us
  between operations: 14.7 us -> 0.67 us
    pallas_call x0 -> x1, Pallas kernels: none -> 205 us  [fused_call(): pl.pallas_call(functools.partial(fused, z), out_shape=outs, in_specs=[any...]
    all_to_all x4 -> x0, waiting for transfers between devices: 151 us -> none  [the longest x1 75.6 us: body(): lax.all_to_all(dw_in.reshape(parts * rows, 3, 1, span), 'shard', 0, 2, ti...]
    psum x1 -> x0, waiting for transfers between devices: 99.9 us -> none  [body(): lax.psum((dw_in, dw_up, dw_out, dw_down), 'rep')]
    unnamed x1 -> x0, blocking collectives: 79.7 us -> none
    all_gather x1 -> x0, blocking collectives: 68.2 us -> none  [body(): vectors = lax.all_gather(vectors, 'shard', axis=0).astype(jnp.float32)]
    dot_general x18 -> x0, matrix products: 60.1 us -> none  [the longest x12 53.3 us: mm(): lax.dot_general(left, right, (dims, ((), ())), preferred_element_type=jnp...]
    psum x1 -> x0, blocking collectives: 22.3 us -> none  [body(): vec, up_vec = lax.psum((vec, jnp.sum(grad_up, axis=0, dtype=f32)), 'rep')]
    all_to_all x4 -> x0, starting transfers between devices: 21 us -> none  [the longest x1 6.35 us: body(): lax.all_to_all(in_proj.reshape(rows, 3, parts, span), 'shard', 2, 0, tile...]
  transfers between devices with their start and end apart: 8 -> 0, of which waited for: 3 -> 0; matrix products, arithmetic and copies ran while one was open for 10% -> 0% of each run, Pallas kernels for 0% -> 0%
where the time goes in v2:
time: 231 us; the launch traced here: 228 us
  Pallas kernels  205 us (89%)
  local copies, waits for them, and re-layouts  11.5 us (5%)
  other arithmetic  10.4 us (5%)
    pallas_call x1, Pallas kernels, fused_call(): pl.pallas_call(functools.partial(fused, z), out_shape=outs, in_specs=[any...  205 us
    unnamed x22, local copies, waits for them, and re-layouts  7.04 us

profile of v2, /device:TPU:0, one launch (start us, length us, event | category | flops | bytes accessed | tf_op | source)
XLA Modules:
  0.0 228.1 jit_solution(8240357995039980772)
XLA Ops:
  0.6 0.7 constant_dynamic-update-slice_fusion.7
  1.3 0.7 constant_dynamic-update-slice_fusion.6
  2.0 0.7 constant_dynamic-update-slice_fusion.5
  2.7 0.7 constant_dynamic-update-slice_fusion.4
  3.4 0.7 constant_dynamic-update-slice_fusion.3
  4.0 0.7 constant_dynamic-update-slice_fusion.2
  4.7 0.7 constant_dynamic-update-slice_fusion.1
  5.3 0.7 constant_dynamic-update-slice_fusion
  6.0 0.6 convert_element_type.22.refs_6_
  6.6 205.4 %block_step.1 = (bf16[256,1024]{1,0:T(8,128)(2,1)}, f32[256,1024]{1,0:T(8,128)}, bf16[256,3072]{1,0:T(8,128)(2,1)}, bf16[256,4096]{1,0:T(8,128)(2,1)}, bf16[1024...) custom-call(bf16[256,1024]{1,0:T(8,128)(2,1)} %refs_0_.1, bf16[256,1024]{1,0:T(8,128)(2,1)} %refs_1_.1, ...), custom_call_target="tpu_custom_call" | custom-call | tf_op jit(solution)/shard_map/block_step/pallas_call | solution.py:888
  212.1 1.3 fusion
  213.3 0.0 copy-start.5
  213.3 0.7 slice_reduce_fusion
  214.0 0.6 slice.43
  214.6 1.3 slice.46
  215.9 0.0 copy-start
  215.9 4.2 %convert_element_type.25 = f32[256,4096]{1,0:T(8,128)} convert(bf16[256,4096]{1,0:T(8,128)(2,1)} %get-tuple-element.26) | non-fusion elementwise | flops 1048576 | bytes 6291456 | tf_op jit(solution)/shard_map/convert_element_type | solution.py:918
  220.1 0.0 copy-done
  220.1 0.0 copy-start.1
  220.2 2.5 %convert_element_type.26 = f32[1024,1024]{1,0:T(8,128)} convert(bf16[1024,1024]{1,0:T(8,128)(2,1)S(1)} %copy-done) | non-fusion elementwise | flops 1048576 | bytes 6291456 | tf_op jit(solution)/shard_map/convert_element_type | solution.py:919
  222.6 0.0 copy-done.1
  222.6 0.0 copy-start.3
  222.6 0.0 copy-start.4
  222.6 2.0 convert_element_type.23
  224.7 0.0 copy-start.2
  224.7 0.0 copy-done.3
  224.7 1.1 convert_element_type.24
  225.7 0.0 copy-done.5
  225.7 0.6 copy.39
  226.3 0.0 copy-done.4
  226.3 0.8 copy.40
  227.1 0.0 copy-done.2
  227.1 1.0 copy.41
Async XLA Ops:
  213.3 12.4 %copy-start.5 = (f32[1,1,256]{2,1,0:T(1,128)}, f32[1,1,256]{2,1,0:T(1,128)S(1)}, u32[]{:S(2)}) copy-start(f32[1,1,256]{2,1,0:T(1,128)S(1)} %get-tuple-element.32) | copy-start | bytes 3076
  215.9 4.3 %copy-start = (bf16[1024,1024]{1,0:T(8,128)(2,1)S(1)}, bf16[1024,1024]{1,0:T(8,128)(2,1)}, u32[]{:S(2)}) copy-start(bf16[1024,1024]{1,0:T(8,128)(2,1)} %get-tuple-element.27) | copy-start | bytes 6291460
  220.1 2.5 %copy-start.1 = (bf16[256,3072]{1,0:T(8,128)(2,1)S(1)}, bf16[256,3072]{1,0:T(8,128)(2,1)}, u32[]{:S(2)}) copy-start(bf16[256,3072]{1,0:T(8,128)(2,1)} %get-tuple-element.23) | copy-start | bytes 4718596
  222.6 2.0 copy-start.3
  222.6 3.7 %copy-start.4 = (bf16[256,1024]{1,0:T(8,128)(2,1)S(1)}, bf16[256,1024]{1,0:T(8,128)(2,1)}, u32[]{:S(2)}) copy-start(bf16[256,1024]{1,0:T(8,128)(2,1)} %get-tuple-element.75) | copy-start | bytes 1572868
  224.7 2.5 %copy-start.2 = (f32[256,1024]{1,0:T(8,128)S(1)}, f32[256,1024]{1,0:T(8,128)}, u32[]{:S(2)}) copy-start(f32[256,1024]{1,0:T(8,128)} %get-tuple-element.76) | copy-start | bytes 3145732

commit v3 on v2

v3 whole, which is shorter than its diff:
```python
import functools

import jax
import jax.numpy as jnp
import numpy as np
from jax import lax
from jax.experimental import pallas as pl
from jax.experimental.pallas import tpu as pltpu
from jax.sharding import PartitionSpec as P

HEAD_DIM = 64
ROT = 16
EPS = 1e-05
MASKED = -1e30


def rotary_tables(length):
    half = ROT // 2
    inverse = jnp.exp(-jnp.log(10000.0) * (2.0 * jnp.arange(half, dtype=jnp.float32) / ROT))
    angles = jnp.arange(length, dtype=jnp.float32)[:, None] * inverse[None, :]
    return (jnp.cos(angles)[:, None, :], jnp.sin(angles)[:, None, :])


def rotate(values, cosine, sine, sign):
    half = ROT // 2
    first = values[..., :half]
    second = values[..., half:ROT]
    return jnp.concatenate(
        [
            first * cosine - sign * second * sine,
            second * cosine + sign * first * sine,
            values[..., ROT:],
        ],
        axis=-1,
    )


def mm(left, right, dims=((1,), (0,))):
    return lax.dot_general(left, right, (dims, ((), ())), preferred_element_type=jnp.float32)


def make_body(parts):
    def body(
        tokens,
        in_proj,
        in_bias,
        out_proj,
        out_bias,
        up_proj,
        up_bias,
        down_proj,
        down_bias,
        first_gain,
        first_shift,
        second_gain,
        second_shift,
        cotangent,
    ):
        length, width = tokens.shape
        me = lax.axis_index("shard")
        heads = width // parts // HEAD_DIM
        span = width // parts
        rows = in_proj.shape[0]
        hidden = up_bias.shape[0]
        scale = HEAD_DIM ** (-0.5)
        vectors = jnp.concatenate(
            [in_bias, out_bias, down_bias, first_gain, first_shift, second_gain, second_shift]
        )
        vectors = lax.all_gather(vectors, "shard", axis=0).astype(jnp.float32)
        cuts = [in_bias.shape[0]] + [span] * 6
        offsets = [sum(cuts[:i]) for i in range(len(cuts))]
        whole = [vectors[:, o : o + c].reshape(-1) for o, c in zip(offsets, cuts)]
        in_b, out_b, down_b, gain1, shift1, gain2, shift2 = whole
        both = lax.all_gather(jnp.stack([tokens, cotangent]), "shard", axis=1, tiled=True)
        x_all, g_all = both[0], both[1]
        w_in = lax.all_to_all(
            in_proj.reshape(rows, 3, parts, span), "shard", 2, 0, tiled=True
        ).reshape(parts * rows, 3 * span)
        w_up = lax.all_to_all(up_proj, "shard", 1, 0, tiled=True)
        b_in = lax.dynamic_slice_in_dim(in_b.reshape(3, parts, span), me, 1, axis=1).reshape(-1)
        x = x_all.astype(jnp.float32)
        mean = jnp.mean(x, axis=1, keepdims=True)
        cen = x - mean
        inv = lax.rsqrt(jnp.mean(cen * cen, axis=1, keepdims=True) + EPS)
        xhat = cen * inv
        attn_in = (xhat * gain1 + shift1).astype(jnp.bfloat16)
        mlp_in = (xhat * gain2 + shift2).astype(jnp.bfloat16)
        total_rows = x.shape[0]
        qkv = (mm(attn_in, w_in) + b_in).reshape(parts, length, 3, heads, HEAD_DIM)
        cosine, sine = rotary_tables(length)
        query = rotate(qkv[:, :, 0], cosine, sine, 1.0).astype(jnp.bfloat16)
        keys = rotate(qkv[:, :, 1], cosine, sine, 1.0).astype(jnp.bfloat16)
        values = qkv[:, :, 2].astype(jnp.bfloat16)
        causal = jnp.arange(length)[:, None] >= jnp.arange(length)[None, :]

        def ein(eq, a, b):
            return jnp.einsum(eq, a, b, preferred_element_type=jnp.float32)

        scores = jnp.where(causal, ein("sqhd,skhd->shqk", query, keys) * scale, MASKED)
        expo = jnp.exp(scores)
        probs_full = expo / jnp.sum(expo, axis=-1, keepdims=True)
        probs = probs_full.astype(jnp.bfloat16)
        attended = ein("shqk,skhd->sqhd", probs, values).astype(jnp.bfloat16)
        attended = attended.reshape(total_rows, span)
        up = mm(mlp_in, w_up) + up_bias.astype(jnp.float32)
        activated, pull = jax.vjp(lambda t: jax.nn.gelu(t, approximate=False), up)
        activated = activated.astype(jnp.bfloat16)
        partial = mm(attended, out_proj) + mm(activated, down_proj)
        branch = lax.psum_scatter(
            partial.astype(jnp.bfloat16), "shard", scatter_dimension=0, tiled=True
        )
        mixed = (tokens.astype(jnp.float32) + branch.astype(jnp.float32) + out_b + down_b).astype(
            jnp.bfloat16
        )
        grad_att = mm(g_all, out_proj, ((1,), (1,))).astype(jnp.bfloat16)
        grad_att = grad_att.reshape(parts, length, heads, HEAD_DIM)
        grad_act = mm(g_all, down_proj, ((1,), (1,)))
        grad_up = pull(grad_act)[0].astype(jnp.bfloat16)
        d_probs = ein("sqhd,skhd->shqk", grad_att, values)
        d_values = ein("shqk,sqhd->skhd", probs, grad_att)
        inner = jnp.sum(d_probs * probs_full, axis=-1, keepdims=True)
        d_scores = (probs_full * (d_probs - inner)).astype(jnp.bfloat16)
        d_query = ein("shqk,skhd->sqhd", d_scores, keys) * scale
        d_keys = ein("shqk,sqhd->skhd", d_scores, query) * scale
        d_query = rotate(d_query, cosine, sine, -1.0)
        d_keys = rotate(d_keys, cosine, sine, -1.0)
        grad_qkv = jnp.stack([d_query, d_keys, d_values], axis=2).astype(jnp.bfloat16)
        grad_qkv = grad_qkv.reshape(total_rows, 3 * span)
        d1 = mm(grad_qkv, w_in, ((1,), (1,)))
        d2 = mm(grad_up, w_up, ((1,), (1,)))
        scaled = (d1 * gain1 + d2 * gain2).astype(jnp.bfloat16)
        e = lax.psum_scatter(scaled, "shard", scatter_dimension=0, tiled=True).astype(jnp.float32)
        own = lambda a: lax.dynamic_slice_in_dim(a, me * length, length, axis=0)
        xh, rv = own(xhat), own(inv)
        tokens_grad = cotangent.astype(jnp.float32) + rv * (
            e - jnp.mean(e, axis=1, keepdims=True) - xh * jnp.mean(e * xh, axis=1, keepdims=True)
        )
        left = ((0,), (0,))
        dw_in = mm(attn_in, grad_qkv, left).astype(jnp.bfloat16)
        dw_up = mm(mlp_in, grad_up, left).astype(jnp.bfloat16)
        dw_out = mm(attended, g_all, left).astype(jnp.bfloat16)
        dw_down = mm(activated, g_all, left).astype(jnp.bfloat16)
        dw_in, dw_up, dw_out, dw_down = lax.psum((dw_in, dw_up, dw_out, dw_down), "rep")
        dw_in = lax.all_to_all(
            dw_in.reshape(parts * rows, 3, 1, span), "shard", 0, 2, tiled=True
        ).reshape(rows, 3 * width)
        dw_up = lax.all_to_all(dw_up, "shard", 0, 1, tiled=True)
        f32 = jnp.float32
        place = lambda v: lax.dynamic_update_slice_in_dim(
            jnp.zeros((3, parts, span), f32), v.reshape(3, 1, span), me, axis=1
        ).reshape(-1)
        vec = [
            place(jnp.sum(grad_qkv, axis=0, dtype=f32)),
            jnp.sum(cotangent.astype(f32), axis=0),
            jnp.sum(d1 * xhat, axis=0),
            jnp.sum(d1, axis=0),
            jnp.sum(d2 * xhat, axis=0),
            jnp.sum(d2, axis=0),
        ]
        vec = jnp.concatenate([v.reshape(parts, -1) for v in vec], axis=1)
        vec = lax.psum_scatter(vec, "shard", scatter_dimension=0, tiled=True)[0]
        vec, up_vec = lax.psum((vec, jnp.sum(grad_up, axis=0, dtype=f32)), "rep")
        o = in_bias.shape[0]
        bias_grad = vec[o : o + span]
        rest = [vec[o + span * i : o + span * (i + 1)] for i in range(1, 5)]
        return (
            mixed,
            tokens_grad,
            dw_in.astype(f32),
            vec[:o],
            dw_out.astype(f32),
            bias_grad,
            dw_up.astype(f32),
            up_vec,
            dw_down.astype(f32),
            bias_grad,
            *rest,
        )

    return body


BF = jnp.bfloat16
F32 = jnp.float32
MESH = pl.DeviceIdType.MESH
VMEM_LIMIT = 67_000_000
NN = ((1,), (0,))
NT = ((1,), (1,))
TN = ((0,), (0,))
IN, UP, DOWN, OUT = range(4)


class Sizes:
    def __init__(self, mesh_shape, length, width, hidden):
        self.copies = mesh_shape["rep"]
        self.n = self.copies // 2
        self.s = mesh_shape["shard"]
        self.l = length
        self.d = width
        self.ff = hidden
        self.span = width // self.n
        self.hid = hidden // self.n
        self.rs = width // self.s
        self.hb = hidden // self.s // self.n
        self.rows = self.n * length

    def fits(self):
        return (
            self.copies == 8
            and self.s == 4
            and self.rs == 256
            and self.span == 256
            and self.hb == 256
            and self.l % 256 == 0
        )


def rotary_lanes(length):
    half = ROT // 2
    inverse = np.exp(-np.log(10000.0) * (2.0 * np.arange(half) / ROT))
    angles = np.arange(length)[:, None] * inverse[None, :]
    cosine, sine = np.cos(angles), np.sin(angles)
    table = np.zeros((3, length, 128), np.float32)
    table[0] = 1.0
    for start in (0, HEAD_DIM):
        table[0, :, start : start + half] = cosine
        table[0, :, start + half : start + ROT] = cosine
        table[1, :, start : start + half] = -sine
        table[2, :, start + half : start + ROT] = sine
    return table


def dot(left, right, dims=NN):
    return lax.dot_general(left, right, (dims, ((), ())), preferred_element_type=F32)


def mo(value, m):
    return pl.multiple_of(value, m)


def fused(z, *refs):
    (tok, cot, inp, upp, outp, downp) = refs[:6]
    vectors_in, rot = refs[6:14], refs[14]
    (mixed_o, tgrad_o, gin_o, gup_o, gdown_o, gout_o, vec_o) = refs[15:22]
    (
        x_all, g_all, a1, a2, wi, wu, wo, wd, qkv, pt, der, act, att, gatt, gup, gqkv,
        msend, mrecv, mpre, mown, esend, erecv, epre, eown,
        dwi, dwu, dwd, dwo, xri, xru, xrd, xro, zri, zru, zrd, zro, fi, fu, fd, fo,
        vec, va, inb, vfull, vz, vu, vr, mean_r, inv_r, vacc, bin_r, bup_r,
        loc, v_s, v_r, x_s, x_r, g_s, g_r, w_s, w_r, wc_s, wc_r,
        o_s, o_r, oc_s, oc_r, m_s, m_r, e_s, e_r, xs_s, xs_r, zs_s, zs_r,
        ag_s, ag_r, agc_s, agc_r, agl, v1_s, v1_r, v2_s, v2_r,
    ) = refs[22:]
    n, s_n, length, width = z.n, z.s, z.l, z.d
    span, hid, rs, hb = z.span, z.hid, z.rs, z.hb
    iw = 3 * span
    scale = HEAD_DIM**-0.5
    r = lax.axis_index("rep")
    zz = lax.axis_index("shard")
    p = lax.div(r, 2)
    c = lax.rem(r, 2)
    other = 1 - c
    partner = (2 * p + other, zz)
    py, px = lax.div(p, 2), lax.rem(p, 2)
    xn, yn, dg = 2 * py + 1 - px, 2 * (1 - py) + px, 2 * (1 - py) + 1 - px
    dev_x, dev_y = (2 * xn + c, zz), (2 * yn + c, zz)
    zp, zo = lax.div(zz, 2), lax.rem(zz, 2)
    is_end = zp == zo
    inner = zp != zo
    mate = 2 * zp + 1 - zo
    mate_dev = (r, mate)
    far_end, far_inner = 3 * (1 - zp), 2 - zp
    left, right = (r, zz - 1), (r, zz + 1)
    has_left, has_right = zz > 0, zz < s_n - 1

    def rc(src, dst, ss, rr, dev):
        return pltpu.make_async_remote_copy(
            src_ref=src, dst_ref=dst, send_sem=ss, recv_sem=rr, device_id=dev, device_id_type=MESH
        )

    def got(ref, rr):
        rc(ref, ref, rr, rr, partner).wait_recv()

    def seq(ref, s):
        return ref.at[pl.ds(mo(s * length, length), length)]

    sends = []

    def start(copy, cond=None):
        if cond is None:
            copy.start()
        else:
            pl.when(cond)(copy.start)
        sends.append((cond, copy))

    own_rows = pl.ds(mo(zz * rs, rs), rs)
    own_hb = pl.ds(mo(zz * hb, hb), hb)
    local_u = [
        pltpu.make_async_copy(
            upp.at[:, pl.ds(mo(i * (hb * n) + p * hb, hb), hb)],
            wu.at[own_rows, pl.ds(i * hb, hb)],
            loc.at[i],
        )
        for i in range(s_n)
    ]
    local_i = [
        pltpu.make_async_copy(
            inp.at[:, pl.ds(mo(i * width + p * span, span), span)],
            wi.at[own_rows, pl.ds(i * span, span)],
            loc.at[s_n + i],
        )
        for i in range(3)
    ]
    at_loc = s_n + 3
    local_d = pltpu.make_async_copy(
        downp.at[pl.ds(mo(p * hb, hb), hb)], wd.at[own_hb], loc.at[at_loc]
    )
    local_x = pltpu.make_async_copy(tok, seq(x_all, p), loc.at[at_loc + 1])
    local_g = pltpu.make_async_copy(cot, seq(g_all, p), loc.at[at_loc + 2])
    local_o = pltpu.make_async_copy(outp, wo, loc.at[at_loc + 3])
    at_home = zz == p
    away = jnp.logical_not(at_home)
    for cp in local_u + [local_x, local_g, local_d] + local_i:
        cp.start()
    pl.when(at_home)(local_o.start)
    off = 0
    for ref in vectors_in:
        size = ref.shape[0]
        vec[:, off : off + size] = ref[...].astype(F32).reshape(1, size)
        off += size

    barrier = pltpu.get_barrier_semaphore()
    for i in range(1, 2 * n):
        pl.semaphore_signal(
            barrier, 1, device_id=(lax.rem(r + i, 2 * n), zz), device_id_type=MESH
        )
    for i in range(1, s_n):
        pl.semaphore_signal(barrier, 1, device_id=(r, lax.rem(zz + i, s_n)), device_id_type=MESH)
    pl.semaphore_wait(barrier, 2 * n - 1 + s_n - 1)

    def line(i):
        q = lax.rem(zz + i, s_n)
        return q, (r, q)

    def plane_send(src, dst, ss, rr, cond=None):
        start(rc(src(0), dst(p, 0), ss(0), rr(p, 0), dev_x), cond)
        start(rc(src(1), dst(p, 1), ss(1), rr(p, 1), dev_y), cond)
        start(rc(src(1), dst(p, 1), ss(2), rr(p, 1), dev_x), cond)
        start(rc(src(0), dst(p, 0), ss(3), rr(p, 0), dev_y), cond)

    def plane_relay(dst, ss, rr):
        got(dst(xn, 0), rr(xn, 0))
        start(rc(dst(xn, 0), dst(xn, 0), ss(4), rr(xn, 0), dev_y))
        got(dst(yn, 1), rr(yn, 1))
        start(rc(dst(yn, 1), dst(yn, 1), ss(5), rr(yn, 1), dev_x))

    def plane_near(dst, rr):
        got(dst(xn, 1), rr(xn, 1))
        got(dst(yn, 0), rr(yn, 0))

    def plane_far(dst, rr):
        got(dst(dg, 0), rr(dg, 0))
        got(dst(dg, 1), rr(dg, 1))

    lh = length // 2

    def part(ref):
        return lambda q, h: ref.at[pl.ds(mo(q * length + h * lh, lh), lh)]

    def sem1(ref):
        return lambda i: ref.at[i]

    def sem2(ref):
        return lambda q, h: ref.at[q, h]

    def rows_of(ref):
        return lambda h: ref.at[pl.ds(h * lh, lh)]

    for i in range(1, s_n):
        q, dev = line(i)
        start(rc(vec, va.at[zz], v_s.at[i], v_r.at[zz], dev))
    plane_send(rows_of(tok), part(x_all), sem1(x_s), sem2(x_r))

    half, hhalf, ohalf = rs // 2, hb // 2, span // 2

    def piece(ref, block):
        return lambda q, core: ref.at[pl.ds(mo(q * block + core * (block // 2), block // 2), block // 2)]

    u_piece, d_piece, i_piece = piece(wu, rs), piece(wd, hb), piece(wi, rs)

    def own_sends(t, get):
        start(rc(get(zz, c), get(zz, c), w_s.at[t, 0], w_r.at[t, zz], left), has_left)
        start(rc(get(zz, c), get(zz, c), w_s.at[t, 1], w_r.at[t, zz], right), has_right)

    def relay(t, get, d):
        def take(q, has, onward, more, slot):
            @pl.when(has)
            def _():
                got(get(q, c), w_r.at[t, q])

            start(
                rc(get(q, c), get(q, c), w_s.at[t, slot], w_r.at[t, q], onward),
                jnp.logical_and(has, more),
            )
            start(rc(get(q, c), get(q, c), wc_s.at[t, slot], wc_r.at[t, q], partner), has)

        take(zz - d, zz - d >= 0, right, has_right, 2 * d)
        take(zz + d, zz + d <= s_n - 1, left, has_left, 2 * d + 1)

    def relay_done(t, get):
        for i in range(1, s_n):
            q, _ = line(i)
            got(get(q, other), wc_r.at[t, q])

    for cp in local_u:
        cp.wait()
    own_sends(UP, u_piece)

    for i in range(1, s_n):
        q, dev = line(i)
        got(va.at[q], v_r.at[q])
    va[zz] = vec[...]
    n_in = 3 * width // s_n
    n_up = hb * n
    at_up = n_in
    at_rest = n_in + n_up

    def vector(i):
        off = at_rest + i * rs
        return jnp.concatenate([va[q, :, off : off + rs] for q in range(s_n)], axis=1)

    out_b, down_b, gain1, shift1, gain2, shift2 = [vector(i) for i in range(6)]
    for q in range(s_n):
        inb[:, q * n_in : (q + 1) * n_in] = va[q, :, :n_in]

    def norm(s):
        step = 32

        def body(i, carry):
            row = pl.ds(mo(s * length + i * step, step), step)
            xv = x_all[row, :].astype(F32)
            mu = jnp.mean(xv, axis=1, keepdims=True)
            cen = xv - mu
            inv = lax.rsqrt(jnp.mean(cen * cen, axis=1, keepdims=True) + EPS)
            xh = cen * inv
            a1[row, :] = (xh * gain1 + shift1).astype(BF)
            a2[row, :] = (xh * gain2 + shift2).astype(BF)
            mean_r[row, :] = mu
            inv_r[row, :] = inv
            return carry

        lax.fori_loop(0, length // step, body, 0)

    local_x.wait()
    norm(p)
    relay(UP, u_piece, 1)
    plane_relay(part(x_all), sem1(x_s), sem2(x_r))
    plane_send(rows_of(cot), part(g_all), sem1(g_s), sem2(g_r))
    relay(UP, u_piece, 2)
    local_d.wait()
    own_sends(DOWN, d_piece)
    plane_near(part(x_all), sem2(x_r))
    norm(xn)
    norm(yn)
    plane_far(part(x_all), sem2(x_r))
    norm(dg)
    relay(UP, u_piece, 3)
    relay_done(UP, u_piece)

    def up_block(s):
        row = pl.ds(mo(s * length, length), length)
        left_a = a2[row, :]
        for j in range(s_n):
            col = pl.ds(j * hb, hb)
            bias = va[j, :, pl.ds(mo(at_up + p * hb, hb), hb)]
            u = dot(left_a, wu[:, j * hb : (j + 1) * hb]) + bias
            phi = 0.5 * (1.0 + lax.erf(u * 0.7071067811865476))
            act[row, col] = (u * phi).astype(BF)
            der[row, col] = phi + u * (0.3989422804014327 * jnp.exp(-0.5 * u * u))

    lax.fori_loop(0, n, lambda s, _: (up_block(s), 0)[1], 0)

    relay(DOWN, d_piece, 1)
    plane_relay(part(g_all), sem1(g_s), sem2(g_r))
    relay(DOWN, d_piece, 2)
    for cp in local_i:
        cp.wait()
    pl.when(at_home)(local_o.wait)
    near_first = ((mate, mate_dev), (far_inner, (r, far_inner)), (far_end, (r, far_end)))
    for i, (q, dev) in enumerate(near_first):
        start(rc(i_piece(zz, c), i_piece(zz, c), w_s.at[IN, i], w_r.at[IN, zz], dev))
    o_piece = lambda core: wo.at[pl.ds(mo(core * ohalf, ohalf), ohalf)]
    for i, (q, dev) in enumerate(near_first):
        start(rc(o_piece(c), o_piece(c), o_s.at[i], o_r.at[0], dev), at_home)
    relay(DOWN, d_piece, 3)
    relay_done(DOWN, d_piece)
    local_g.wait()
    plane_near(part(g_all), sem2(g_r))
    plane_far(part(g_all), sem2(g_r))

    def exchange(t, dw, xr, block_half):
        src = dw.at[:, pl.ds(mo(other * block_half, block_half), block_half)]
        start(rc(src, xr, xs_s.at[t], xs_r.at[t], partner))

    def core_sum(t, dw, xr, block_half):
        mine = pl.ds(mo(c * block_half, block_half), block_half)
        got(xr, xs_r.at[t])

        def body(q, carry):
            xr[q] = (dw[q, mine].astype(F32) + xr[q].astype(F32)).astype(BF)
            return carry

        lax.fori_loop(0, dw.shape[0], body, 0)

    def pair_sum(t, dw, xr, zr, block_half):
        core_sum(t, dw, xr, block_half)
        start(rc(xr.at[far_end], zr.at[2], zs_s.at[t, 0], zs_r.at[t, 2], mate_dev), is_end)
        start(rc(xr.at[far_inner], zr.at[3], zs_s.at[t, 1], zs_r.at[t, 3], mate_dev), is_end)
        start(rc(xr.at[mate], zr.at[0], zs_s.at[t, 2], zs_r.at[t, 0], mate_dev))

    def pass_on(t, xr, zr):
        @pl.when(inner)
        def _():
            for slot, q in ((2, far_end), (3, far_inner)):
                got(zr.at[slot], zs_r.at[t, slot])
                xr[q] = (xr[q].astype(F32) + zr[slot].astype(F32)).astype(BF)
                rc(xr.at[q], zr.at[1], zs_s.at[t, slot - 2], zs_r.at[t, 1], (r, q)).start()

        for slot, q in ((2, far_end), (3, far_inner)):
            cp = rc(xr.at[q], zr.at[1], zs_s.at[t, slot - 2], zs_r.at[t, 1], (r, q))
            sends.append((inner, cp))

    def line_sum(t, xr, zr, fin):
        got(zr.at[0], zs_r.at[t, 0])
        got(zr.at[1], zs_r.at[t, 1])
        total = xr[zz].astype(F32) + zr[0].astype(F32) + zr[1].astype(F32)
        fin[...] = total.astype(BF)

    outs_of = {IN: (gin_o, fi), UP: (gup_o, fu), DOWN: (gdown_o, fd)}

    def area(t):
        o = outs_of[t][0]
        rows = o.shape[2] // 2
        return lambda q, h: o.at[q, c, pl.ds(h * rows, rows)]

    def fin_half(t):
        fin = outs_of[t][1]
        rows = fin.shape[0] // 2
        return lambda h: fin.at[pl.ds(h * rows, rows)]

    def ag1(t):
        return lambda i: ag_s.at[t, i]

    def ag2(t):
        return lambda q, h: ag_r.at[t, q, h]

    local_out = []

    def spread(t):
        o, fin = outs_of[t]
        plane_send(fin_half(t), area(t), ag1(t), ag2(t))
        start(rc(fin, o.at[p, c], agc_s.at[t, 0], agc_r.at[t, p], partner))
        cp = pltpu.make_async_copy(fin, o.at[p, c], agl.at[t])
        cp.start()
        local_out.append((None, cp))

    def spread_relay(t):
        plane_relay(area(t), ag1(t), ag2(t))

    def spread_on(t):
        o = outs_of[t][0]
        plane_near(area(t), ag2(t))
        start(rc(o.at[xn, c], o.at[xn, c], agc_s.at[t, 1], agc_r.at[t, xn], partner))
        start(rc(o.at[yn, c], o.at[yn, c], agc_s.at[t, 2], agc_r.at[t, yn], partner))
        plane_far(area(t), ag2(t))
        start(rc(o.at[dg, c], o.at[dg, c], agc_s.at[t, 3], agc_r.at[t, dg], partner))

    def spread_end(t):
        o = outs_of[t][0]
        for i in range(n):
            q = lax.rem(p + i, n)
            got(o.at[q, other], agc_r.at[t, q])

    for j in range(s_n):
        dwd[j] = dot(act[:, j * hb : (j + 1) * hb], g_all[...], TN).astype(BF)
    exchange(DOWN, dwd, xrd, hhalf)

    bup_r[...] = jnp.zeros_like(bup_r)
    bin_r[...] = jnp.zeros_like(bin_r)

    def grad_up_block(s):
        row = pl.ds(mo(s * length, length), length)
        gs = g_all[row, :]
        for j in range(s_n):
            col = pl.ds(j * hb, hb)
            gu = (dot(gs, wd[j * hb : (j + 1) * hb, :], NT) * der[row, col]).astype(BF)
            gup[row, col] = gu
            bup_r[:, col] += jnp.sum(gu.astype(F32), axis=0, keepdims=True)

    def grad_up_blocks(first, last):
        lax.fori_loop(first, last, lambda s, _: (grad_up_block(s), 0)[1], 0)

    grad_up_blocks(0, 2)
    pair_sum(DOWN, dwd, xrd, zrd, hhalf)
    grad_up_blocks(2, n)
    for j in range(s_n):
        dwu[j] = dot(a2[:, j * rs : (j + 1) * rs], gup[...], TN).astype(BF)
    exchange(UP, dwu, xru, half)

    table = [rot[i] for i in range(3)]

    def turn(t, sign):
        fwd = pltpu.roll(t, 128 - ROT // 2, 1)
        back = pltpu.roll(t, ROT // 2, 1)
        return t * table[0] + (fwd * table[1] + back * table[2]) * sign

    def qkv_block(s):
        row = pl.ds(mo(s * length, length), length)
        left_a = a1[row, :]
        for i in range(3):
            bias = inb[:, pl.ds(mo(i * width + p * span, span), span)]
            v = dot(left_a, wi[:, i * span : (i + 1) * span]) + bias
            for h in range(span // 128):
                cut = v[:, h * 128 : (h + 1) * 128]
                if i < 2:
                    cut = turn(cut, 1.0)
                qkv[row, i * span + h * 128 : i * span + (h + 1) * 128] = cut.astype(BF)

    for i, (q, dev) in enumerate(near_first):
        got(i_piece(q, c), w_r.at[IN, q])
        start(rc(i_piece(q, c), i_piece(q, c), wc_s.at[IN, i], wc_r.at[IN, q], partner))
    pair_sum(UP, dwu, xru, zru, half)
    relay_done(IN, i_piece)
    lax.fori_loop(0, n, lambda s, _: (qkv_block(s), 0)[1], 0)

    pass_on(DOWN, xrd, zrd)
    lane = lax.broadcasted_iota(jnp.int32, (1, 128), 1)
    first = lane < HEAD_DIM
    masks = [first.astype(F32).astype(BF), (1.0 - first.astype(F32)).astype(BF)]
    pairs = span // 128

    def att_forward(idx, carry):
        s = lax.div(idx, pairs)
        pr = lax.rem(idx, pairs)
        row = pl.ds(mo(s * length, length), length)
        q2 = qkv[row, pl.ds(mo(pr * 128, 128), 128)]
        k2 = qkv[row, pl.ds(mo(span + pr * 128, 128), 128)]
        v2 = qkv[row, pl.ds(mo(2 * span + pr * 128, 128), 128)]
        key_i = lax.broadcasted_iota(jnp.int32, (length, length), 0)
        query_i = lax.broadcasted_iota(jnp.int32, (length, length), 1)
        found = []
        for h in range(2):
            st = dot(k2, q2 * masks[h], NT) * scale
            ex = jnp.exp(jnp.where(key_i <= query_i, st, MASKED))
            pr_t = ex / jnp.sum(ex, axis=0, keepdims=True)
            pt[idx * 2 + h] = pr_t
            found.append(dot(pr_t.astype(BF), v2, TN))
        att[row, pl.ds(mo(pr * 128, 128), 128)] = jnp.where(first, found[0], found[1]).astype(BF)
        return carry

    lax.fori_loop(0, n * pairs, att_forward, 0)

    @pl.when(away)
    def _():
        got(o_piece(c), o_r.at[0])

    start(rc(o_piece(c), o_piece(c), oc_s.at[0], oc_r.at[0], partner), away)

    @pl.when(away)
    def _():
        got(o_piece(other), oc_r.at[0])

    def shares(send, pre, ss, rr, k):
        @pl.when(k == 0)
        def _():
            for h, dev in ((0, dev_x), (1, dev_y)):
                rc(send.at[0, pl.ds(h * lh, lh)], pre.at[h], ss.at[h], rr.at[h], dev).start()

    def shares_on(send, recv, pre, ss, rr):
        for k, h, dev in ((2, 1, dev_x), (3, 0, dev_y)):
            got(pre.at[h], rr.at[h])
            row = pl.ds(h * lh, lh)
            send[k, row] = (send[k, row].astype(F32) + pre[h].astype(F32)).astype(BF)
            start(rc(send.at[k], recv.at[k - 2], ss.at[k], rr.at[k], dev))

    def shares_left(send, pre, ss, rr):
        for h, dev in ((0, dev_x), (1, dev_y)):
            rc(send.at[0, pl.ds(h * lh, lh)], pre.at[h], ss.at[h], rr.at[h], dev).wait_send()

    def turn_of(k):
        return jnp.where(k == 0, dg, jnp.where(k == 1, p, jnp.where(k == 2, xn, yn)))

    def out_block(k, carry):
        s = turn_of(k)
        row = pl.ds(mo(s * length, length), length)
        for j in range(width // 256):
            col = slice(j * 256, (j + 1) * 256)
            v = dot(att[row, :], wo[:, col]) + dot(act[row, :], wd[:, col])
            msend[k, :, col] = v.astype(BF)

            @pl.when(k == 1)
            def _():
                mown[:, col] = v

        shares(msend, mpre, m_s, m_r, k)
        return carry

    lax.fori_loop(0, n, out_block, 0)

    dwo[0] = dot(att[...], g_all[...], TN).astype(BF)
    exchange(OUT, dwo, xro, ohalf)

    def grad_att_block(s):
        row = pl.ds(mo(s * length, length), length)
        gatt[row, :] = dot(g_all[row, :], wo[...], NT).astype(BF)

    lax.fori_loop(0, n, lambda s, _: (grad_att_block(s), 0)[1], 0)
    core_sum(OUT, dwo, xro, ohalf)
    to_mate = p == mate
    to_far = lax.div(p, 2) != zp
    start(rc(xro.at[0], zro.at[0], zs_s.at[OUT, 0], zs_r.at[OUT, 0], mate_dev), to_mate)
    start(
        rc(xro.at[0], zro.at[2], zs_s.at[OUT, 1], zs_r.at[OUT, 2], mate_dev),
        jnp.logical_and(to_far, is_end),
    )
    shares_on(msend, mrecv, mpre, m_s, m_r)

    def att_backward(idx, carry):
        s = lax.div(idx, pairs)
        pr = lax.rem(idx, pairs)
        row = pl.ds(mo(s * length, length), length)
        q_col = pl.ds(mo(pr * 128, 128), 128)
        k_col = pl.ds(mo(span + pr * 128, 128), 128)
        v_col = pl.ds(mo(2 * span + pr * 128, 128), 128)
        q2, k2, v2 = qkv[row, q_col], qkv[row, k_col], qkv[row, v_col]
        g2 = gatt[row, q_col]
        dq, dk, dv = [], [], []
        for h in range(2):
            pr_t = pt[idx * 2 + h]
            dp = dot(v2, g2 * masks[h], NT)
            total = jnp.sum(dp * pr_t, axis=0, keepdims=True)
            ds = (pr_t * (dp - total)).astype(BF)
            dv.append(dot(pr_t.astype(BF), g2))
            dk.append(dot(ds, q2))
            dq.append(dot(ds, k2, TN))
        dqv = turn(jnp.where(first, dq[0], dq[1]) * scale, -1.0).astype(BF)
        dkv = turn(jnp.where(first, dk[0], dk[1]) * scale, -1.0).astype(BF)
        dvv = jnp.where(first, dv[0], dv[1]).astype(BF)
        for col, val in ((q_col, dqv), (k_col, dkv), (v_col, dvv)):
            gqkv[row, col] = val
            bin_r[:, col] += jnp.sum(val.astype(F32), axis=0, keepdims=True)
        return carry

    lax.fori_loop(0, n * pairs, att_backward, 0)

    for j in range(s_n):
        dwi[j] = dot(a1[:, j * rs : (j + 1) * rs], gqkv[...], TN).astype(BF)
    exchange(IN, dwi, xri, half)

    vacc[...] = jnp.zeros_like(vacc)

    def in_block(k, carry):
        s = turn_of(k)
        row = pl.ds(mo(s * length, length), length)
        gq = gqkv[row, :]
        gu = gup[row, :]
        mu = mean_r[row, :]
        inv = inv_r[row, :]
        for j in range(s_n):
            col = slice(j * rs, (j + 1) * rs)
            d1 = dot(gq, wi[col, :], NT)
            d2 = dot(gu, wu[col, :], NT)
            xh = (x_all[row, col].astype(F32) - mu) * inv
            vacc[0, :, col] += jnp.sum(d1 * xh, axis=0, keepdims=True)
            vacc[1, :, col] += jnp.sum(d1, axis=0, keepdims=True)
            vacc[2, :, col] += jnp.sum(d2 * xh, axis=0, keepdims=True)
            vacc[3, :, col] += jnp.sum(d2, axis=0, keepdims=True)
            e = d1 * gain1[:, col] + d2 * gain2[:, col]
            esend[k, :, col] = e.astype(BF)

            @pl.when(k == 1)
            def _():
                eown[:, col] = e

        shares(esend, epre, e_s, e_r, k)
        return carry

    lax.fori_loop(0, 2, in_block, 0)
    pair_sum(IN, dwi, xri, zri, half)
    lax.fori_loop(2, n, in_block, 0)

    pass_on(UP, xru, zru)
    line_sum(DOWN, xrd, zrd, fd)
    spread(DOWN)

    slots = vfull.shape[0] // s_n
    vfull[...] = jnp.zeros_like(vfull)
    per = n_in // span
    for i in range(3):
        b = i * n + p
        vfull[lax.div(b, per) * slots + lax.rem(b, per)] = bin_r[:, i * span : (i + 1) * span]
    for q in range(s_n):
        vfull[q * slots + per + p] = bup_r[:, q * hb : (q + 1) * hb]
        col = slice(q * rs, (q + 1) * rs)
        g_own = g_all[pl.ds(mo(p * length, length), length), col].astype(F32)
        vfull[q * slots + per + n] = jnp.sum(g_own, axis=0, keepdims=True)
        for i in range(4):
            vfull[q * slots + per + n + 1 + i] = vacc[i, :, col]
    for i in range(1, s_n):
        q, dev = line(i)
        start(rc(vfull.at[pl.ds(q * slots, slots)], vz.at[zz], v1_s.at[i], v1_r.at[zz], dev))

    shares_on(esend, erecv, epre, e_s, e_r)

    far_and_inner = jnp.logical_and(to_far, inner)
    on = rc(xro.at[0], zro.at[1], zs_s.at[OUT, 2], zs_r.at[OUT, 1], (r, p))

    @pl.when(far_and_inner)
    def _():
        got(zro.at[2], zs_r.at[OUT, 2])
        xro[0] = (xro[0].astype(F32) + zro[2].astype(F32)).astype(BF)
        on.start()

    sends.append((far_and_inner, on))

    got(mrecv.at[0], m_r.at[2])
    got(mrecv.at[1], m_r.at[3])

    def mixed_rows(i, carry):
        step = 32
        row = pl.ds(mo(i * step, step), step)
        xv = x_all[pl.ds(mo(p * length + i * step, step), step), :].astype(F32)
        t = mown[row, :] + mrecv[0, row, :].astype(F32) + mrecv[1, row, :].astype(F32)
        mixed_o[row, :] = (xv + t + out_b + down_b).astype(BF)
        return carry

    lax.fori_loop(0, length // 32, mixed_rows, 0)

    spread_relay(DOWN)
    pass_on(IN, xri, zri)
    line_sum(UP, xru, zru, fu)
    spread(UP)
    spread_on(DOWN)

    @pl.when(at_home)
    def _():
        got(zro.at[0], zs_r.at[OUT, 0])
        got(zro.at[1], zs_r.at[OUT, 1])
        total = xro[0].astype(F32) + zro[0].astype(F32) + zro[1].astype(F32)
        fo[...] = total.astype(BF)

    oq = ohalf // 2
    o_area = lambda q, h: gout_o.at[c, pl.ds(h * oq, oq)]
    plane_send(lambda h: fo.at[pl.ds(h * oq, oq)], o_area, ag1(OUT), ag2(OUT), at_home)
    start(rc(fo, gout_o.at[c], agc_s.at[OUT, 0], agc_r.at[OUT, zz], partner), at_home)
    cp = pltpu.make_async_copy(fo, gout_o.at[c], agl.at[OUT])
    pl.when(at_home)(cp.start)
    local_out.append((at_home, cp))

    total = [vfull[zz * slots + k] for k in range(slots)]
    for i in range(1, s_n):
        q, dev = line(i)
        got(vz.at[q], v1_r.at[q])
        total = [t + vz[q, k] for k, t in enumerate(total)]
    for k in range(slots):
        vu[k] = total[k]
        vr[r, k] = total[k]
    for i in range(1, 2 * n):
        start(rc(vu, vr.at[r], v2_s.at[i], v2_r.at[r], (lax.rem(r + i, 2 * n), zz)))

    line_sum(IN, xri, zri, fi)
    spread(IN)
    spread_relay(UP)

    from_x, from_y = xn == zz, yn == zz

    @pl.when(away)
    def _():
        got(o_area(zz, 0), ag_r.at[OUT, zz, 0])

    start(rc(o_area(zz, 0), o_area(zz, 0), ag_s.at[OUT, 4], ag_r.at[OUT, zz, 0], dev_y), from_x)

    @pl.when(away)
    def _():
        got(o_area(zz, 1), ag_r.at[OUT, zz, 1])

    start(rc(o_area(zz, 1), o_area(zz, 1), ag_s.at[OUT, 5], ag_r.at[OUT, zz, 1], dev_x), from_y)
    start(
        rc(gout_o.at[c], gout_o.at[c], agc_s.at[OUT, 1], agc_r.at[OUT, zz], partner), away
    )
    spread_relay(IN)
    spread_on(UP)

    got(erecv.at[0], e_r.at[2])
    got(erecv.at[1], e_r.at[3])

    def tgrad_rows(i, carry):
        step = 32
        row = pl.ds(mo(i * step, step), step)
        far = pl.ds(mo(p * length + i * step, step), step)
        inv = inv_r[far, :]
        xh = (x_all[far, :].astype(F32) - mean_r[far, :]) * inv
        e = eown[row, :] + erecv[0, row, :].astype(F32) + erecv[1, row, :].astype(F32)
        m0 = jnp.mean(e, axis=1, keepdims=True)
        m1 = jnp.mean(e * xh, axis=1, keepdims=True)
        tgrad_o[row, :] = g_all[far, :].astype(F32) + inv * (e - m0 - xh * m1)
        return carry

    lax.fori_loop(0, length // 32, tgrad_rows, 0)

    for i in range(1, 2 * n):
        q = lax.rem(r + i, 2 * n)
        got(vr.at[q], v2_r.at[q])
    for k in range(slots):
        t = vr[0, k]
        for q in range(1, 2 * n):
            t = t + vr[q, k]
        vec_o[k] = t
    spread_on(IN)
    for t in (DOWN, UP, IN):
        spread_end(t)
    got(gout_o.at[other], agc_r.at[OUT, zz])

    for cond, cp in local_out:
        if cond is None:
            cp.wait()
        else:
            pl.when(cond)(cp.wait)
    shares_left(msend, mpre, m_s, m_r)
    shares_left(esend, epre, e_s, e_r)
    for cond, cp in sends:
        if cond is None:
            cp.wait_send()
        else:
            pl.when(cond)(cp.wait_send)


def fused_call(z, tok, cot, inp, upp, outp, downp, vectors):
    n, s_n, length, width, span, hid = z.n, z.s, z.l, z.d, z.span, z.hid
    rs, hb, rows = z.rs, z.hb, z.rows
    iw = 3 * span
    nv = sum(v.shape[0] for v in vectors)
    slots = 3 * width // s_n // span + n + 5
    V = pltpu.VMEM
    dma = lambda *shape: pltpu.SemaphoreType.DMA(shape)
    share = [
        V((n, length, width), BF), V((2, length, width), BF), V((2, length // 2, width), BF),
        V((length, width), F32),
    ]
    halves = [
        V((s_n, rs // 2, iw), BF), V((s_n, rs // 2, hid), BF), V((s_n, hb // 2, width), BF),
    ]
    scratch = [
        *[V((rows, width), BF)] * 4,
        V((width, iw), BF), V((width, hid), BF), V((span, width), BF), V((hid, width), BF),
        V((rows, iw), BF), V((n * span // HEAD_DIM, length, length), F32),
        V((rows, hid), F32), V((rows, hid), BF), V((rows, span), BF),
        V((rows, span), BF), V((rows, hid), BF), V((rows, iw), BF),
        *share, *share,
        V((s_n, rs, iw), BF), V((s_n, rs, hid), BF), V((s_n, hb, width), BF), V((1, span, width), BF),
        *halves, V((1, span // 2, width), BF),
        *halves, V((3, span // 2, width), BF),
        V((rs // 2, iw), BF), V((rs // 2, hid), BF), V((hb // 2, width), BF), V((span // 2, width), BF),
        V((1, nv), F32), V((s_n, 1, nv), F32), V((1, 3 * width), F32), V((s_n * slots, 1, 256), F32),
        V((s_n, slots, 1, 256), F32), V((slots, 1, 256), F32), V((2 * n, slots, 1, 256), F32),
        V((rows, 1), F32), V((rows, 1), F32), V((4, 1, width), F32), V((1, iw), F32), V((1, hid), F32),
        dma(s_n + 7), dma(s_n), dma(s_n), dma(6), dma(n, 2), dma(6), dma(n, 2),
        dma(3, 2 * s_n), dma(3, s_n), dma(3, 2 * s_n), dma(3, s_n),
        dma(3), dma(1), dma(1), dma(1),
        dma(n), dma(n), dma(n), dma(n), dma(4), dma(4), dma(4, 3), dma(4, 4),
        dma(4, 6), dma(4, n, 2), dma(4, n), dma(4, n), dma(4),
        dma(s_n), dma(s_n), dma(2 * n), dma(2 * n),
    ]
    any_ = pl.BlockSpec(memory_space=pl.ANY)
    vm = pl.BlockSpec(memory_space=pltpu.VMEM)
    outs = [
        jax.ShapeDtypeStruct((length, width), BF),
        jax.ShapeDtypeStruct((length, width), F32),
        jax.ShapeDtypeStruct((n, 2, rs // 2, iw), BF),
        jax.ShapeDtypeStruct((n, 2, rs // 2, hid), BF),
        jax.ShapeDtypeStruct((n, 2, hb // 2, width), BF),
        jax.ShapeDtypeStruct((2, span // 2, width), BF),
        jax.ShapeDtypeStruct((slots, 1, 256), F32),
    ]
    return pl.pallas_call(
        functools.partial(fused, z),
        out_shape=outs,
        in_specs=[any_] * 6 + [vm] * 9,
        out_specs=[vm, vm, any_, any_, any_, any_, vm],
        scratch_shapes=scratch,
        compiler_params=pltpu.CompilerParams(
            collective_id=0, has_side_effects=True, vmem_limit_bytes=VMEM_LIMIT
        ),
        name="block_step",
    )(tok, cot, inp, upp, outp, downp, *vectors, jnp.asarray(rotary_lanes(length)))


def finish(z, *refs):
    mixed, tgrad, g_in, g_up, g_down, g_out, vec = refs[:7]
    mixed_o, tgrad_o, in_o, up_o, down_o, out_o = refs[7:13]
    vec_o = refs[13:21]
    m_v, t_v, bi, bu, bd, bo, fi, fu, fd, fo, m_sem, r_sem, w_sem = refs[21:]
    n, s_n, width, span, hb, rs = z.n, z.s, z.d, z.span, z.hb, z.rs
    half = rs // 2
    jobs = []
    for q in range(n):
        for core in range(2):
            row = slice(core * half, (core + 1) * half)
            jobs.append((g_up.at[q, core], bu.at[q, core], fu.at[q, core], [
                (up_o.at[row, k * hb * n + q * hb : k * hb * n + (q + 1) * hb], slice(k * hb, (k + 1) * hb))
                for k in range(s_n)
            ]))
    for q in range(n):
        for core in range(2):
            start = q * hb + core * (hb // 2)
            jobs.append((g_down.at[q, core], bd.at[q, core], fd.at[q, core], [
                (down_o.at[start : start + hb // 2], slice(None)),
            ]))
    for q in range(n):
        for core in range(2):
            row = slice(core * half, (core + 1) * half)
            jobs.append((g_in.at[q, core], bi.at[q, core], fi.at[q, core], [
                (in_o.at[row, k * width + q * span : k * width + (q + 1) * span], slice(k * span, (k + 1) * span))
                for k in range(3)
            ]))
    for core in range(2):
        start = core * (span // 2)
        jobs.append((g_out.at[core], bo.at[core], fo.at[core], [
            (out_o.at[start : start + span // 2], slice(None)),
        ]))
    through = [
        (pltpu.make_async_copy(a, b, m_sem.at[2 * i]), pltpu.make_async_copy(b, o, m_sem.at[2 * i + 1]))
        for i, (a, b, o) in enumerate(((mixed, m_v, mixed_o), (tgrad, t_v, tgrad_o)))
    ]
    reads = [pltpu.make_async_copy(src, dst, r_sem.at[i]) for i, (src, dst, _, _) in enumerate(jobs)]
    for cp in reads:
        cp.start()
    for cp, _ in through:
        cp.start()
    writes = []
    for (_, low, wide, places), read in zip(jobs, reads):
        read.wait()

        def body(i, carry, low=low, wide=wide):
            row = pl.ds(mo(i * 32, 32), 32)
            wide[row, :] = low[row, :].astype(F32)
            return carry

        lax.fori_loop(0, low.shape[0] // 32, body, 0)
        for place, col in places:
            cp = pltpu.make_async_copy(wide.at[:, col], place, w_sem.at[len(writes)])
            cp.start()
            writes.append(cp)
    for a, b in through:
        a.wait()
        b.start()
    k = 0
    for ref in vec_o:
        blocks = ref.shape[0] // 256
        if ref is vec_o[3]:
            k -= blocks
        for i in range(blocks):
            ref[i * 256 : (i + 1) * 256] = vec[k + i].reshape(256)
        k += blocks
    for cp in writes:
        cp.wait()
    for _, b in through:
        b.wait()


def finish_call(z, pieces):
    n, width, span = z.n, z.d, z.span
    V = pltpu.VMEM
    S = jax.ShapeDtypeStruct
    any_ = pl.BlockSpec(memory_space=pl.ANY)
    vm = pl.BlockSpec(memory_space=pltpu.VMEM)
    rs = z.rs
    outs = [
        S((z.l, width), BF), S((z.l, width), F32), S((rs, 3 * width), F32), S((rs, z.ff), F32),
        S((z.hb * n, width), F32), S((span, width), F32),
        S((3 * width // z.s,), F32), S((z.hb * n,), F32), *[S((rs,), F32)] * 6,
    ]
    shapes = [p.shape for p in pieces[2:6]]
    dma = lambda k: pltpu.SemaphoreType.DMA((k,))
    return pl.pallas_call(
        functools.partial(finish, z),
        out_shape=outs,
        in_specs=[any_] * 6 + [vm],
        out_specs=[any_] * 6 + [vm] * 8,
        scratch_shapes=[
            V((z.l, width), BF), V((z.l, width), F32),
            *[V(s, BF) for s in shapes], *[V(s, F32) for s in shapes],
            dma(4), dma(6 * n + 2), dma(2 * n * (z.s + 4) + 2),
        ],
        compiler_params=pltpu.CompilerParams(vmem_limit_bytes=VMEM_LIMIT),
        name="finish",
    )(*pieces)


def make_fused_body(z):
    def body(
        tokens, in_proj, in_bias, out_proj, out_bias, up_proj, up_bias, down_proj, down_bias,
        first_gain, first_shift, second_gain, second_shift, cotangent,
    ):
        vectors = (in_bias, up_bias, out_bias, down_bias, first_gain, first_shift, second_gain, second_shift)
        pieces = fused_call(z, tokens, cotangent, in_proj, up_proj, out_proj, down_proj, vectors)
        mixed, tgrad, g_in, g_up, g_down, g_out, b_in, b_up, b_out, b_down, *rest = finish_call(
            z, pieces
        )
        return (mixed, tgrad, g_in, b_in, g_out, b_out, g_up, b_up, g_down, b_down, *rest)

    return body


def solution(mesh):
    rows = P(("rep", "shard"), None)
    mat = P("shard", None)
    vec = P("shard")
    in_specs = (rows, mat, vec, mat, vec, mat, vec, mat, vec, vec, vec, vec, vec, rows)
    out_specs = (rows, rows, mat, vec, mat, vec, mat, vec, mat, vec, vec, vec, vec, vec)
    shape = dict(mesh.shape)

    def step(*args):
        tokens, up_proj = args[0], args[5]
        devices = shape["rep"] * shape["shard"]
        z = Sizes(shape, tokens.shape[0] // devices, tokens.shape[1], up_proj.shape[1])
        body = make_fused_body(z) if z.fits() else make_body(shape["shard"])
        return jax.shard_map(
            body, mesh=mesh, in_specs=in_specs, out_specs=out_specs, check_vma=False
        )(*args)

    return step
```

time: 231 us -> 180 us (0.78)
  the two profiles are of different devices: /device:TPU:0 before, /device:TPU:9 now
where the time goes in v3:
time: 180 us; the launch traced here: 179 us
  Pallas kernels  178 us (99%)
    pallas_call x1, Pallas kernels, fused_call(): pl.pallas_call(functools.partial(fused, z), out_shape=outs, in_specs=[any...  169 us
    pallas_call x1, Pallas kernels, finish_call(): pl.pallas_call(functools.partial(finish, z), out_shape=outs, in_specs=[an...  9.56 us

profile of v3, /device:TPU:9, one launch (start us, length us, event | category | flops | bytes accessed | tf_op | source)
XLA Modules:
  0.0 179.3 jit_solution(3739402476861374253)
XLA Ops:
  0.7 168.9 %block_step.1 = (bf16[256,1024]{1,0:T(8,128)(2,1)}, f32[256,1024]{1,0:T(8,128)}, bf16[4,2,128,768]{3,2,1,0:T(8,128)(2,1)}, bf16[4,2,128,1024]{3,2,1,0:T(8,128)(2...) custom-call(bf16[256,1024]{1,0:T(8,128)(2,1)} %refs_0_.1, ...), custom_call_target="tpu_custom_call" | custom-call | tf_op jit(solution)/shard_map/block_step/pallas_call | solution.py:985
  169.6 9.6 %finish.1 = (bf16[256,1024]{1,0:T(8,128)(2,1)}, f32[256,1024]{1,0:T(8,128)}, f32[256,3072]{1,0:T(8,128)}, f32[256,4096]{1,0:T(8,128)}, f32[1024,1024]{1,0:T(8,12...) custom-call(bf16[256,1024]{1,0:T(8,128)(2,1)} %get-tuple-element.35., ...), custom_call_target="tpu_custom_call" | custom-call | tf_op jit(solution)/shard_map/finish/pallas_call | solution.py:1085

commit v4 on v3

--- a/solution.py
+++ b/solution.py
@@ -305,22 +305,25 @@
     ]
     local_i = [
         pltpu.make_async_copy(
-            inp.at[:, pl.ds(mo(i * width + p * span, span), span)],
-            wi.at[own_rows, pl.ds(i * span, span)],
-            loc.at[s_n + i],
+            inp.at[:, pl.ds(mo(i * width + (p + n * k) * 128, 128), 128)],
+            wi.at[own_rows, pl.ds(i * span + k * 128, 128)],
+            loc.at[s_n + 2 * i + k],
         )
         for i in range(3)
+        for k in range(2)
     ]
-    at_loc = s_n + 3
+    at_loc = s_n + 6
     local_d = pltpu.make_async_copy(
         downp.at[pl.ds(mo(p * hb, hb), hb)], wd.at[own_hb], loc.at[at_loc]
     )
     local_x = pltpu.make_async_copy(tok, seq(x_all, p), loc.at[at_loc + 1])
     local_g = pltpu.make_async_copy(cot, seq(g_all, p), loc.at[at_loc + 2])
-    local_o = pltpu.make_async_copy(outp, wo, loc.at[at_loc + 3])
-    at_home = zz == p
+    local_o = pltpu.make_async_copy(
+        outp.at[pl.ds(mo(px * 128, 128), 128)], wo.at[pl.ds(mo(zp * 128, 128), 128)], loc.at[at_loc + 3]
+    )
+    at_home = zo == py
     away = jnp.logical_not(at_home)
-    for cp in local_u + [local_x, local_g, local_d] + local_i:
+    for cp in local_i + [local_x] + local_u + [local_g, local_d]:
         cp.start()
     pl.when(at_home)(local_o.start)
     off = 0
@@ -381,40 +384,50 @@
         start(rc(vec, va.at[zz], v_s.at[i], v_r.at[zz], dev))
     plane_send(rows_of(tok), part(x_all), sem1(x_s), sem2(x_r))
 
-    half, hhalf, ohalf = rs // 2, hb // 2, span // 2
-
-    def piece(ref, block):
-        return lambda q, core: ref.at[pl.ds(mo(q * block + core * (block // 2), block // 2), block // 2)]
-
-    u_piece, d_piece, i_piece = piece(wu, rs), piece(wd, hb), piece(wi, rs)
+    half, hhalf, ohalf = rs // 2, hb // 2, span // 4
+    cuts = {IN: 2, UP: 1, DOWN: 1}
+
+    def piece(t, ref, block):
+        rows = block // 2 // cuts[t]
+        return lambda q, core, h: ref.at[pl.ds(mo(q * block + core * (block // 2) + h * rows, rows), rows)]
+
+    u_piece, d_piece, i_piece = piece(UP, wu, rs), piece(DOWN, wd, hb), piece(IN, wi, rs)
 
     def own_sends(t, get):
-        start(rc(get(zz, c), get(zz, c), w_s.at[t, 0], w_r.at[t, zz], left), has_left)
-        start(rc(get(zz, c), get(zz, c), w_s.at[t, 1], w_r.at[t, zz], right), has_right)
-
-    def relay(t, get, d):
-        def take(q, has, onward, more, slot):
+        for h in range(cuts[t]):
+            mine = get(zz, c, h)
+            start(rc(mine, mine, w_s.at[t, h, 0], w_r.at[t, h, zz], left), has_left)
+            start(rc(mine, mine, w_s.at[t, h, 1], w_r.at[t, h, zz], right), has_right)
+
+    def relay(t, get, d, who):
+        def take(h, q, has, onward, more, slot):
+            ref = get(q, c, h)
+
             @pl.when(has)
             def _():
-                got(get(q, c), w_r.at[t, q])
+                got(ref, w_r.at[t, h, q])
 
             start(
-                rc(get(q, c), get(q, c), w_s.at[t, slot], w_r.at[t, q], onward),
+                rc(ref, ref, w_s.at[t, h, slot], w_r.at[t, h, q], onward),
                 jnp.logical_and(has, more),
             )
-            start(rc(get(q, c), get(q, c), wc_s.at[t, slot], wc_r.at[t, q], partner), has)
-
-        take(zz - d, zz - d >= 0, right, has_right, 2 * d)
-        take(zz + d, zz + d <= s_n - 1, left, has_left, 2 * d + 1)
+            start(rc(ref, ref, wc_s.at[t, h, slot], wc_r.at[t, h, q], partner), has)
+
+        for h in range(cuts[t]):
+            from_left = jnp.logical_and(who, zz - d >= 0)
+            from_right = jnp.logical_and(who, zz + d <= s_n - 1)
+            take(h, zz - d, from_left, right, has_right, 2 * d)
+            take(h, zz + d, from_right, left, has_left, 2 * d + 1)
 
     def relay_done(t, get):
-        for i in range(1, s_n):
-            q, _ = line(i)
-            got(get(q, other), wc_r.at[t, q])
-
-    for cp in local_u:
+        for h in range(cuts[t]):
+            for i in range(1, s_n):
+                q, _ = line(i)
+                got(get(q, other, h), wc_r.at[t, h, q])
+
+    for cp in local_i:
         cp.wait()
-    own_sends(UP, u_piece)
+    own_sends(IN, i_piece)
 
     for i in range(1, s_n):
         q, dev = line(i)
@@ -451,162 +464,6 @@
 
         lax.fori_loop(0, length // step, body, 0)
 
-    local_x.wait()
-    norm(p)
-    relay(UP, u_piece, 1)
-    plane_relay(part(x_all), sem1(x_s), sem2(x_r))
-    plane_send(rows_of(cot), part(g_all), sem1(g_s), sem2(g_r))
-    relay(UP, u_piece, 2)
-    local_d.wait()
-    own_sends(DOWN, d_piece)
-    plane_near(part(x_all), sem2(x_r))
-    norm(xn)
-    norm(yn)
-    plane_far(part(x_all), sem2(x_r))
-    norm(dg)
-    relay(UP, u_piece, 3)
-    relay_done(UP, u_piece)
-
-    def up_block(s):
-        row = pl.ds(mo(s * length, length), length)
-        left_a = a2[row, :]
-        for j in range(s_n):
-            col = pl.ds(j * hb, hb)
-            bias = va[j, :, pl.ds(mo(at_up + p * hb, hb), hb)]
-            u = dot(left_a, wu[:, j * hb : (j + 1) * hb]) + bias
-            phi = 0.5 * (1.0 + lax.erf(u * 0.7071067811865476))
-            act[row, col] = (u * phi).astype(BF)
-            der[row, col] = phi + u * (0.3989422804014327 * jnp.exp(-0.5 * u * u))
-
-    lax.fori_loop(0, n, lambda s, _: (up_block(s), 0)[1], 0)
-
-    relay(DOWN, d_piece, 1)
-    plane_relay(part(g_all), sem1(g_s), sem2(g_r))
-    relay(DOWN, d_piece, 2)
-    for cp in local_i:
-        cp.wait()
-    pl.when(at_home)(local_o.wait)
-    near_first = ((mate, mate_dev), (far_inner, (r, far_inner)), (far_end, (r, far_end)))
-    for i, (q, dev) in enumerate(near_first):
-        start(rc(i_piece(zz, c), i_piece(zz, c), w_s.at[IN, i], w_r.at[IN, zz], dev))
-    o_piece = lambda core: wo.at[pl.ds(mo(core * ohalf, ohalf), ohalf)]
-    for i, (q, dev) in enumerate(near_first):
-        start(rc(o_piece(c), o_piece(c), o_s.at[i], o_r.at[0], dev), at_home)
-    relay(DOWN, d_piece, 3)
-    relay_done(DOWN, d_piece)
-    local_g.wait()
-    plane_near(part(g_all), sem2(g_r))
-    plane_far(part(g_all), sem2(g_r))
-
-    def exchange(t, dw, xr, block_half):
-        src = dw.at[:, pl.ds(mo(other * block_half, block_half), block_half)]
-        start(rc(src, xr, xs_s.at[t], xs_r.at[t], partner))
-
-    def core_sum(t, dw, xr, block_half):
-        mine = pl.ds(mo(c * block_half, block_half), block_half)
-        got(xr, xs_r.at[t])
-
-        def body(q, carry):
-            xr[q] = (dw[q, mine].astype(F32) + xr[q].astype(F32)).astype(BF)
-            return carry
-
-        lax.fori_loop(0, dw.shape[0], body, 0)
-
-    def pair_sum(t, dw, xr, zr, block_half):
-        core_sum(t, dw, xr, block_half)
-        start(rc(xr.at[far_end], zr.at[2], zs_s.at[t, 0], zs_r.at[t, 2], mate_dev), is_end)
-        start(rc(xr.at[far_inner], zr.at[3], zs_s.at[t, 1], zs_r.at[t, 3], mate_dev), is_end)
-        start(rc(xr.at[mate], zr.at[0], zs_s.at[t, 2], zs_r.at[t, 0], mate_dev))
-
-    def pass_on(t, xr, zr):
-        @pl.when(inner)
-        def _():
-            for slot, q in ((2, far_end), (3, far_inner)):
-                got(zr.at[slot], zs_r.at[t, slot])
-                xr[q] = (xr[q].astype(F32) + zr[slot].astype(F32)).astype(BF)
-                rc(xr.at[q], zr.at[1], zs_s.at[t, slot - 2], zs_r.at[t, 1], (r, q)).start()
-
-        for slot, q in ((2, far_end), (3, far_inner)):
-            cp = rc(xr.at[q], zr.at[1], zs_s.at[t, slot - 2], zs_r.at[t, 1], (r, q))
-            sends.append((inner, cp))
-
-    def line_sum(t, xr, zr, fin):
-        got(zr.at[0], zs_r.at[t, 0])
-        got(zr.at[1], zs_r.at[t, 1])
-        total = xr[zz].astype(F32) + zr[0].astype(F32) + zr[1].astype(F32)
-        fin[...] = total.astype(BF)
-
-    outs_of = {IN: (gin_o, fi), UP: (gup_o, fu), DOWN: (gdown_o, fd)}
-
-    def area(t):
-        o = outs_of[t][0]
-        rows = o.shape[2] // 2
-        return lambda q, h: o.at[q, c, pl.ds(h * rows, rows)]
-
-    def fin_half(t):
-        fin = outs_of[t][1]
-        rows = fin.shape[0] // 2
-        return lambda h: fin.at[pl.ds(h * rows, rows)]
-
-    def ag1(t):
-        return lambda i: ag_s.at[t, i]
-
-    def ag2(t):
-        return lambda q, h: ag_r.at[t, q, h]
-
-    local_out = []
-
-    def spread(t):
-        o, fin = outs_of[t]
-        plane_send(fin_half(t), area(t), ag1(t), ag2(t))
-        start(rc(fin, o.at[p, c], agc_s.at[t, 0], agc_r.at[t, p], partner))
-        cp = pltpu.make_async_copy(fin, o.at[p, c], agl.at[t])
-        cp.start()
-        local_out.append((None, cp))
-
-    def spread_relay(t):
-        plane_relay(area(t), ag1(t), ag2(t))
-
-    def spread_on(t):
-        o = outs_of[t][0]
-        plane_near(area(t), ag2(t))
-        start(rc(o.at[xn, c], o.at[xn, c], agc_s.at[t, 1], agc_r.at[t, xn], partner))
-        start(rc(o.at[yn, c], o.at[yn, c], agc_s.at[t, 2], agc_r.at[t, yn], partner))
-        plane_far(area(t), ag2(t))
-        start(rc(o.at[dg, c], o.at[dg, c], agc_s.at[t, 3], agc_r.at[t, dg], partner))
-
-    def spread_end(t):
-        o = outs_of[t][0]
-        for i in range(n):
-            q = lax.rem(p + i, n)
-            got(o.at[q, other], agc_r.at[t, q])
-
-    for j in range(s_n):
-        dwd[j] = dot(act[:, j * hb : (j + 1) * hb], g_all[...], TN).astype(BF)
-    exchange(DOWN, dwd, xrd, hhalf)
-
-    bup_r[...] = jnp.zeros_like(bup_r)
-    bin_r[...] = jnp.zeros_like(bin_r)
-
-    def grad_up_block(s):
-        row = pl.ds(mo(s * length, length), length)
-        gs = g_all[row, :]
-        for j in range(s_n):
-            col = pl.ds(j * hb, hb)
-            gu = (dot(gs, wd[j * hb : (j + 1) * hb, :], NT) * der[row, col]).astype(BF)
-            gup[row, col] = gu
-            bup_r[:, col] += jnp.sum(gu.astype(F32), axis=0, keepdims=True)
-
-    def grad_up_blocks(first, last):
-        lax.fori_loop(first, last, lambda s, _: (grad_up_block(s), 0)[1], 0)
-
-    grad_up_blocks(0, 2)
-    pair_sum(DOWN, dwd, xrd, zrd, hhalf)
-    grad_up_blocks(2, n)
-    for j in range(s_n):
-        dwu[j] = dot(a2[:, j * rs : (j + 1) * rs], gup[...], TN).astype(BF)
-    exchange(UP, dwu, xru, half)
-
     table = [rot[i] for i in range(3)]
 
     def turn(t, sign):
@@ -614,26 +471,54 @@
         back = pltpu.roll(t, ROT // 2, 1)
         return t * table[0] + (fwd * table[1] + back * table[2]) * sign
 
-    def qkv_block(s):
-        row = pl.ds(mo(s * length, length), length)
+    def turn_of(k):
+        return jnp.where(k == 0, p, jnp.where(k == 1, xn, jnp.where(k == 2, yn, dg)))
+
+    def qkv_block(k, carry):
+        row = pl.ds(mo(turn_of(k) * length, length), length)
         left_a = a1[row, :]
         for i in range(3):
-            bias = inb[:, pl.ds(mo(i * width + p * span, span), span)]
-            v = dot(left_a, wi[:, i * span : (i + 1) * span]) + bias
-            for h in range(span // 128):
-                cut = v[:, h * 128 : (h + 1) * 128]
+            v = dot(left_a, wi[:, i * span : (i + 1) * span])
+            for h in range(2):
+                bias = inb[:, pl.ds(mo(i * width + (p + n * h) * 128, 128), 128)]
+                cut = v[:, h * 128 : (h + 1) * 128] + bias
                 if i < 2:
                     cut = turn(cut, 1.0)
                 qkv[row, i * span + h * 128 : i * span + (h + 1) * 128] = cut.astype(BF)
-
-    for i, (q, dev) in enumerate(near_first):
-        got(i_piece(q, c), w_r.at[IN, q])
-        start(rc(i_piece(q, c), i_piece(q, c), wc_s.at[IN, i], wc_r.at[IN, q], partner))
-    pair_sum(UP, dwu, xru, zru, half)
+        return carry
+
+    relay(IN, i_piece, 1, inner)
+    local_x.wait()
+    norm(p)
+    relay(IN, i_piece, 2, inner)
+    for cp in local_u:
+        cp.wait()
+    own_sends(UP, u_piece)
+    plane_relay(part(x_all), sem1(x_s), sem2(x_r))
+    plane_send(rows_of(cot), part(g_all), sem1(g_s), sem2(g_r))
+    plane_near(part(x_all), sem2(x_r))
+    norm(xn)
+    norm(yn)
+    relay(UP, u_piece, 1, inner)
+    for d in range(1, s_n):
+        relay(IN, i_piece, d, is_end)
     relay_done(IN, i_piece)
-    lax.fori_loop(0, n, lambda s, _: (qkv_block(s), 0)[1], 0)
-
-    pass_on(DOWN, xrd, zrd)
+    lax.fori_loop(0, 3, qkv_block, 0)
+    relay(UP, u_piece, 2, inner)
+    local_d.wait()
+    own_sends(DOWN, d_piece)
+    def o_piece(block, core):
+        return wo.at[pl.ds(mo(block * 128 + core * ohalf, ohalf), ohalf)]
+
+    pl.when(at_home)(local_o.wait)
+    near_first = (mate_dev, (r, far_inner), (r, far_end))
+    for i, dev in enumerate(near_first):
+        start(rc(o_piece(zp, c), o_piece(zp, c), o_s.at[i], o_r.at[zp], dev), at_home)
+    plane_far(part(x_all), sem2(x_r))
+    norm(dg)
+    lax.fori_loop(3, n, qkv_block, 0)
+    plane_relay(part(g_all), sem1(g_s), sem2(g_r))
+
     lane = lax.broadcasted_iota(jnp.int32, (1, 128), 1)
     first = lane < HEAD_DIM
     masks = [first.astype(F32).astype(BF), (1.0 - first.astype(F32)).astype(BF)]
@@ -658,72 +543,160 @@
         att[row, pl.ds(mo(pr * 128, 128), 128)] = jnp.where(first, found[0], found[1]).astype(BF)
         return carry
 
-    lax.fori_loop(0, n * pairs, att_forward, 0)
-
-    @pl.when(away)
-    def _():
-        got(o_piece(c), o_r.at[0])
-
-    start(rc(o_piece(c), o_piece(c), oc_s.at[0], oc_r.at[0], partner), away)
-
-    @pl.when(away)
-    def _():
-        got(o_piece(other), oc_r.at[0])
-
-    def shares(send, pre, ss, rr, k):
-        @pl.when(k == 0)
+    lax.fori_loop(0, n * pairs // 2, att_forward, 0)
+    relay(DOWN, d_piece, 1, inner)
+    lax.fori_loop(n * pairs // 2, n * pairs, att_forward, 0)
+    for d in range(1, s_n):
+        relay(UP, u_piece, d, is_end)
+    relay_done(UP, u_piece)
+
+    def up_block(s, carry):
+        row = pl.ds(mo(s * length, length), length)
+        left_a = a2[row, :]
+        for j in range(s_n):
+            col = pl.ds(j * hb, hb)
+            bias = va[j, :, pl.ds(mo(at_up + p * hb, hb), hb)]
+            u = dot(left_a, wu[:, j * hb : (j + 1) * hb]) + bias
+            phi = 0.5 * (1.0 + lax.erf(u * 0.7071067811865476))
+            act[row, col] = (u * phi).astype(BF)
+            der[row, col] = phi + u * (0.3989422804014327 * jnp.exp(-0.5 * u * u))
+        return carry
+
+    lax.fori_loop(0, n, up_block, 0)
+    relay(DOWN, d_piece, 2, inner)
+
+    def exchange(t, dw, xr, block_half):
+        src = dw.at[:, pl.ds(mo(other * block_half, block_half), block_half)]
+        start(rc(src, xr, xs_s.at[t], xs_r.at[t], partner))
+
+    def core_sum(t, dw, xr, block_half):
+        mine = pl.ds(mo(c * block_half, block_half), block_half)
+        got(xr, xs_r.at[t])
+
+        def body(q, carry):
+            xr[q] = (dw[q, mine].astype(F32) + xr[q].astype(F32)).astype(BF)
+            return carry
+
+        lax.fori_loop(0, dw.shape[0], body, 0)
+
+    def pair_sum(t, dw, xr, zr, block_half):
+        core_sum(t, dw, xr, block_half)
+        start(rc(xr.at[far_end], zr.at[2], zs_s.at[t, 0], zs_r.at[t, 2], mate_dev), is_end)
+        start(rc(xr.at[far_inner], zr.at[3], zs_s.at[t, 1], zs_r.at[t, 3], mate_dev), is_end)
+        start(rc(xr.at[mate], zr.at[0], zs_s.at[t, 2], zs_r.at[t, 0], mate_dev))
+
+    def pass_on(t, xr, zr):
+        @pl.when(inner)
         def _():
-            for h, dev in ((0, dev_x), (1, dev_y)):
-                rc(send.at[0, pl.ds(h * lh, lh)], pre.at[h], ss.at[h], rr.at[h], dev).start()
-
-    def shares_on(send, recv, pre, ss, rr):
-        for k, h, dev in ((2, 1, dev_x), (3, 0, dev_y)):
-            got(pre.at[h], rr.at[h])
-            row = pl.ds(h * lh, lh)
-            send[k, row] = (send[k, row].astype(F32) + pre[h].astype(F32)).astype(BF)
-            start(rc(send.at[k], recv.at[k - 2], ss.at[k], rr.at[k], dev))
-
-    def shares_left(send, pre, ss, rr):
-        for h, dev in ((0, dev_x), (1, dev_y)):
-            rc(send.at[0, pl.ds(h * lh, lh)], pre.at[h], ss.at[h], rr.at[h], dev).wait_send()
-
-    def turn_of(k):
-        return jnp.where(k == 0, dg, jnp.where(k == 1, p, jnp.where(k == 2, xn, yn)))
-
-    def out_block(k, carry):
-        s = turn_of(k)
-        row = pl.ds(mo(s * length, length), length)
-        for j in range(width // 256):
-            col = slice(j * 256, (j + 1) * 256)
-            v = dot(att[row, :], wo[:, col]) + dot(act[row, :], wd[:, col])
-            msend[k, :, col] = v.astype(BF)
-
-            @pl.when(k == 1)
-            def _():
-                mown[:, col] = v
-
-        shares(msend, mpre, m_s, m_r, k)
-        return carry
-
-    lax.fori_loop(0, n, out_block, 0)
-
-    dwo[0] = dot(att[...], g_all[...], TN).astype(BF)
+            for slot, q in ((2, far_end), (3, far_inner)):
+                got(zr.at[slot], zs_r.at[t, slot])
+                xr[q] = (xr[q].astype(F32) + zr[slot].astype(F32)).astype(BF)
+                rc(xr.at[q], zr.at[1], zs_s.at[t, slot - 2], zs_r.at[t, 1], (r, q)).start()
+
+        for slot, q in ((2, far_end), (3, far_inner)):
+            cp = rc(xr.at[q], zr.at[1], zs_s.at[t, slot - 2], zs_r.at[t, 1], (r, q))
+            sends.append((inner, cp))
+
+    def line_sum(t, xr, zr, fin):
+        got(zr.at[0], zs_r.at[t, 0])
+        got(zr.at[1], zs_r.at[t, 1])
+        total = xr[zz].astype(F32) + zr[0].astype(F32) + zr[1].astype(F32)
+        fin[...] = total.astype(BF)
+
+    outs_of = {IN: (gin_o, fi), UP: (gup_o, fu), DOWN: (gdown_o, fd)}
+
+    def area(t):
+        o = outs_of[t][0]
+        rows = o.shape[2] // 2
+        return lambda q, h: o.at[q, c, pl.ds(h * rows, rows)]
+
+    def fin_half(t):
+        fin = outs_of[t][1]
+        rows = fin.shape[0] // 2
+        return lambda h: fin.at[pl.ds(h * rows, rows)]
+
+    def ag1(t):
+        return lambda i: ag_s.at[t, i]
+
+    def ag2(t):
+        return lambda q, h: ag_r.at[t, q, h]
+
+    local_out = []
+
+    def spread(t):
+        o, fin = outs_of[t]
+        plane_send(fin_half(t), area(t), ag1(t), ag2(t))
+        start(rc(fin, o.at[p, c], agc_s.at[t, 0], agc_r.at[t, p], partner))
+        cp = pltpu.make_async_copy(fin, o.at[p, c], agl.at[t])
+        cp.start()
+        local_out.append((None, cp))
+
+    def spread_relay(t):
+        plane_relay(area(t), ag1(t), ag2(t))
+
+    def spread_near(t):
+        o = outs_of[t][0]
+        plane_near(area(t), ag2(t))
+        start(rc(o.at[xn, c], o.at[xn, c], agc_s.at[t, 1], agc_r.at[t, xn], partner))
+        start(rc(o.at[yn, c], o.at[yn, c], agc_s.at[t, 2], agc_r.at[t, yn], partner))
+
+    def spread_far(t):
+        o = outs_of[t][0]
+        plane_far(area(t), ag2(t))
+        start(rc(o.at[dg, c], o.at[dg, c], agc_s.at[t, 3], agc_r.at[t, dg], partner))
+
+    def spread_end(t):
+        o = outs_of[t][0]
+        for i in range(n):
+            q = lax.rem(p + i, n)
+            got(o.at[q, other], agc_r.at[t, q])
+
+    local_g.wait()
+    plane_near(part(g_all), sem2(g_r))
+    plane_far(part(g_all), sem2(g_r))
+
+    for j in range(s_n):
+        dwd[j] = dot(act[:, j * hb : (j + 1) * hb], g_all[...], TN).astype(BF)
+    exchange(DOWN, dwd, xrd, hhalf)
+    dwo_all = dot(att[...], g_all[...], TN).astype(BF)
+    for i in range(2):
+        dwo[i] = dwo_all[i * 128 : (i + 1) * 128]
     exchange(OUT, dwo, xro, ohalf)
-
-    def grad_att_block(s):
+    pair_sum(DOWN, dwd, xrd, zrd, hhalf)
+    core_sum(OUT, dwo, xro, ohalf)
+    near_b, far_b = zp, 1 - zp
+    start(rc(xro.at[near_b], zro.at[0], zs_s.at[OUT, 0], zs_r.at[OUT, 0], mate_dev), away)
+    start(rc(xro.at[far_b], zro.at[2], zs_s.at[OUT, 1], zs_r.at[OUT, 2], mate_dev), is_end)
+
+    def o_take(block, cond):
+        @pl.when(cond)
+        def _():
+            got(o_piece(block, c), o_r.at[block])
+
+        start(
+            rc(o_piece(block, c), o_piece(block, c), oc_s.at[block], oc_r.at[block], partner), cond
+        )
+
+    def o_done(block, cond):
+        @pl.when(cond)
+        def _():
+            got(o_piece(block, other), oc_r.at[block])
+
+    always = zz >= 0
+    o_take(near_b, away)
+    o_take(far_b, always)
+    o_done(near_b, away)
+    o_done(far_b, always)
+
+    bup_r[...] = jnp.zeros_like(bup_r)
+    bin_r[...] = jnp.zeros_like(bin_r)
+
+    def grad_att_block(s, carry):
         row = pl.ds(mo(s * length, length), length)
         gatt[row, :] = dot(g_all[row, :], wo[...], NT).astype(BF)
-
-    lax.fori_loop(0, n, lambda s, _: (grad_att_block(s), 0)[1], 0)
-    core_sum(OUT, dwo, xro, ohalf)
-    to_mate = p == mate
-    to_far = lax.div(p, 2) != zp
-    start(rc(xro.at[0], zro.at[0], zs_s.at[OUT, 0], zs_r.at[OUT, 0], mate_dev), to_mate)
-    start(
-        rc(xro.at[0], zro.at[2], zs_s.at[OUT, 1], zs_r.at[OUT, 2], mate_dev),
-        jnp.logical_and(to_far, is_end),
-    )
-    shares_on(msend, mrecv, mpre, m_s, m_r)
+        return carry
+
+    lax.fori_loop(0, n, grad_att_block, 0)
 
     def att_backward(idx, carry):
         s = lax.div(idx, pairs)
@@ -756,12 +729,66 @@
     for j in range(s_n):
         dwi[j] = dot(a1[:, j * rs : (j + 1) * rs], gqkv[...], TN).astype(BF)
     exchange(IN, dwi, xri, half)
+    for d in range(1, s_n):
+        relay(DOWN, d_piece, d, is_end)
+    relay_done(DOWN, d_piece)
+
+    def shares(send, pre, ss, rr, k):
+        @pl.when(k == 0)
+        def _():
+            for h, dev in ((0, dev_x), (1, dev_y)):
+                rc(send.at[0, pl.ds(h * lh, lh)], pre.at[h], ss.at[h], rr.at[h], dev).start()
+
+    def shares_on(send, recv, pre, ss, rr):
+        for k, h, dev in ((1, 1, dev_x), (2, 0, dev_y)):
+            got(pre.at[h], rr.at[h])
+            row = pl.ds(h * lh, lh)
+            send[k, row] = (send[k, row].astype(F32) + pre[h].astype(F32)).astype(BF)
+            start(rc(send.at[k], recv.at[k - 1], ss.at[k + 1], rr.at[k + 1], dev))
+
+    def shares_left(send, pre, ss, rr):
+        for h, dev in ((0, dev_x), (1, dev_y)):
+            rc(send.at[0, pl.ds(h * lh, lh)], pre.at[h], ss.at[h], rr.at[h], dev).wait_send()
+
+    def share_of(k):
+        return jnp.where(k == 0, dg, jnp.where(k == 1, xn, jnp.where(k == 2, yn, p)))
+
+    def out_block(k, carry):
+        row = pl.ds(mo(share_of(k) * length, length), length)
+        for j in range(width // 256):
+            col = slice(j * 256, (j + 1) * 256)
+            v = dot(att[row, :], wo[:, col]) + dot(act[row, :], wd[:, col])
+            msend[k, :, col] = v.astype(BF)
+            mown[:, col] = v
+        shares(msend, mpre, m_s, m_r, k)
+        return carry
+
+    lax.fori_loop(0, 2, out_block, 0)
+    pair_sum(IN, dwi, xri, zri, half)
+    lax.fori_loop(2, n, out_block, 0)
+    pass_on(DOWN, xrd, zrd)
+
+    def grad_up_block(s, carry):
+        row = pl.ds(mo(s * length, length), length)
+        gs = g_all[row, :]
+        for j in range(s_n):
+            col = pl.ds(j * hb, hb)
+            gu = (dot(gs, wd[j * hb : (j + 1) * hb, :], NT) * der[row, col]).astype(BF)
+            gup[row, col] = gu
+            bup_r[:, col] += jnp.sum(gu.astype(F32), axis=0, keepdims=True)
+        return carry
+
+    lax.fori_loop(0, 2, grad_up_block, 0)
+    shares_on(msend, mrecv, mpre, m_s, m_r)
+    lax.fori_loop(2, n, grad_up_block, 0)
+    for j in range(s_n):
+        dwu[j] = dot(a2[:, j * rs : (j + 1) * rs], gup[...], TN).astype(BF)
+    exchange(UP, dwu, xru, half)
 
     vacc[...] = jnp.zeros_like(vacc)
 
     def in_block(k, carry):
-        s = turn_of(k)
-        row = pl.ds(mo(s * length, length), length)
+        row = pl.ds(mo(share_of(k) * length, length), length)
         gq = gqkv[row, :]
         gu = gup[row, :]
         mu = mean_r[row, :]
@@ -777,51 +804,71 @@
             vacc[3, :, col] += jnp.sum(d2, axis=0, keepdims=True)
             e = d1 * gain1[:, col] + d2 * gain2[:, col]
             esend[k, :, col] = e.astype(BF)
-
-            @pl.when(k == 1)
-            def _():
-                eown[:, col] = e
-
+            eown[:, col] = e
         shares(esend, epre, e_s, e_r, k)
         return carry
 
-    lax.fori_loop(0, 2, in_block, 0)
-    pair_sum(IN, dwi, xri, zri, half)
-    lax.fori_loop(2, n, in_block, 0)
-
-    pass_on(UP, xru, zru)
+    lax.fori_loop(0, 1, in_block, 0)
+    pair_sum(UP, dwu, xru, zru, half)
+    lax.fori_loop(1, n, in_block, 0)
+
+    on = rc(xro.at[far_b], zro.at[1], zs_s.at[OUT, 2], zs_r.at[OUT, 1], (r, 2 * (1 - zp) + py))
+
+    @pl.when(inner)
+    def _():
+        got(zro.at[2], zs_r.at[OUT, 2])
+        xro[far_b] = (xro[far_b].astype(F32) + zro[2].astype(F32)).astype(BF)
+        on.start()
+
+    sends.append((inner, on))
     line_sum(DOWN, xrd, zrd, fd)
     spread(DOWN)
+    pass_on(IN, xri, zri)
+
+    shares_on(esend, erecv, epre, e_s, e_r)
 
     slots = vfull.shape[0] // s_n
     vfull[...] = jnp.zeros_like(vfull)
-    per = n_in // span
+    per = n_in // 128
     for i in range(3):
-        b = i * n + p
-        vfull[lax.div(b, per) * slots + lax.rem(b, per)] = bin_r[:, i * span : (i + 1) * span]
+        for h in range(2):
+            b = i * 2 * n + p + n * h
+            col = slice(i * span + h * 128, i * span + (h + 1) * 128)
+            vfull[lax.div(b, per) * slots + lax.rem(b, per)] = bin_r[:, col]
+    at_g = per + 2 * n
     for q in range(s_n):
-        vfull[q * slots + per + p] = bup_r[:, q * hb : (q + 1) * hb]
-        col = slice(q * rs, (q + 1) * rs)
-        g_own = g_all[pl.ds(mo(p * length, length), length), col].astype(F32)
-        vfull[q * slots + per + n] = jnp.sum(g_own, axis=0, keepdims=True)
-        for i in range(4):
-            vfull[q * slots + per + n + 1 + i] = vacc[i, :, col]
+        for h in range(2):
+            up_col = slice(q * hb + h * 128, q * hb + (h + 1) * 128)
+            vfull[q * slots + per + 2 * p + h] = bup_r[:, up_col]
+            col = slice(q * rs + h * 128, q * rs + (h + 1) * 128)
+            g_own = g_all[pl.ds(mo(p * length, length), length), col].astype(F32)
+            vfull[q * slots + at_g + h] = jnp.sum(g_own, axis=0, keepdims=True)
+            for i in range(4):
+                vfull[q * slots + at_g + 2 + 2 * i + h] = vacc[i, :, col]
     for i in range(1, s_n):
         q, dev = line(i)
         start(rc(vfull.at[pl.ds(q * slots, slots)], vz.at[zz], v1_s.at[i], v1_r.at[zz], dev))
 
-    shares_on(esend, erecv, epre, e_s, e_r)
-
-    far_and_inner = jnp.logical_and(to_far, inner)
-    on = rc(xro.at[0], zro.at[1], zs_s.at[OUT, 2], zs_r.at[OUT, 1], (r, p))
-
-    @pl.when(far_and_inner)
+    @pl.when(at_home)
     def _():
-        got(zro.at[2], zs_r.at[OUT, 2])
-        xro[0] = (xro[0].astype(F32) + zro[2].astype(F32)).astype(BF)
-        on.start()
-
-    sends.append((far_and_inner, on))
+        got(zro.at[0], zs_r.at[OUT, 0])
+        got(zro.at[1], zs_r.at[OUT, 1])
+        total = xro[near_b].astype(F32) + zro[0].astype(F32) + zro[1].astype(F32)
+        fo[...] = total.astype(BF)
+
+    oq = ohalf // 2
+
+    def o_whole(q):
+        return gout_o.at[lax.rem(q, 2), c]
+
+    def o_area(q, h):
+        return gout_o.at[lax.rem(q, 2), c, pl.ds(h * oq, oq)]
+
+    plane_send(lambda h: fo.at[pl.ds(h * oq, oq)], o_area, ag1(OUT), ag2(OUT), at_home)
+    start(rc(fo, o_whole(p), agc_s.at[OUT, 0], agc_r.at[OUT, p], partner), at_home)
+    cp = pltpu.make_async_copy(fo, o_whole(p), agl.at[OUT])
+    pl.when(at_home)(cp.start)
+    local_out.append((at_home, cp))
 
     got(mrecv.at[0], m_r.at[2])
     got(mrecv.at[1], m_r.at[3])
@@ -837,25 +884,9 @@
     lax.fori_loop(0, length // 32, mixed_rows, 0)
 
     spread_relay(DOWN)
-    pass_on(IN, xri, zri)
-    line_sum(UP, xru, zru, fu)
-    spread(UP)
-    spread_on(DOWN)
-
-    @pl.when(at_home)
-    def _():
-        got(zro.at[0], zs_r.at[OUT, 0])
-        got(zro.at[1], zs_r.at[OUT, 1])
-        total = xro[0].astype(F32) + zro[0].astype(F32) + zro[1].astype(F32)
-        fo[...] = total.astype(BF)
-
-    oq = ohalf // 2
-    o_area = lambda q, h: gout_o.at[c, pl.ds(h * oq, oq)]
-    plane_send(lambda h: fo.at[pl.ds(h * oq, oq)], o_area, ag1(OUT), ag2(OUT), at_home)
-    start(rc(fo, gout_o.at[c], agc_s.at[OUT, 0], agc_r.at[OUT, zz], partner), at_home)
-    cp = pltpu.make_async_copy(fo, gout_o.at[c], agl.at[OUT])
-    pl.when(at_home)(cp.start)
-    local_out.append((at_home, cp))
+    line_sum(IN, xri, zri, fi)
+    spread(IN)
+    pass_on(UP, xru, zru)
 
     total = [vfull[zz * slots + k] for k in range(slots)]
     for i in range(1, s_n):
@@ -868,28 +899,21 @@
     for i in range(1, 2 * n):
         start(rc(vu, vr.at[r], v2_s.at[i], v2_r.at[r], (lax.rem(r + i, 2 * n), zz)))
 
-    line_sum(IN, xri, zri, fi)
-    spread(IN)
-    spread_relay(UP)
-
-    from_x, from_y = xn == zz, yn == zz
-
-    @pl.when(away)
-    def _():
-        got(o_area(zz, 0), ag_r.at[OUT, zz, 0])
-
-    start(rc(o_area(zz, 0), o_area(zz, 0), ag_s.at[OUT, 4], ag_r.at[OUT, zz, 0], dev_y), from_x)
-
-    @pl.when(away)
-    def _():
-        got(o_area(zz, 1), ag_r.at[OUT, zz, 1])
-
-    start(rc(o_area(zz, 1), o_area(zz, 1), ag_s.at[OUT, 5], ag_r.at[OUT, zz, 1], dev_x), from_y)
-    start(
-        rc(gout_o.at[c], gout_o.at[c], agc_s.at[OUT, 1], agc_r.at[OUT, zz], partner), away
-    )
+    def o_got(q, h, cond):
+        @pl.when(cond)
+        def _():
+            got(o_area(q, h), ag_r.at[OUT, q, h])
+
+    o_got(xn, 0, at_home)
+    start(rc(o_area(xn, 0), o_area(xn, 0), ag_s.at[OUT, 4], ag_r.at[OUT, xn, 0], dev_y), at_home)
+    o_got(yn, 1, away)
+    start(rc(o_area(yn, 1), o_area(yn, 1), ag_s.at[OUT, 5], ag_r.at[OUT, yn, 1], dev_x), away)
+    spread_near(DOWN)
+    spread_far(DOWN)
     spread_relay(IN)
-    spread_on(UP)
+
+    line_sum(UP, xru, zru, fu)
+    spread(UP)
 
     got(erecv.at[0], e_r.at[2])
     got(erecv.at[1], e_r.at[3])
@@ -908,6 +932,14 @@
 
     lax.fori_loop(0, length // 32, tgrad_rows, 0)
 
+    o_got(xn, 1, at_home)
+    start(rc(o_whole(xn), o_whole(xn), agc_s.at[OUT, 1], agc_r.at[OUT, xn], partner), at_home)
+    o_got(yn, 0, away)
+    start(rc(o_whole(yn), o_whole(yn), agc_s.at[OUT, 2], agc_r.at[OUT, yn], partner), away)
+    o_got(dg, 0, away)
+    o_got(dg, 1, away)
+    start(rc(o_whole(dg), o_whole(dg), agc_s.at[OUT, 3], agc_r.at[OUT, dg], partner), away)
+
     for i in range(1, 2 * n):
         q = lax.rem(r + i, 2 * n)
         got(vr.at[q], v2_r.at[q])
@@ -916,10 +948,18 @@
         for q in range(1, 2 * n):
             t = t + vr[q, k]
         vec_o[k] = t
-    spread_on(IN)
-    for t in (DOWN, UP, IN):
+    spread_near(IN)
+    spread_far(IN)
+    spread_relay(UP)
+    spread_near(UP)
+    spread_far(UP)
+    for t in (DOWN, IN, UP):
         spread_end(t)
-    got(gout_o.at[other], agc_r.at[OUT, zz])
+    for q, cond in ((p, at_home), (xn, at_home), (yn, away), (dg, away)):
+
+        @pl.when(cond)
+        def _():
+            got(gout_o.at[lax.rem(q, 2), other], agc_r.at[OUT, q])
 
     for cond, cp in local_out:
         if cond is None:
@@ -940,7 +980,7 @@
     rs, hb, rows = z.rs, z.hb, z.rows
     iw = 3 * span
     nv = sum(v.shape[0] for v in vectors)
-    slots = 3 * width // s_n // span + n + 5
+    slots = (3 * width // s_n + hb * n + 5 * rs) // 128
     V = pltpu.VMEM
     dma = lambda *shape: pltpu.SemaphoreType.DMA(shape)
     share = [
@@ -957,16 +997,16 @@
         V((rows, hid), F32), V((rows, hid), BF), V((rows, span), BF),
         V((rows, span), BF), V((rows, hid), BF), V((rows, iw), BF),
         *share, *share,
-        V((s_n, rs, iw), BF), V((s_n, rs, hid), BF), V((s_n, hb, width), BF), V((1, span, width), BF),
-        *halves, V((1, span // 2, width), BF),
-        *halves, V((3, span // 2, width), BF),
-        V((rs // 2, iw), BF), V((rs // 2, hid), BF), V((hb // 2, width), BF), V((span // 2, width), BF),
-        V((1, nv), F32), V((s_n, 1, nv), F32), V((1, 3 * width), F32), V((s_n * slots, 1, 256), F32),
-        V((s_n, slots, 1, 256), F32), V((slots, 1, 256), F32), V((2 * n, slots, 1, 256), F32),
+        V((s_n, rs, iw), BF), V((s_n, rs, hid), BF), V((s_n, hb, width), BF), V((2, span // 2, width), BF),
+        *halves, V((2, span // 4, width), BF),
+        *halves, V((3, span // 4, width), BF),
+        V((rs // 2, iw), BF), V((rs // 2, hid), BF), V((hb // 2, width), BF), V((span // 4, width), BF),
+        V((1, nv), F32), V((s_n, 1, nv), F32), V((1, 3 * width), F32), V((s_n * slots, 1, 128), F32),
+        V((s_n, slots, 1, 128), F32), V((slots, 1, 128), F32), V((2 * n, slots, 1, 128), F32),
         V((rows, 1), F32), V((rows, 1), F32), V((4, 1, width), F32), V((1, iw), F32), V((1, hid), F32),
-        dma(s_n + 7), dma(s_n), dma(s_n), dma(6), dma(n, 2), dma(6), dma(n, 2),
-        dma(3, 2 * s_n), dma(3, s_n), dma(3, 2 * s_n), dma(3, s_n),
-        dma(3), dma(1), dma(1), dma(1),
+        dma(s_n + 10), dma(s_n), dma(s_n), dma(6), dma(n, 2), dma(6), dma(n, 2),
+        dma(3, 2, 2 * s_n), dma(3, 2, s_n), dma(3, 2, 2 * s_n), dma(3, 2, s_n),
+        dma(3), dma(2), dma(2), dma(2),
         dma(n), dma(n), dma(n), dma(n), dma(4), dma(4), dma(4, 3), dma(4, 4),
         dma(4, 6), dma(4, n, 2), dma(4, n), dma(4, n), dma(4),
         dma(s_n), dma(s_n), dma(2 * n), dma(2 * n),
@@ -979,8 +1019,8 @@
         jax.ShapeDtypeStruct((n, 2, rs // 2, iw), BF),
         jax.ShapeDtypeStruct((n, 2, rs // 2, hid), BF),
         jax.ShapeDtypeStruct((n, 2, hb // 2, width), BF),
-        jax.ShapeDtypeStruct((2, span // 2, width), BF),
-        jax.ShapeDtypeStruct((slots, 1, 256), F32),
+        jax.ShapeDtypeStruct((2, 2, span // 4, width), BF),
+        jax.ShapeDtypeStruct((slots, 1, 128), F32),
     ]
     return pl.pallas_call(
         functools.partial(fused, z),
@@ -1020,14 +1060,19 @@
         for core in range(2):
             row = slice(core * half, (core + 1) * half)
             jobs.append((g_in.at[q, core], bi.at[q, core], fi.at[q, core], [
-                (in_o.at[row, k * width + q * span : k * width + (q + 1) * span], slice(k * span, (k + 1) * span))
+                (
+                    in_o.at[row, k * width + (q + n * h) * 128 : k * width + (q + n * h + 1) * 128],
+                    slice(k * span + h * 128, k * span + (h + 1) * 128),
+                )
                 for k in range(3)
+                for h in range(2)
             ]))
-    for core in range(2):
-        start = core * (span // 2)
-        jobs.append((g_out.at[core], bo.at[core], fo.at[core], [
-            (out_o.at[start : start + span // 2], slice(None)),
-        ]))
+    for j in range(2):
+        for core in range(2):
+            start = (2 * j + core) * (span // 4)
+            jobs.append((g_out.at[j, core], bo.at[j, core], fo.at[j, core], [
+                (out_o.at[start : start + span // 4], slice(None)),
+            ]))
     through = [
         (pltpu.make_async_copy(a, b, m_sem.at[2 * i]), pltpu.make_async_copy(b, o, m_sem.at[2 * i + 1]))
         for i, (a, b, o) in enumerate(((mixed, m_v, mixed_o), (tgrad, t_v, tgrad_o)))
@@ -1056,11 +1101,11 @@
         b.start()
     k = 0
     for ref in vec_o:
-        blocks = ref.shape[0] // 256
+        blocks = ref.shape[0] // 128
         if ref is vec_o[3]:
             k -= blocks
         for i in range(blocks):
-            ref[i * 256 : (i + 1) * 256] = vec[k + i].reshape(256)
+            ref[i * 128 : (i + 1) * 128] = vec[k + i].reshape(128)
         k += blocks
     for cp in writes:
         cp.wait()
@@ -1090,7 +1135,7 @@
         scratch_shapes=[
             V((z.l, width), BF), V((z.l, width), F32),
             *[V(s, BF) for s in shapes], *[V(s, F32) for s in shapes],
-            dma(4), dma(6 * n + 2), dma(2 * n * (z.s + 4) + 2),
+            dma(4), dma(6 * n + 4), dma(2 * n * (z.s + 7) + 4),
         ],
         compiler_params=pltpu.CompilerParams(vmem_limit_bytes=VMEM_LIMIT),
         name="finish",

time: 180 us -> 149 us (0.83)
  the two profiles are of different devices: /device:TPU:9 before, /device:TPU:0 now
where the time goes in v4:
time: 149 us; the launch traced here: 147 us
  Pallas kernels  146 us (98%)
    pallas_call x1, Pallas kernels, fused_call(): pl.pallas_call(functools.partial(fused, z), out_shape=outs, in_specs=[any...  136 us
    pallas_call x1, Pallas kernels, finish_call(): pl.pallas_call(functools.partial(finish, z), out_shape=outs, in_specs=[an...  9.81 us

profile of v4, /device:TPU:0, one launch (start us, length us, event | category | flops | bytes accessed | tf_op | source)
XLA Modules:
  0.0 147.1 jit_solution(11578005682019520197)
XLA Ops:
  0.7 136.4 %block_step.1 = (bf16[256,1024]{1,0:T(8,128)(2,1)}, f32[256,1024]{1,0:T(8,128)}, bf16[4,2,128,768]{3,2,1,0:T(8,128)(2,1)}, bf16[4,2,128,1024]{3,2,1,0:T(8,128)(2...) custom-call(bf16[256,1024]{1,0:T(8,128)(2,1)} %refs_0_.1, ...), custom_call_target="tpu_custom_call" | custom-call | tf_op jit(solution)/shard_map/block_step/pallas_call | solution.py:1025
  137.1 9.8 %finish.1 = (bf16[256,1024]{1,0:T(8,128)(2,1)}, f32[256,1024]{1,0:T(8,128)}, f32[256,3072]{1,0:T(8,128)}, f32[256,4096]{1,0:T(8,128)}, f32[1024,1024]{1,0:T(8,12...) custom-call(bf16[256,1024]{1,0:T(8,128)(2,1)} %get-tuple-element.35., ...), custom_call_target="tpu_custom_call" | custom-call | tf_op jit(solution)/shard_map/finish/pallas_call | solution.py:1130

commit v5 on v4

--- a/solution.py
+++ b/solution.py
@@ -246,7 +246,7 @@
         x_all, g_all, a1, a2, wi, wu, wo, wd, qkv, pt, der, act, att, gatt, gup, gqkv,
         msend, mrecv, mpre, mown, esend, erecv, epre, eown,
         dwi, dwu, dwd, dwo, xri, xru, xrd, xro, zri, zru, zrd, zro, fi, fu, fd, fo,
-        vec, va, inb, vfull, vz, vu, vr, mean_r, inv_r, vacc, bin_r, bup_r,
+        vec, va, inb, vfull, vz, vu, vr, stat, vacc, bin_r, bup_r,
         loc, v_s, v_r, x_s, x_r, g_s, g_r, w_s, w_r, wc_s, wc_r,
         o_s, o_r, oc_s, oc_r, m_s, m_r, e_s, e_r, xs_s, xs_r, zs_s, zs_r,
         ag_s, ag_r, agc_s, agc_r, agl, v1_s, v1_r, v2_s, v2_r,
@@ -458,8 +458,8 @@
             xh = cen * inv
             a1[row, :] = (xh * gain1 + shift1).astype(BF)
             a2[row, :] = (xh * gain2 + shift2).astype(BF)
-            mean_r[row, :] = mu
-            inv_r[row, :] = inv
+            stat[row, 0:1] = mu
+            stat[row, 1:2] = inv
             return carry
 
         lax.fori_loop(0, length // step, body, 0)
@@ -655,18 +655,18 @@
     plane_near(part(g_all), sem2(g_r))
     plane_far(part(g_all), sem2(g_r))
 
-    for j in range(s_n):
-        dwd[j] = dot(act[:, j * hb : (j + 1) * hb], g_all[...], TN).astype(BF)
-    exchange(DOWN, dwd, xrd, hhalf)
     dwo_all = dot(att[...], g_all[...], TN).astype(BF)
     for i in range(2):
         dwo[i] = dwo_all[i * 128 : (i + 1) * 128]
     exchange(OUT, dwo, xro, ohalf)
-    pair_sum(DOWN, dwd, xrd, zrd, hhalf)
+    for j in range(s_n):
+        dwd[j] = dot(act[:, j * hb : (j + 1) * hb], g_all[...], TN).astype(BF)
+    exchange(DOWN, dwd, xrd, hhalf)
     core_sum(OUT, dwo, xro, ohalf)
     near_b, far_b = zp, 1 - zp
+    start(rc(xro.at[far_b], zro.at[2], zs_s.at[OUT, 1], zs_r.at[OUT, 2], mate_dev), is_end)
     start(rc(xro.at[near_b], zro.at[0], zs_s.at[OUT, 0], zs_r.at[OUT, 0], mate_dev), away)
-    start(rc(xro.at[far_b], zro.at[2], zs_s.at[OUT, 1], zs_r.at[OUT, 2], mate_dev), is_end)
+    pair_sum(DOWN, dwd, xrd, zrd, hhalf)
 
     def o_take(block, cond):
         @pl.when(cond)
@@ -724,34 +724,62 @@
             bin_r[:, col] += jnp.sum(val.astype(F32), axis=0, keepdims=True)
         return carry
 
-    lax.fori_loop(0, n * pairs, att_backward, 0)
-
-    for j in range(s_n):
-        dwi[j] = dot(a1[:, j * rs : (j + 1) * rs], gqkv[...], TN).astype(BF)
-    exchange(IN, dwi, xri, half)
+    lax.fori_loop(0, n * pairs - 4, att_backward, 0)
+    on = rc(xro.at[far_b], zro.at[1], zs_s.at[OUT, 2], zs_r.at[OUT, 1], (r, 2 * (1 - zp) + py))
+
+    @pl.when(inner)
+    def _():
+        got(zro.at[2], zs_r.at[OUT, 2])
+        xro[far_b] = (xro[far_b].astype(F32) + zro[2].astype(F32)).astype(BF)
+        on.start()
+
+    sends.append((inner, on))
+    lax.fori_loop(n * pairs - 4, n * pairs - 2, att_backward, 0)
+
     for d in range(1, s_n):
         relay(DOWN, d_piece, d, is_end)
     relay_done(DOWN, d_piece)
 
-    def shares(send, pre, ss, rr, k):
-        @pl.when(k == 0)
-        def _():
-            for h, dev in ((0, dev_x), (1, dev_y)):
-                rc(send.at[0, pl.ds(h * lh, lh)], pre.at[h], ss.at[h], rr.at[h], dev).start()
+    def ways(send, recv, pre, ss, rr):
+        row = lambda h: pl.ds(h * lh, lh)
+        return (
+            (0, rc(send.at[0, row(0)], pre.at[0], ss.at[0], rr.at[0], dev_x)),
+            (0, rc(send.at[0, row(1)], pre.at[1], ss.at[1], rr.at[1], dev_y)),
+            (1, rc(send.at[1, row(0)], recv.at[0, row(0)], ss.at[2], rr.at[2], dev_x)),
+            (2, rc(send.at[2, row(1)], recv.at[1, row(1)], ss.at[3], rr.at[3], dev_y)),
+        )
+
+    def shares(k, *refs):
+        for j in range(3):
+
+            @pl.when(k == j)
+            def _():
+                for i, cp in ways(*refs):
+                    if i == j:
+                        cp.start()
 
     def shares_on(send, recv, pre, ss, rr):
         for k, h, dev in ((1, 1, dev_x), (2, 0, dev_y)):
             got(pre.at[h], rr.at[h])
             row = pl.ds(h * lh, lh)
             send[k, row] = (send[k, row].astype(F32) + pre[h].astype(F32)).astype(BF)
-            start(rc(send.at[k], recv.at[k - 1], ss.at[k + 1], rr.at[k + 1], dev))
-
-    def shares_left(send, pre, ss, rr):
-        for h, dev in ((0, dev_x), (1, dev_y)):
-            rc(send.at[0, pl.ds(h * lh, lh)], pre.at[h], ss.at[h], rr.at[h], dev).wait_send()
+            start(rc(send.at[k, row], recv.at[k - 1, row], ss.at[k + 3], rr.at[k + 3], dev))
+
+    def shares_got(recv, rr):
+        for k, h in ((0, 0), (1, 1)):
+            row, rest = pl.ds(h * lh, lh), pl.ds((1 - h) * lh, lh)
+            got(recv.at[k, row], rr.at[k + 2])
+            got(recv.at[k, rest], rr.at[k + 4])
+
+    def shares_left(*refs):
+        for _, cp in ways(*refs):
+            cp.wait_send()
 
     def share_of(k):
         return jnp.where(k == 0, dg, jnp.where(k == 1, xn, jnp.where(k == 2, yn, p)))
+
+    m_refs = (msend, mrecv, mpre, m_s, m_r)
+    e_refs = (esend, erecv, epre, e_s, e_r)
 
     def out_block(k, carry):
         row = pl.ds(mo(share_of(k) * length, length), length)
@@ -760,13 +788,38 @@
             v = dot(att[row, :], wo[:, col]) + dot(act[row, :], wd[:, col])
             msend[k, :, col] = v.astype(BF)
             mown[:, col] = v
-        shares(msend, mpre, m_s, m_r, k)
+        shares(k, *m_refs)
         return carry
 
-    lax.fori_loop(0, 2, out_block, 0)
-    pair_sum(IN, dwi, xri, zri, half)
-    lax.fori_loop(2, n, out_block, 0)
+    lax.fori_loop(0, n, out_block, 0)
+    @pl.when(at_home)
+    def _():
+        got(zro.at[0], zs_r.at[OUT, 0])
+        got(zro.at[1], zs_r.at[OUT, 1])
+        total = xro[near_b].astype(F32) + zro[0].astype(F32) + zro[1].astype(F32)
+        fo[...] = total.astype(BF)
+
+    oq = ohalf // 2
+
+    def o_whole(q):
+        return gout_o.at[lax.rem(q, 2), c]
+
+    def o_area(q, h):
+        return gout_o.at[lax.rem(q, 2), c, pl.ds(h * oq, oq)]
+
+    plane_send(lambda h: fo.at[pl.ds(h * oq, oq)], o_area, ag1(OUT), ag2(OUT), at_home)
+    start(rc(fo, o_whole(p), agc_s.at[OUT, 0], agc_r.at[OUT, p], partner), at_home)
+    cp = pltpu.make_async_copy(fo, o_whole(p), agl.at[OUT])
+    pl.when(at_home)(cp.start)
+    local_out.append((at_home, cp))
+
     pass_on(DOWN, xrd, zrd)
+    lax.fori_loop(n * pairs - 2, n * pairs, att_backward, 0)
+    shares_on(*m_refs)
+
+    for j in range(s_n):
+        dwi[j] = dot(a1[:, j * rs : (j + 1) * rs], gqkv[...], TN).astype(BF)
+    exchange(IN, dwi, xri, half)
 
     def grad_up_block(s, carry):
         row = pl.ds(mo(s * length, length), length)
@@ -779,7 +832,7 @@
         return carry
 
     lax.fori_loop(0, 2, grad_up_block, 0)
-    shares_on(msend, mrecv, mpre, m_s, m_r)
+    pair_sum(IN, dwi, xri, zri, half)
     lax.fori_loop(2, n, grad_up_block, 0)
     for j in range(s_n):
         dwu[j] = dot(a2[:, j * rs : (j + 1) * rs], gup[...], TN).astype(BF)
@@ -791,8 +844,8 @@
         row = pl.ds(mo(share_of(k) * length, length), length)
         gq = gqkv[row, :]
         gu = gup[row, :]
-        mu = mean_r[row, :]
-        inv = inv_r[row, :]
+        mu = stat[row, 0:1]
+        inv = stat[row, 1:2]
         for j in range(s_n):
             col = slice(j * rs, (j + 1) * rs)
             d1 = dot(gq, wi[col, :], NT)
@@ -805,27 +858,19 @@
             e = d1 * gain1[:, col] + d2 * gain2[:, col]
             esend[k, :, col] = e.astype(BF)
             eown[:, col] = e
-        shares(esend, epre, e_s, e_r, k)
+        shares(k, *e_refs)
         return carry
 
     lax.fori_loop(0, 1, in_block, 0)
     pair_sum(UP, dwu, xru, zru, half)
-    lax.fori_loop(1, n, in_block, 0)
-
-    on = rc(xro.at[far_b], zro.at[1], zs_s.at[OUT, 2], zs_r.at[OUT, 1], (r, 2 * (1 - zp) + py))
-
-    @pl.when(inner)
-    def _():
-        got(zro.at[2], zs_r.at[OUT, 2])
-        xro[far_b] = (xro[far_b].astype(F32) + zro[2].astype(F32)).astype(BF)
-        on.start()
-
-    sends.append((inner, on))
+    lax.fori_loop(1, 3, in_block, 0)
+    pass_on(IN, xri, zri)
+    lax.fori_loop(3, n, in_block, 0)
+
     line_sum(DOWN, xrd, zrd, fd)
     spread(DOWN)
-    pass_on(IN, xri, zri)
-
-    shares_on(esend, erecv, epre, e_s, e_r)
+
+    shares_on(*e_refs)
 
     slots = vfull.shape[0] // s_n
     vfull[...] = jnp.zeros_like(vfull)
@@ -849,29 +894,9 @@
         q, dev = line(i)
         start(rc(vfull.at[pl.ds(q * slots, slots)], vz.at[zz], v1_s.at[i], v1_r.at[zz], dev))
 
-    @pl.when(at_home)
-    def _():
-        got(zro.at[0], zs_r.at[OUT, 0])
-        got(zro.at[1], zs_r.at[OUT, 1])
-        total = xro[near_b].astype(F32) + zro[0].astype(F32) + zro[1].astype(F32)
-        fo[...] = total.astype(BF)
-
-    oq = ohalf // 2
-
-    def o_whole(q):
-        return gout_o.at[lax.rem(q, 2), c]
-
-    def o_area(q, h):
-        return gout_o.at[lax.rem(q, 2), c, pl.ds(h * oq, oq)]
-
-    plane_send(lambda h: fo.at[pl.ds(h * oq, oq)], o_area, ag1(OUT), ag2(OUT), at_home)
-    start(rc(fo, o_whole(p), agc_s.at[OUT, 0], agc_r.at[OUT, p], partner), at_home)
-    cp = pltpu.make_async_copy(fo, o_whole(p), agl.at[OUT])
-    pl.when(at_home)(cp.start)
-    local_out.append((at_home, cp))
-
-    got(mrecv.at[0], m_r.at[2])
-    got(mrecv.at[1], m_r.at[3])
+    pass_on(UP, xru, zru)
+
+    shares_got(mrecv, m_r)
 
     def mixed_rows(i, carry):
         step = 32
@@ -886,8 +911,22 @@
     spread_relay(DOWN)
     line_sum(IN, xri, zri, fi)
     spread(IN)
-    pass_on(UP, xru, zru)
-
+    def o_got(q, h, cond):
+        @pl.when(cond)
+        def _():
+            got(o_area(q, h), ag_r.at[OUT, q, h])
+
+    o_got(xn, 0, at_home)
+    start(rc(o_area(xn, 0), o_area(xn, 0), ag_s.at[OUT, 4], ag_r.at[OUT, xn, 0], dev_y), at_home)
+    o_got(yn, 1, away)
+    start(rc(o_area(yn, 1), o_area(yn, 1), ag_s.at[OUT, 5], ag_r.at[OUT, yn, 1], dev_x), away)
+    line_sum(UP, xru, zru, fu)
+    spread(UP)
+
+    spread_relay(IN)
+
+    spread_near(DOWN)
+    spread_far(DOWN)
     total = [vfull[zz * slots + k] for k in range(slots)]
     for i in range(1, s_n):
         q, dev = line(i)
@@ -899,31 +938,14 @@
     for i in range(1, 2 * n):
         start(rc(vu, vr.at[r], v2_s.at[i], v2_r.at[r], (lax.rem(r + i, 2 * n), zz)))
 
-    def o_got(q, h, cond):
-        @pl.when(cond)
-        def _():
-            got(o_area(q, h), ag_r.at[OUT, q, h])
-
-    o_got(xn, 0, at_home)
-    start(rc(o_area(xn, 0), o_area(xn, 0), ag_s.at[OUT, 4], ag_r.at[OUT, xn, 0], dev_y), at_home)
-    o_got(yn, 1, away)
-    start(rc(o_area(yn, 1), o_area(yn, 1), ag_s.at[OUT, 5], ag_r.at[OUT, yn, 1], dev_x), away)
-    spread_near(DOWN)
-    spread_far(DOWN)
-    spread_relay(IN)
-
-    line_sum(UP, xru, zru, fu)
-    spread(UP)
-
-    got(erecv.at[0], e_r.at[2])
-    got(erecv.at[1], e_r.at[3])
+    shares_got(erecv, e_r)
 
     def tgrad_rows(i, carry):
         step = 32
         row = pl.ds(mo(i * step, step), step)
         far = pl.ds(mo(p * length + i * step, step), step)
-        inv = inv_r[far, :]
-        xh = (x_all[far, :].astype(F32) - mean_r[far, :]) * inv
+        inv = stat[far, 1:2]
+        xh = (x_all[far, :].astype(F32) - stat[far, 0:1]) * inv
         e = eown[row, :] + erecv[0, row, :].astype(F32) + erecv[1, row, :].astype(F32)
         m0 = jnp.mean(e, axis=1, keepdims=True)
         m1 = jnp.mean(e * xh, axis=1, keepdims=True)
@@ -932,6 +954,7 @@
 
     lax.fori_loop(0, length // 32, tgrad_rows, 0)
 
+    spread_relay(UP)
     o_got(xn, 1, at_home)
     start(rc(o_whole(xn), o_whole(xn), agc_s.at[OUT, 1], agc_r.at[OUT, xn], partner), at_home)
     o_got(yn, 0, away)
@@ -940,6 +963,8 @@
     o_got(dg, 1, away)
     start(rc(o_whole(dg), o_whole(dg), agc_s.at[OUT, 3], agc_r.at[OUT, dg], partner), away)
 
+    spread_near(IN)
+    spread_far(IN)
     for i in range(1, 2 * n):
         q = lax.rem(r + i, 2 * n)
         got(vr.at[q], v2_r.at[q])
@@ -948,9 +973,6 @@
         for q in range(1, 2 * n):
             t = t + vr[q, k]
         vec_o[k] = t
-    spread_near(IN)
-    spread_far(IN)
-    spread_relay(UP)
     spread_near(UP)
     spread_far(UP)
     for t in (DOWN, IN, UP):
@@ -966,8 +988,8 @@
             cp.wait()
         else:
             pl.when(cond)(cp.wait)
-    shares_left(msend, mpre, m_s, m_r)
-    shares_left(esend, epre, e_s, e_r)
+    shares_left(*m_refs)
+    shares_left(*e_refs)
     for cond, cp in sends:
         if cond is None:
             cp.wait_send()
@@ -1003,11 +1025,11 @@
         V((rs // 2, iw), BF), V((rs // 2, hid), BF), V((hb // 2, width), BF), V((span // 4, width), BF),
         V((1, nv), F32), V((s_n, 1, nv), F32), V((1, 3 * width), F32), V((s_n * slots, 1, 128), F32),
         V((s_n, slots, 1, 128), F32), V((slots, 1, 128), F32), V((2 * n, slots, 1, 128), F32),
-        V((rows, 1), F32), V((rows, 1), F32), V((4, 1, width), F32), V((1, iw), F32), V((1, hid), F32),
+        V((rows, 2), F32), V((4, 1, width), F32), V((1, iw), F32), V((1, hid), F32),
         dma(s_n + 10), dma(s_n), dma(s_n), dma(6), dma(n, 2), dma(6), dma(n, 2),
         dma(3, 2, 2 * s_n), dma(3, 2, s_n), dma(3, 2, 2 * s_n), dma(3, 2, s_n),
         dma(3), dma(2), dma(2), dma(2),
-        dma(n), dma(n), dma(n), dma(n), dma(4), dma(4), dma(4, 3), dma(4, 4),
+        dma(6), dma(6), dma(6), dma(6), dma(4), dma(4), dma(4, 3), dma(4, 4),
         dma(4, 6), dma(4, n, 2), dma(4, n), dma(4, n), dma(4),
         dma(s_n), dma(s_n), dma(2 * n), dma(2 * n),
     ]

time: 149 us -> 143 us (0.960); the launches traced: 147 us -> 143 us
  Pallas kernels: 146 us -> 142 us
    pallas_call x1, Pallas kernels: 136 us -> 132 us  [fused_call(): pl.pallas_call(functools.partial(fused, z), out_shape=outs, in_specs=[any...]
where the time goes in v5:
time: 143 us
  Pallas kernels  142 us (99%)
    pallas_call x1, Pallas kernels, fused_call(): pl.pallas_call(functools.partial(fused, z), out_shape=outs, in_specs=[any...  132 us
    pallas_call x1, Pallas kernels, finish_call(): pl.pallas_call(functools.partial(finish, z), out_shape=outs, in_specs=[an...  9.81 us

profile of v5, /device:TPU:0, one launch (start us, length us, event | category | flops | bytes accessed | tf_op | source)
XLA Modules:
  0.0 142.6 jit_solution(12861848246632617870)
XLA Ops:
  0.7 131.9 %block_step.1 = (bf16[256,1024]{1,0:T(8,128)(2,1)}, f32[256,1024]{1,0:T(8,128)}, bf16[4,2,128,768]{3,2,1,0:T(8,128)(2,1)}, bf16[4,2,128,1024]{3,2,1,0:T(8,128)(2...) custom-call(bf16[256,1024]{1,0:T(8,128)(2,1)} %refs_0_.1, ...), custom_call_target="tpu_custom_call" | custom-call | tf_op jit(solution)/shard_map/block_step/pallas_call | solution.py:1047
  132.6 9.8 %finish.1 = (bf16[256,1024]{1,0:T(8,128)(2,1)}, f32[256,1024]{1,0:T(8,128)}, f32[256,3072]{1,0:T(8,128)}, f32[256,4096]{1,0:T(8,128)}, f32[1024,1024]{1,0:T(8,12...) custom-call(bf16[256,1024]{1,0:T(8,128)(2,1)} %get-tuple-element.35., ...), custom_call_target="tpu_custom_call" | custom-call | tf_op jit(solution)/shard_map/finish/pallas_call | solution.py:1152

commit v6 on v5

--- a/solution.py
+++ b/solution.py
@@ -188,6 +188,7 @@
 NT = ((1,), (1,))
 TN = ((0,), (0,))
 IN, UP, DOWN, OUT = range(4)
+VECTORS, TOKENS, COTANGENTS, ROWS, OUTPUT, INPUT, SUMS, TOTALS = range(8)
 
 
 class Sizes:
@@ -240,16 +241,16 @@
 
 def fused(z, *refs):
     (tok, cot, inp, upp, outp, downp) = refs[:6]
-    vectors_in, rot = refs[6:14], refs[14]
+    vectors_in, rot_in = refs[6:14], refs[14]
     (mixed_o, tgrad_o, gin_o, gup_o, gdown_o, gout_o, vec_o) = refs[15:22]
     (
         x_all, g_all, a1, a2, wi, wu, wo, wd, qkv, pt, der, act, att, gatt, gup, gqkv,
         msend, mrecv, mpre, mown, esend, erecv, epre, eown,
         dwi, dwu, dwd, dwo, xri, xru, xrd, xro, zri, zru, zrd, zro, fi, fu, fd, fo,
         vec, va, inb, vfull, vz, vu, vr, stat, vacc, bin_r, bup_r,
-        loc, v_s, v_r, x_s, x_r, g_s, g_r, w_s, w_r, wc_s, wc_r,
-        o_s, o_r, oc_s, oc_r, m_s, m_r, e_s, e_r, xs_s, xs_r, zs_s, zs_r,
-        ag_s, ag_r, agc_s, agc_r, agl, v1_s, v1_r, v2_s, v2_r,
+        loc, io, one_s, one_r, x_r, g_r, w_s, w_r, wc_s, wc_r, o_r, oc_s, oc_r,
+        m_r, e_r, xs_s, xs_r, zs_s, zs_r, zo_s, zo_r, ag_s, ag_r, agc_s, agc_r, agl,
+        rot, mixed_v, tgrad_v, vec_v, *vectors_v,
     ) = refs[22:]
     n, s_n, length, width = z.n, z.s, z.l, z.d
     span, hid, rs, hb = z.span, z.hid, z.rs, z.hb
@@ -270,7 +271,7 @@
     mate = 2 * zp + 1 - zo
     mate_dev = (r, mate)
     far_end, far_inner = 3 * (1 - zp), 2 - zp
-    left, right = (r, zz - 1), (r, zz + 1)
+    to_left, to_right = (r, zz - 1), (r, zz + 1)
     has_left, has_right = zz > 0, zz < s_n - 1
 
     def rc(src, dst, ss, rr, dev):
@@ -283,15 +284,19 @@
 
     def seq(ref, s):
         return ref.at[pl.ds(mo(s * length, length), length)]
-
-    sends = []
 
     def start(copy, cond=None):
         if cond is None:
             copy.start()
         else:
             pl.when(cond)(copy.start)
-        sends.append((cond, copy))
+
+    def left(ref, ss, cond=None):
+        cp = rc(ref, ref, ss, ss, partner)
+        if cond is None:
+            cp.wait_send()
+        else:
+            pl.when(cond)(cp.wait_send)
 
     own_rows = pl.ds(mo(zz * rs, rs), rs)
     own_hb = pl.ds(mo(zz * hb, hb), hb)
@@ -299,7 +304,7 @@
         pltpu.make_async_copy(
             upp.at[:, pl.ds(mo(i * (hb * n) + p * hb, hb), hb)],
             wu.at[own_rows, pl.ds(i * hb, hb)],
-            loc.at[i],
+            loc.at[1],
         )
         for i in range(s_n)
     ]
@@ -307,27 +312,32 @@
         pltpu.make_async_copy(
             inp.at[:, pl.ds(mo(i * width + (p + n * k) * 128, 128), 128)],
             wi.at[own_rows, pl.ds(i * span + k * 128, 128)],
-            loc.at[s_n + 2 * i + k],
+            loc.at[0],
         )
         for i in range(3)
         for k in range(2)
     ]
-    at_loc = s_n + 6
     local_d = pltpu.make_async_copy(
-        downp.at[pl.ds(mo(p * hb, hb), hb)], wd.at[own_hb], loc.at[at_loc]
+        downp.at[pl.ds(mo(p * hb, hb), hb)], wd.at[own_hb], loc.at[2]
     )
-    local_x = pltpu.make_async_copy(tok, seq(x_all, p), loc.at[at_loc + 1])
-    local_g = pltpu.make_async_copy(cot, seq(g_all, p), loc.at[at_loc + 2])
+    local_x = pltpu.make_async_copy(tok, seq(x_all, p), loc.at[3])
+    local_g = pltpu.make_async_copy(cot, seq(g_all, p), loc.at[4])
     local_o = pltpu.make_async_copy(
-        outp.at[pl.ds(mo(px * 128, 128), 128)], wo.at[pl.ds(mo(zp * 128, 128), 128)], loc.at[at_loc + 3]
+        outp.at[pl.ds(mo(px * 128, 128), 128)], wo.at[pl.ds(mo(zp * 128, 128), 128)], loc.at[5]
     )
     at_home = zo == py
     away = jnp.logical_not(at_home)
-    for cp in local_i + [local_x] + local_u + [local_g, local_d]:
+    local_v = [
+        pltpu.make_async_copy(src, dst, io.at[i])
+        for i, (src, dst) in enumerate(zip(vectors_in, vectors_v))
+    ]
+    local_r = pltpu.make_async_copy(rot_in, rot, io.at[8])
+    for cp in local_v + local_i + [local_x] + local_u + [local_g, local_d, local_r]:
         cp.start()
     pl.when(at_home)(local_o.start)
     off = 0
-    for ref in vectors_in:
+    for ref, cp in zip(vectors_v, local_v):
+        cp.wait()
         size = ref.shape[0]
         vec[:, off : off + size] = ref[...].astype(F32).reshape(1, size)
         off += size
@@ -346,46 +356,43 @@
         return q, (r, q)
 
     def plane_send(src, dst, ss, rr, cond=None):
-        start(rc(src(0), dst(p, 0), ss(0), rr(p, 0), dev_x), cond)
-        start(rc(src(1), dst(p, 1), ss(1), rr(p, 1), dev_y), cond)
-        start(rc(src(1), dst(p, 1), ss(2), rr(p, 1), dev_x), cond)
-        start(rc(src(0), dst(p, 0), ss(3), rr(p, 0), dev_y), cond)
+        start(rc(src(0), dst(p, 0), ss, rr(0), dev_x), cond)
+        start(rc(src(1), dst(p, 1), ss, rr(1), dev_y), cond)
+        start(rc(src(1), dst(p, 1), ss, rr(2), dev_x), cond)
+        start(rc(src(0), dst(p, 0), ss, rr(2), dev_y), cond)
 
     def plane_relay(dst, ss, rr):
-        got(dst(xn, 0), rr(xn, 0))
-        start(rc(dst(xn, 0), dst(xn, 0), ss(4), rr(xn, 0), dev_y))
-        got(dst(yn, 1), rr(yn, 1))
-        start(rc(dst(yn, 1), dst(yn, 1), ss(5), rr(yn, 1), dev_x))
-
-    def plane_near(dst, rr):
-        got(dst(xn, 1), rr(xn, 1))
-        got(dst(yn, 0), rr(yn, 0))
-
-    def plane_far(dst, rr):
-        got(dst(dg, 0), rr(dg, 0))
-        got(dst(dg, 1), rr(dg, 1))
+        got(dst(xn, 0), rr(0))
+        start(rc(dst(xn, 0), dst(xn, 0), ss, rr(3), dev_y))
+        got(dst(yn, 1), rr(1))
+        start(rc(dst(yn, 1), dst(yn, 1), ss, rr(3), dev_x))
+
+    def plane_near(block, rr):
+        got(block, rr(2))
+
+    def plane_far(block, rr):
+        got(block, rr(3))
 
     lh = length // 2
 
     def part(ref):
         return lambda q, h: ref.at[pl.ds(mo(q * length + h * lh, lh), lh)]
 
-    def sem1(ref):
+    def sems(ref):
         return lambda i: ref.at[i]
-
-    def sem2(ref):
-        return lambda q, h: ref.at[q, h]
 
     def rows_of(ref):
         return lambda h: ref.at[pl.ds(h * lh, lh)]
 
     for i in range(1, s_n):
         q, dev = line(i)
-        start(rc(vec, va.at[zz], v_s.at[i], v_r.at[zz], dev))
-    plane_send(rows_of(tok), part(x_all), sem1(x_s), sem2(x_r))
+        start(rc(vec, va.at[zz], one_s.at[VECTORS], one_r.at[0], dev))
+    plane_send(rows_of(tok), part(x_all), one_s.at[TOKENS], sems(x_r))
 
     half, hhalf, ohalf = rs // 2, hb // 2, span // 4
     cuts = {IN: 2, UP: 1, DOWN: 1}
+    stream = {IN: 0, UP: 2, DOWN: 3}
+    weight = {IN: wi, UP: wu, DOWN: wd}
 
     def piece(t, ref, block):
         rows = block // 2 // cuts[t]
@@ -396,42 +403,40 @@
     def own_sends(t, get):
         for h in range(cuts[t]):
             mine = get(zz, c, h)
-            start(rc(mine, mine, w_s.at[t, h, 0], w_r.at[t, h, zz], left), has_left)
-            start(rc(mine, mine, w_s.at[t, h, 1], w_r.at[t, h, zz], right), has_right)
+            k = stream[t] + h
+            start(rc(mine, mine, w_s.at[k], w_r.at[k, zz], to_left), has_left)
+            start(rc(mine, mine, w_s.at[k], w_r.at[k, zz], to_right), has_right)
 
     def relay(t, get, d, who):
-        def take(h, q, has, onward, more, slot):
+        def take(h, q, has, onward, more):
             ref = get(q, c, h)
+            k = stream[t] + h
 
             @pl.when(has)
             def _():
-                got(ref, w_r.at[t, h, q])
-
-            start(
-                rc(ref, ref, w_s.at[t, h, slot], w_r.at[t, h, q], onward),
-                jnp.logical_and(has, more),
-            )
-            start(rc(ref, ref, wc_s.at[t, h, slot], wc_r.at[t, h, q], partner), has)
+                got(ref, w_r.at[k, q])
+
+            start(rc(ref, ref, w_s.at[k], w_r.at[k, q], onward), jnp.logical_and(has, more))
+            start(rc(ref, ref, wc_s.at[k], wc_r.at[k], partner), has)
 
         for h in range(cuts[t]):
             from_left = jnp.logical_and(who, zz - d >= 0)
             from_right = jnp.logical_and(who, zz + d <= s_n - 1)
-            take(h, zz - d, from_left, right, has_right, 2 * d)
-            take(h, zz + d, from_right, left, has_left, 2 * d + 1)
-
-    def relay_done(t, get):
+            take(h, zz - d, from_left, to_right, has_right)
+            take(h, zz + d, from_right, to_left, has_left)
+
+    def pieces(t, count):
+        rows = weight[t].shape[0] // s_n // 2 // cuts[t]
+        return weight[t].at[pl.ds(0, count * rows)]
+
+    def relay_done(t):
         for h in range(cuts[t]):
-            for i in range(1, s_n):
-                q, _ = line(i)
-                got(get(q, other, h), wc_r.at[t, h, q])
-
-    for cp in local_i:
-        cp.wait()
+            got(pieces(t, s_n - 1), wc_r.at[stream[t] + h])
+
+    pltpu.make_async_copy(wi.at[own_rows], wi.at[own_rows], loc.at[0]).wait()
     own_sends(IN, i_piece)
 
-    for i in range(1, s_n):
-        q, dev = line(i)
-        got(va.at[q], v_r.at[q])
+    got(va.at[pl.ds(0, s_n - 1)], one_r.at[0])
     va[zz] = vec[...]
     n_in = 3 * width // s_n
     n_up = hb * n
@@ -464,6 +469,7 @@
 
         lax.fori_loop(0, length // step, body, 0)
 
+    local_r.wait()
     table = [rot[i] for i in range(3)]
 
     def turn(t, sign):
@@ -491,18 +497,17 @@
     local_x.wait()
     norm(p)
     relay(IN, i_piece, 2, inner)
-    for cp in local_u:
-        cp.wait()
+    pltpu.make_async_copy(wu.at[own_rows], wu.at[own_rows], loc.at[1]).wait()
     own_sends(UP, u_piece)
-    plane_relay(part(x_all), sem1(x_s), sem2(x_r))
-    plane_send(rows_of(cot), part(g_all), sem1(g_s), sem2(g_r))
-    plane_near(part(x_all), sem2(x_r))
+    plane_relay(part(x_all), one_s.at[TOKENS], sems(x_r))
+    plane_send(rows_of(cot), part(g_all), one_s.at[COTANGENTS], sems(g_r))
+    plane_near(seq(x_all, xn), sems(x_r))
     norm(xn)
     norm(yn)
     relay(UP, u_piece, 1, inner)
     for d in range(1, s_n):
         relay(IN, i_piece, d, is_end)
-    relay_done(IN, i_piece)
+    relay_done(IN)
     lax.fori_loop(0, 3, qkv_block, 0)
     relay(UP, u_piece, 2, inner)
     local_d.wait()
@@ -512,12 +517,12 @@
 
     pl.when(at_home)(local_o.wait)
     near_first = (mate_dev, (r, far_inner), (r, far_end))
-    for i, dev in enumerate(near_first):
-        start(rc(o_piece(zp, c), o_piece(zp, c), o_s.at[i], o_r.at[zp], dev), at_home)
-    plane_far(part(x_all), sem2(x_r))
+    for dev in near_first:
+        start(rc(o_piece(zp, c), o_piece(zp, c), one_s.at[ROWS], o_r.at[zp], dev), at_home)
+    plane_far(seq(x_all, dg), sems(x_r))
     norm(dg)
     lax.fori_loop(3, n, qkv_block, 0)
-    plane_relay(part(g_all), sem1(g_s), sem2(g_r))
+    plane_relay(part(g_all), one_s.at[COTANGENTS], sems(g_r))
 
     lane = lax.broadcasted_iota(jnp.int32, (1, 128), 1)
     first = lane < HEAD_DIM
@@ -548,7 +553,7 @@
     lax.fori_loop(n * pairs // 2, n * pairs, att_forward, 0)
     for d in range(1, s_n):
         relay(UP, u_piece, d, is_end)
-    relay_done(UP, u_piece)
+    relay_done(UP)
 
     def up_block(s, carry):
         row = pl.ds(mo(s * length, length), length)
@@ -581,25 +586,20 @@
 
     def pair_sum(t, dw, xr, zr, block_half):
         core_sum(t, dw, xr, block_half)
-        start(rc(xr.at[far_end], zr.at[2], zs_s.at[t, 0], zs_r.at[t, 2], mate_dev), is_end)
-        start(rc(xr.at[far_inner], zr.at[3], zs_s.at[t, 1], zs_r.at[t, 3], mate_dev), is_end)
-        start(rc(xr.at[mate], zr.at[0], zs_s.at[t, 2], zs_r.at[t, 0], mate_dev))
+        start(rc(xr.at[far_end], zr.at[2], zs_s.at[t], zs_r.at[t, 1], mate_dev), is_end)
+        start(rc(xr.at[far_inner], zr.at[3], zs_s.at[t], zs_r.at[t, 2], mate_dev), is_end)
+        start(rc(xr.at[mate], zr.at[0], zs_s.at[t], zs_r.at[t, 0], mate_dev))
 
     def pass_on(t, xr, zr):
         @pl.when(inner)
         def _():
             for slot, q in ((2, far_end), (3, far_inner)):
-                got(zr.at[slot], zs_r.at[t, slot])
+                got(zr.at[slot], zs_r.at[t, slot - 1])
                 xr[q] = (xr[q].astype(F32) + zr[slot].astype(F32)).astype(BF)
-                rc(xr.at[q], zr.at[1], zs_s.at[t, slot - 2], zs_r.at[t, 1], (r, q)).start()
-
-        for slot, q in ((2, far_end), (3, far_inner)):
-            cp = rc(xr.at[q], zr.at[1], zs_s.at[t, slot - 2], zs_r.at[t, 1], (r, q))
-            sends.append((inner, cp))
+                rc(xr.at[q], zr.at[1], zs_s.at[t], zs_r.at[t, 0], (r, q)).start()
 
     def line_sum(t, xr, zr, fin):
-        got(zr.at[0], zs_r.at[t, 0])
-        got(zr.at[1], zs_r.at[t, 1])
+        got(zr.at[pl.ds(0, 2)], zs_r.at[t, 0])
         total = xr[zz].astype(F32) + zr[0].astype(F32) + zr[1].astype(F32)
         fin[...] = total.astype(BF)
 
@@ -615,45 +615,38 @@
         rows = fin.shape[0] // 2
         return lambda h: fin.at[pl.ds(h * rows, rows)]
 
-    def ag1(t):
-        return lambda i: ag_s.at[t, i]
-
-    def ag2(t):
-        return lambda q, h: ag_r.at[t, q, h]
-
     local_out = []
 
     def spread(t):
         o, fin = outs_of[t]
-        plane_send(fin_half(t), area(t), ag1(t), ag2(t))
-        start(rc(fin, o.at[p, c], agc_s.at[t, 0], agc_r.at[t, p], partner))
+        plane_send(fin_half(t), area(t), ag_s.at[t], sems(ag_r.at[t]))
+        start(rc(fin, o.at[p, c], agc_s.at[t], agc_r.at[t], partner))
         cp = pltpu.make_async_copy(fin, o.at[p, c], agl.at[t])
         cp.start()
         local_out.append((None, cp))
 
     def spread_relay(t):
-        plane_relay(area(t), ag1(t), ag2(t))
+        plane_relay(area(t), ag_s.at[t], sems(ag_r.at[t]))
+
+    def across(t, q):
+        o = outs_of[t][0]
+        start(rc(o.at[q, c], o.at[q, c], agc_s.at[t], agc_r.at[t], partner))
 
     def spread_near(t):
-        o = outs_of[t][0]
-        plane_near(area(t), ag2(t))
-        start(rc(o.at[xn, c], o.at[xn, c], agc_s.at[t, 1], agc_r.at[t, xn], partner))
-        start(rc(o.at[yn, c], o.at[yn, c], agc_s.at[t, 2], agc_r.at[t, yn], partner))
+        plane_near(outs_of[t][0].at[xn, c], sems(ag_r.at[t]))
+        across(t, xn)
+        across(t, yn)
 
     def spread_far(t):
-        o = outs_of[t][0]
-        plane_far(area(t), ag2(t))
-        start(rc(o.at[dg, c], o.at[dg, c], agc_s.at[t, 3], agc_r.at[t, dg], partner))
+        plane_far(outs_of[t][0].at[dg, c], sems(ag_r.at[t]))
+        across(t, dg)
 
     def spread_end(t):
-        o = outs_of[t][0]
-        for i in range(n):
-            q = lax.rem(p + i, n)
-            got(o.at[q, other], agc_r.at[t, q])
+        got(outs_of[t][0].at[:, other], agc_r.at[t])
 
     local_g.wait()
-    plane_near(part(g_all), sem2(g_r))
-    plane_far(part(g_all), sem2(g_r))
+    plane_near(seq(g_all, xn), sems(g_r))
+    plane_far(seq(g_all, dg), sems(g_r))
 
     dwo_all = dot(att[...], g_all[...], TN).astype(BF)
     for i in range(2):
@@ -664,29 +657,29 @@
     exchange(DOWN, dwd, xrd, hhalf)
     core_sum(OUT, dwo, xro, ohalf)
     near_b, far_b = zp, 1 - zp
-    start(rc(xro.at[far_b], zro.at[2], zs_s.at[OUT, 1], zs_r.at[OUT, 2], mate_dev), is_end)
-    start(rc(xro.at[near_b], zro.at[0], zs_s.at[OUT, 0], zs_r.at[OUT, 0], mate_dev), away)
+    start(rc(xro.at[far_b], zro.at[2], zo_s.at[0], zo_r.at[1], mate_dev), is_end)
+    start(rc(xro.at[near_b], zro.at[0], zo_s.at[1], zo_r.at[0], mate_dev), away)
     pair_sum(DOWN, dwd, xrd, zrd, hhalf)
 
-    def o_take(block, cond):
+    def o_take(k, block, cond):
+        ref = o_piece(block, c)
+
         @pl.when(cond)
         def _():
-            got(o_piece(block, c), o_r.at[block])
-
-        start(
-            rc(o_piece(block, c), o_piece(block, c), oc_s.at[block], oc_r.at[block], partner), cond
-        )
-
-    def o_done(block, cond):
+            got(ref, o_r.at[block])
+
+        start(rc(ref, ref, oc_s.at[k], oc_r.at[k], partner), cond)
+
+    def o_done(k, block, cond):
         @pl.when(cond)
         def _():
-            got(o_piece(block, other), oc_r.at[block])
+            got(o_piece(block, other), oc_r.at[k])
 
     always = zz >= 0
-    o_take(near_b, away)
-    o_take(far_b, always)
-    o_done(near_b, away)
-    o_done(far_b, always)
+    o_take(0, near_b, away)
+    o_take(1, far_b, always)
+    o_done(0, near_b, away)
+    o_done(1, far_b, always)
 
     bup_r[...] = jnp.zeros_like(bup_r)
     bin_r[...] = jnp.zeros_like(bin_r)
@@ -725,61 +718,48 @@
         return carry
 
     lax.fori_loop(0, n * pairs - 4, att_backward, 0)
-    on = rc(xro.at[far_b], zro.at[1], zs_s.at[OUT, 2], zs_r.at[OUT, 1], (r, 2 * (1 - zp) + py))
+    on = rc(xro.at[far_b], zro.at[1], zo_s.at[0], zo_r.at[0], (r, 2 * (1 - zp) + py))
 
     @pl.when(inner)
     def _():
-        got(zro.at[2], zs_r.at[OUT, 2])
+        got(zro.at[2], zo_r.at[1])
         xro[far_b] = (xro[far_b].astype(F32) + zro[2].astype(F32)).astype(BF)
         on.start()
 
-    sends.append((inner, on))
     lax.fori_loop(n * pairs - 4, n * pairs - 2, att_backward, 0)
 
     for d in range(1, s_n):
         relay(DOWN, d_piece, d, is_end)
-    relay_done(DOWN, d_piece)
-
-    def ways(send, recv, pre, ss, rr):
+    relay_done(DOWN)
+
+    def shares(k, send, recv, pre, ss, rr):
         row = lambda h: pl.ds(h * lh, lh)
-        return (
-            (0, rc(send.at[0, row(0)], pre.at[0], ss.at[0], rr.at[0], dev_x)),
-            (0, rc(send.at[0, row(1)], pre.at[1], ss.at[1], rr.at[1], dev_y)),
-            (1, rc(send.at[1, row(0)], recv.at[0, row(0)], ss.at[2], rr.at[2], dev_x)),
-            (2, rc(send.at[2, row(1)], recv.at[1, row(1)], ss.at[3], rr.at[3], dev_y)),
-        )
-
-    def shares(k, *refs):
-        for j in range(3):
-
-            @pl.when(k == j)
-            def _():
-                for i, cp in ways(*refs):
-                    if i == j:
-                        cp.start()
+
+        @pl.when(k == 0)
+        def _():
+            rc(send.at[0, row(0)], pre.at[0], ss, rr.at[0], dev_x).start()
+            rc(send.at[0, row(1)], pre.at[1], ss, rr.at[1], dev_y).start()
+
+        @pl.when(k == 1)
+        def _():
+            rc(send.at[1, row(0)], recv.at[0, row(0)], ss, rr.at[2], dev_x).start()
+
+        @pl.when(k == 2)
+        def _():
+            rc(send.at[2, row(1)], recv.at[1, row(1)], ss, rr.at[2], dev_y).start()
 
     def shares_on(send, recv, pre, ss, rr):
         for k, h, dev in ((1, 1, dev_x), (2, 0, dev_y)):
             got(pre.at[h], rr.at[h])
             row = pl.ds(h * lh, lh)
             send[k, row] = (send[k, row].astype(F32) + pre[h].astype(F32)).astype(BF)
-            start(rc(send.at[k, row], recv.at[k - 1, row], ss.at[k + 3], rr.at[k + 3], dev))
-
-    def shares_got(recv, rr):
-        for k, h in ((0, 0), (1, 1)):
-            row, rest = pl.ds(h * lh, lh), pl.ds((1 - h) * lh, lh)
-            got(recv.at[k, row], rr.at[k + 2])
-            got(recv.at[k, rest], rr.at[k + 4])
-
-    def shares_left(*refs):
-        for _, cp in ways(*refs):
-            cp.wait_send()
+            start(rc(send.at[k, row], recv.at[k - 1, row], ss, rr.at[2], dev))
 
     def share_of(k):
         return jnp.where(k == 0, dg, jnp.where(k == 1, xn, jnp.where(k == 2, yn, p)))
 
-    m_refs = (msend, mrecv, mpre, m_s, m_r)
-    e_refs = (esend, erecv, epre, e_s, e_r)
+    m_refs = (msend, mrecv, mpre, one_s.at[OUTPUT], m_r)
+    e_refs = (esend, erecv, epre, one_s.at[INPUT], e_r)
 
     def out_block(k, carry):
         row = pl.ds(mo(share_of(k) * length, length), length)
@@ -794,8 +774,7 @@
     lax.fori_loop(0, n, out_block, 0)
     @pl.when(at_home)
     def _():
-        got(zro.at[0], zs_r.at[OUT, 0])
-        got(zro.at[1], zs_r.at[OUT, 1])
+        got(zro.at[pl.ds(0, 2)], zo_r.at[0])
         total = xro[near_b].astype(F32) + zro[0].astype(F32) + zro[1].astype(F32)
         fo[...] = total.astype(BF)
 
@@ -807,8 +786,8 @@
     def o_area(q, h):
         return gout_o.at[lax.rem(q, 2), c, pl.ds(h * oq, oq)]
 
-    plane_send(lambda h: fo.at[pl.ds(h * oq, oq)], o_area, ag1(OUT), ag2(OUT), at_home)
-    start(rc(fo, o_whole(p), agc_s.at[OUT, 0], agc_r.at[OUT, p], partner), at_home)
+    plane_send(lambda h: fo.at[pl.ds(h * oq, oq)], o_area, ag_s.at[OUT], sems(ag_r.at[OUT]), at_home)
+    start(rc(fo, o_whole(p), agc_s.at[OUT], agc_r.at[OUT], partner), at_home)
     cp = pltpu.make_async_copy(fo, o_whole(p), agl.at[OUT])
     pl.when(at_home)(cp.start)
     local_out.append((at_home, cp))
@@ -892,34 +871,36 @@
                 vfull[q * slots + at_g + 2 + 2 * i + h] = vacc[i, :, col]
     for i in range(1, s_n):
         q, dev = line(i)
-        start(rc(vfull.at[pl.ds(q * slots, slots)], vz.at[zz], v1_s.at[i], v1_r.at[zz], dev))
+        start(rc(vfull.at[pl.ds(q * slots, slots)], vz.at[zz], one_s.at[SUMS], one_r.at[1], dev))
 
     pass_on(UP, xru, zru)
 
-    shares_got(mrecv, m_r)
+    got(mrecv, m_r.at[2])
 
     def mixed_rows(i, carry):
         step = 32
         row = pl.ds(mo(i * step, step), step)
         xv = x_all[pl.ds(mo(p * length + i * step, step), step), :].astype(F32)
         t = mown[row, :] + mrecv[0, row, :].astype(F32) + mrecv[1, row, :].astype(F32)
-        mixed_o[row, :] = (xv + t + out_b + down_b).astype(BF)
+        mixed_v[row, :] = (xv + t + out_b + down_b).astype(BF)
         return carry
 
     lax.fori_loop(0, length // 32, mixed_rows, 0)
+    mixed_out = pltpu.make_async_copy(mixed_v, mixed_o, io.at[9])
+    mixed_out.start()
 
     spread_relay(DOWN)
     line_sum(IN, xri, zri, fi)
     spread(IN)
-    def o_got(q, h, cond):
+    def o_got(ref, k, cond):
         @pl.when(cond)
         def _():
-            got(o_area(q, h), ag_r.at[OUT, q, h])
-
-    o_got(xn, 0, at_home)
-    start(rc(o_area(xn, 0), o_area(xn, 0), ag_s.at[OUT, 4], ag_r.at[OUT, xn, 0], dev_y), at_home)
-    o_got(yn, 1, away)
-    start(rc(o_area(yn, 1), o_area(yn, 1), ag_s.at[OUT, 5], ag_r.at[OUT, yn, 1], dev_x), away)
+            got(ref, ag_r.at[OUT, k])
+
+    o_got(o_area(xn, 0), 0, at_home)
+    start(rc(o_area(xn, 0), o_area(xn, 0), ag_s.at[OUT], ag_r.at[OUT, 3], dev_y), at_home)
+    o_got(o_area(yn, 1), 1, away)
+    start(rc(o_area(yn, 1), o_area(yn, 1), ag_s.at[OUT], ag_r.at[OUT, 3], dev_x), away)
     line_sum(UP, xru, zru, fu)
     spread(UP)
 
@@ -928,17 +909,17 @@
     spread_near(DOWN)
     spread_far(DOWN)
     total = [vfull[zz * slots + k] for k in range(slots)]
+    got(vz.at[pl.ds(0, s_n - 1)], one_r.at[1])
     for i in range(1, s_n):
         q, dev = line(i)
-        got(vz.at[q], v1_r.at[q])
         total = [t + vz[q, k] for k, t in enumerate(total)]
     for k in range(slots):
         vu[k] = total[k]
         vr[r, k] = total[k]
     for i in range(1, 2 * n):
-        start(rc(vu, vr.at[r], v2_s.at[i], v2_r.at[r], (lax.rem(r + i, 2 * n), zz)))
-
-    shares_got(erecv, e_r)
+        start(rc(vu, vr.at[r], one_s.at[TOTALS], one_r.at[2], (lax.rem(r + i, 2 * n), zz)))
+
+    got(erecv, e_r.at[2])
 
     def tgrad_rows(i, carry):
         step = 32
@@ -949,52 +930,72 @@
         e = eown[row, :] + erecv[0, row, :].astype(F32) + erecv[1, row, :].astype(F32)
         m0 = jnp.mean(e, axis=1, keepdims=True)
         m1 = jnp.mean(e * xh, axis=1, keepdims=True)
-        tgrad_o[row, :] = g_all[far, :].astype(F32) + inv * (e - m0 - xh * m1)
+        tgrad_v[row, :] = g_all[far, :].astype(F32) + inv * (e - m0 - xh * m1)
         return carry
 
     lax.fori_loop(0, length // 32, tgrad_rows, 0)
+    tgrad_out = pltpu.make_async_copy(tgrad_v, tgrad_o, io.at[10])
+    tgrad_out.start()
 
     spread_relay(UP)
-    o_got(xn, 1, at_home)
-    start(rc(o_whole(xn), o_whole(xn), agc_s.at[OUT, 1], agc_r.at[OUT, xn], partner), at_home)
-    o_got(yn, 0, away)
-    start(rc(o_whole(yn), o_whole(yn), agc_s.at[OUT, 2], agc_r.at[OUT, yn], partner), away)
-    o_got(dg, 0, away)
-    o_got(dg, 1, away)
-    start(rc(o_whole(dg), o_whole(dg), agc_s.at[OUT, 3], agc_r.at[OUT, dg], partner), away)
+    o_got(o_area(xn, 1), 2, at_home)
+    start(rc(o_whole(xn), o_whole(xn), agc_s.at[OUT], agc_r.at[OUT], partner), at_home)
+    o_got(o_area(yn, 0), 2, away)
+    start(rc(o_whole(yn), o_whole(yn), agc_s.at[OUT], agc_r.at[OUT], partner), away)
+    o_got(o_whole(dg), 3, away)
+    start(rc(o_whole(dg), o_whole(dg), agc_s.at[OUT], agc_r.at[OUT], partner), away)
 
     spread_near(IN)
     spread_far(IN)
-    for i in range(1, 2 * n):
-        q = lax.rem(r + i, 2 * n)
-        got(vr.at[q], v2_r.at[q])
+    got(vr.at[pl.ds(0, 2 * n - 1)], one_r.at[2])
     for k in range(slots):
         t = vr[0, k]
         for q in range(1, 2 * n):
             t = t + vr[q, k]
-        vec_o[k] = t
+        vec_v[k] = t
+    vec_out = pltpu.make_async_copy(vec_v, vec_o, io.at[11])
+    vec_out.start()
     spread_near(UP)
     spread_far(UP)
     for t in (DOWN, IN, UP):
         spread_end(t)
-    for q, cond in ((p, at_home), (xn, at_home), (yn, away), (dg, away)):
-
-        @pl.when(cond)
-        def _():
-            got(gout_o.at[lax.rem(q, 2), other], agc_r.at[OUT, q])
+    two = wo.at[pl.ds(0, 2 * ohalf)]
+    got(two, agc_r.at[OUT])
 
     for cond, cp in local_out:
         if cond is None:
             cp.wait()
         else:
             pl.when(cond)(cp.wait)
-    shares_left(*m_refs)
-    shares_left(*e_refs)
-    for cond, cp in sends:
-        if cond is None:
-            cp.wait_send()
-        else:
-            pl.when(cond)(cp.wait_send)
+    for cp in (mixed_out, tgrad_out, vec_out):
+        cp.wait()
+    left(va.at[pl.ds(0, s_n - 1)], one_s.at[VECTORS])
+    left(x_all.at[pl.ds(0, 3 * length)], one_s.at[TOKENS])
+    left(g_all.at[pl.ds(0, 3 * length)], one_s.at[COTANGENTS])
+    left(wo.at[pl.ds(0, 3 * ohalf)], one_s.at[ROWS], at_home)
+    left(msend.at[pl.ds(0, 3)], one_s.at[OUTPUT])
+    left(esend.at[pl.ds(0, 3)], one_s.at[INPUT])
+    left(vz.at[pl.ds(0, s_n - 1)], one_s.at[SUMS])
+    left(vr.at[pl.ds(0, 2 * n - 1)], one_s.at[TOTALS])
+    for t in (IN, UP, DOWN):
+        for h in range(cuts[t]):
+            k = stream[t] + h
+            left(pieces(t, 1), w_s.at[k], is_end)
+            left(pieces(t, 5), w_s.at[k], inner)
+            left(pieces(t, s_n - 1), wc_s.at[k])
+    left(o_piece(0, 0), oc_s.at[0], away)
+    left(o_piece(0, 0), oc_s.at[1])
+    for t, xr in ((IN, xri), (UP, xru), (DOWN, xrd), (OUT, xro)):
+        left(xr, xs_s.at[t])
+    for t, xr in ((IN, xri), (UP, xru), (DOWN, xrd)):
+        left(xr.at[pl.ds(0, 3)], zs_s.at[t])
+        left(outs_of[t][0].at[pl.ds(0, 3), 0], ag_s.at[t])
+        left(outs_of[t][0].at[:, 0], agc_s.at[t])
+    left(xro.at[0], zo_s.at[0])
+    left(xro.at[0], zo_s.at[1], away)
+    left(wo.at[pl.ds(0, 5 * oq)], ag_s.at[OUT], at_home)
+    left(wo.at[pl.ds(0, oq)], ag_s.at[OUT], away)
+    left(two, agc_s.at[OUT])
 
 
 def fused_call(z, tok, cot, inp, upp, outp, downp, vectors):
@@ -1026,15 +1027,12 @@
         V((1, nv), F32), V((s_n, 1, nv), F32), V((1, 3 * width), F32), V((s_n * slots, 1, 128), F32),
         V((s_n, slots, 1, 128), F32), V((slots, 1, 128), F32), V((2 * n, slots, 1, 128), F32),
         V((rows, 2), F32), V((4, 1, width), F32), V((1, iw), F32), V((1, hid), F32),
-        dma(s_n + 10), dma(s_n), dma(s_n), dma(6), dma(n, 2), dma(6), dma(n, 2),
-        dma(3, 2, 2 * s_n), dma(3, 2, s_n), dma(3, 2, 2 * s_n), dma(3, 2, s_n),
-        dma(3), dma(2), dma(2), dma(2),
-        dma(6), dma(6), dma(6), dma(6), dma(4), dma(4), dma(4, 3), dma(4, 4),
-        dma(4, 6), dma(4, n, 2), dma(4, n), dma(4, n), dma(4),
-        dma(s_n), dma(s_n), dma(2 * n), dma(2 * n),
+        dma(6), dma(12), dma(8), dma(3), dma(4), dma(4), dma(4), dma(4, s_n), dma(4), dma(4), dma(2), dma(2), dma(2),
+        dma(3), dma(3), dma(4), dma(4), dma(3), dma(3, 3), dma(2), dma(2), dma(4), dma(4, 4), dma(4), dma(4), dma(4),
+        V((3, length, 128), F32), V((length, width), BF), V((length, width), F32), V((slots, 1, 128), F32),
+        *[V(v.shape, BF) for v in vectors],
     ]
     any_ = pl.BlockSpec(memory_space=pl.ANY)
-    vm = pl.BlockSpec(memory_space=pltpu.VMEM)
     outs = [
         jax.ShapeDtypeStruct((length, width), BF),
         jax.ShapeDtypeStruct((length, width), F32),
@@ -1047,8 +1045,8 @@
     return pl.pallas_call(
         functools.partial(fused, z),
         out_shape=outs,
-        in_specs=[any_] * 6 + [vm] * 9,
-        out_specs=[vm, vm, any_, any_, any_, any_, vm],
+        in_specs=[any_] * 15,
+        out_specs=[any_] * 7,
         scratch_shapes=scratch,
         compiler_params=pltpu.CompilerParams(
             collective_id=0, has_side_effects=True, vmem_limit_bytes=VMEM_LIMIT
@@ -1061,103 +1059,93 @@
     mixed, tgrad, g_in, g_up, g_down, g_out, vec = refs[:7]
     mixed_o, tgrad_o, in_o, up_o, down_o, out_o = refs[7:13]
     vec_o = refs[13:21]
-    m_v, t_v, bi, bu, bd, bo, fi, fu, fd, fo, m_sem, r_sem, w_sem = refs[21:]
+    m_v, t_v, v_v, bi, bu, bd, bo, fi, fu, fd, fo = refs[21:32]
+    vec_v, (io, r_sem, w_sem) = refs[32:40], refs[40:]
     n, s_n, width, span, hb, rs = z.n, z.s, z.d, z.span, z.hb, z.rs
-    half = rs // 2
-    jobs = []
-    for q in range(n):
-        for core in range(2):
-            row = slice(core * half, (core + 1) * half)
-            jobs.append((g_up.at[q, core], bu.at[q, core], fu.at[q, core], [
-                (up_o.at[row, k * hb * n + q * hb : k * hb * n + (q + 1) * hb], slice(k * hb, (k + 1) * hb))
-                for k in range(s_n)
-            ]))
-    for q in range(n):
-        for core in range(2):
-            start = q * hb + core * (hb // 2)
-            jobs.append((g_down.at[q, core], bd.at[q, core], fd.at[q, core], [
-                (down_o.at[start : start + hb // 2], slice(None)),
-            ]))
-    for q in range(n):
-        for core in range(2):
-            row = slice(core * half, (core + 1) * half)
-            jobs.append((g_in.at[q, core], bi.at[q, core], fi.at[q, core], [
-                (
-                    in_o.at[row, k * width + (q + n * h) * 128 : k * width + (q + n * h + 1) * 128],
-                    slice(k * span + h * 128, k * span + (h + 1) * 128),
-                )
-                for k in range(3)
-                for h in range(2)
-            ]))
-    for j in range(2):
-        for core in range(2):
-            start = (2 * j + core) * (span // 4)
-            jobs.append((g_out.at[j, core], bo.at[j, core], fo.at[j, core], [
-                (out_o.at[start : start + span // 4], slice(None)),
-            ]))
+    half, hhalf, quarter = rs // 2, hb // 2, span // 4
     through = [
-        (pltpu.make_async_copy(a, b, m_sem.at[2 * i]), pltpu.make_async_copy(b, o, m_sem.at[2 * i + 1]))
+        (pltpu.make_async_copy(a, b, io.at[i]), pltpu.make_async_copy(b, o, io.at[3 + i]))
         for i, (a, b, o) in enumerate(((mixed, m_v, mixed_o), (tgrad, t_v, tgrad_o)))
     ]
-    reads = [pltpu.make_async_copy(src, dst, r_sem.at[i]) for i, (src, dst, _, _) in enumerate(jobs)]
-    for cp in reads:
+    vec_in = pltpu.make_async_copy(vec, v_v, io.at[2])
+    blocks = []
+    for q in range(n):
+        blocks.append((1, g_up.at[q], bu.at[q], fu.at[q], [
+            (core, up_o.at[core * half : (core + 1) * half, (k * n + q) * hb : (k * n + q + 1) * hb], slice(k * hb, (k + 1) * hb))
+            for core in range(2) for k in range(s_n)
+        ]))
+    for q in range(n):
+        blocks.append((2, g_down.at[q], bd.at[q], fd.at[q], [
+            (core, down_o.at[q * hb + core * hhalf : q * hb + (core + 1) * hhalf], slice(None)) for core in range(2)
+        ]))
+    for q in range(n):
+        blocks.append((0, g_in.at[q], bi.at[q], fi.at[q], [
+            (core, in_o.at[core * half : (core + 1) * half, k * width + (q + n * h) * 128 : k * width + (q + n * h + 1) * 128],
+             slice(k * span + h * 128, k * span + (h + 1) * 128))
+            for core in range(2) for k in range(3) for h in range(2)
+        ]))
+    for j in range(2):
+        blocks.append((3, g_out.at[j], bo.at[j], fo.at[j], [
+            (core, out_o.at[(2 * j + core) * quarter : (2 * j + core + 1) * quarter], slice(None)) for core in range(2)
+        ]))
+    reads = [pltpu.make_async_copy(src, dst, r_sem.at[i]) for i, (_, src, dst, _, _) in enumerate(blocks)]
+    for cp in [reads[0], *(a for a, _ in through), vec_in, *reads[1:]]:
         cp.start()
-    for cp, _ in through:
-        cp.start()
-    writes = []
-    for (_, low, wide, places), read in zip(jobs, reads):
+    for (t, _, low, wide, places), read in zip(blocks, reads):
         read.wait()
-
-        def body(i, carry, low=low, wide=wide):
-            row = pl.ds(mo(i * 32, 32), 32)
-            wide[row, :] = low[row, :].astype(F32)
-            return carry
-
-        lax.fori_loop(0, low.shape[0] // 32, body, 0)
-        for place, col in places:
-            cp = pltpu.make_async_copy(wide.at[:, col], place, w_sem.at[len(writes)])
-            cp.start()
-            writes.append(cp)
+        for core in range(2):
+
+            def body(i, carry, core=core, low=low, wide=wide):
+                row = pl.ds(mo(i * 32, 32), 32)
+                wide[core, row, :] = low[core, row, :].astype(F32)
+                return carry
+
+            lax.fori_loop(0, low.shape[1] // 32, body, 0)
+        for core, place, col in places:
+            pltpu.make_async_copy(wide.at[core, :, col], place, w_sem.at[t]).start()
     for a, b in through:
         a.wait()
         b.start()
+    vec_in.wait()
     k = 0
-    for ref in vec_o:
-        blocks = ref.shape[0] // 128
-        if ref is vec_o[3]:
-            k -= blocks
-        for i in range(blocks):
-            ref[i * 128 : (i + 1) * 128] = vec[k + i].reshape(128)
-        k += blocks
-    for cp in writes:
+    small = []
+    for i, (ref, out) in enumerate(zip(vec_v, vec_o)):
+        count = ref.shape[0] // 128
+        if i == 3:
+            k -= count
+        for j in range(count):
+            ref[j * 128 : (j + 1) * 128] = v_v[k + j].reshape(128)
+        k += count
+        small.append(pltpu.make_async_copy(ref, out, io.at[5 + i]))
+        small[-1].start()
+    for t, wide in enumerate((fi, fu, fd, fo)):
+        pltpu.make_async_copy(wide, wide, w_sem.at[t]).wait()
+    for cp in [b for _, b in through] + small:
         cp.wait()
-    for _, b in through:
-        b.wait()
 
 
 def finish_call(z, pieces):
-    n, width, span = z.n, z.d, z.span
+    n, width, span, rs = z.n, z.d, z.span, z.rs
     V = pltpu.VMEM
     S = jax.ShapeDtypeStruct
     any_ = pl.BlockSpec(memory_space=pl.ANY)
-    vm = pl.BlockSpec(memory_space=pltpu.VMEM)
-    rs = z.rs
+    small = [3 * width // z.s, z.hb * n] + [rs] * 6
     outs = [
         S((z.l, width), BF), S((z.l, width), F32), S((rs, 3 * width), F32), S((rs, z.ff), F32),
-        S((z.hb * n, width), F32), S((span, width), F32),
-        S((3 * width // z.s,), F32), S((z.hb * n,), F32), *[S((rs,), F32)] * 6,
+        S((z.hb * n, width), F32), S((span, width), F32), *[S((k,), F32) for k in small],
     ]
     shapes = [p.shape for p in pieces[2:6]]
     dma = lambda k: pltpu.SemaphoreType.DMA((k,))
     return pl.pallas_call(
         functools.partial(finish, z),
         out_shape=outs,
-        in_specs=[any_] * 6 + [vm],
-        out_specs=[any_] * 6 + [vm] * 8,
+        in_specs=[any_] * 7,
+        out_specs=[any_] * 14,
         scratch_shapes=[
-            V((z.l, width), BF), V((z.l, width), F32),
+            V((z.l, width), BF), V((z.l, width), F32), V(pieces[6].shape, F32),
             *[V(s, BF) for s in shapes], *[V(s, F32) for s in shapes],
-            dma(4), dma(6 * n + 4), dma(2 * n * (z.s + 7) + 4),
+            *[V((k,), F32) for k in small],
+            dma(13), dma(3 * n + 2), dma(4),
         ],
         compiler_params=pltpu.CompilerParams(vmem_limit_bytes=VMEM_LIMIT),
         name="finish",

time: 143 us -> 137 us (0.958)
  Pallas kernels: 142 us -> 136 us
    pallas_call x1, Pallas kernels: 132 us -> 129 us  [fused_call(): pl.pallas_call(functools.partial(fused, z), out_shape=outs, in_specs=[any...]
    pallas_call x1, Pallas kernels: 9.81 us -> 7.67 us  [finish_call(): pl.pallas_call(functools.partial(finish, z), out_shape=outs, in_specs=[an...]
where the time goes in v6:
time: 137 us
  Pallas kernels  136 us (99%)
    pallas_call x1, Pallas kernels, fused_call(): pl.pallas_call(functools.partial(fused, z), out_shape=outs, in_specs=[any...  129 us
    pallas_call x1, Pallas kernels, finish_call(): pl.pallas_call(functools.partial(finish, z), out_shape=outs, in_specs=[an...  7.67 us

profile of v6, /device:TPU:0, one launch (start us, length us, event | category | flops | bytes accessed | tf_op | source)
XLA Modules:
  0.0 137.1 jit_solution(1606532257632557635)
XLA Ops:
  0.7 128.6 %block_step.1 = (bf16[256,1024]{1,0:T(8,128)(2,1)}, f32[256,1024]{1,0:T(8,128)}, bf16[4,2,128,768]{3,2,1,0:T(8,128)(2,1)}, bf16[4,2,128,1024]{3,2,1,0:T(8,128)(2...) custom-call(bf16[256,1024]{1,0:T(8,128)(2,1)} %refs_0_.1, ...), custom_call_target="tpu_custom_call" | custom-call | tf_op jit(solution)/shard_map/block_step/pallas_call | solution.py:1045
  129.2 7.7 %finish.1 = (bf16[256,1024]{1,0:T(8,128)(2,1)}, f32[256,1024]{1,0:T(8,128)}, f32[256,3072]{1,0:T(8,128)}, f32[256,4096]{1,0:T(8,128)}, f32[1024,1024]{1,0:T(8,12...) custom-call(bf16[256,1024]{1,0:T(8,128)(2,1)} %get-tuple-element.35., ...), custom_call_target="tpu_custom_call" | custom-call | tf_op jit(solution)/shard_map/finish/pallas_call | solution.py:1139

commit v7 on v6

--- a/solution.py
+++ b/solution.py
@@ -335,13 +335,6 @@
     for cp in local_v + local_i + [local_x] + local_u + [local_g, local_d, local_r]:
         cp.start()
     pl.when(at_home)(local_o.start)
-    off = 0
-    for ref, cp in zip(vectors_v, local_v):
-        cp.wait()
-        size = ref.shape[0]
-        vec[:, off : off + size] = ref[...].astype(F32).reshape(1, size)
-        off += size
-
     barrier = pltpu.get_barrier_semaphore()
     for i in range(1, 2 * n):
         pl.semaphore_signal(
@@ -349,6 +342,12 @@
         )
     for i in range(1, s_n):
         pl.semaphore_signal(barrier, 1, device_id=(r, lax.rem(zz + i, s_n)), device_id_type=MESH)
+    off = 0
+    for ref, cp in zip(vectors_v, local_v):
+        cp.wait()
+        size = ref.shape[0]
+        vec[:, off : off + size] = ref[...].astype(F32).reshape(1, size)
+        off += size
     pl.semaphore_wait(barrier, 2 * n - 1 + s_n - 1)
 
     def line(i):
@@ -550,9 +549,10 @@
 
     lax.fori_loop(0, n * pairs // 2, att_forward, 0)
     relay(DOWN, d_piece, 1, inner)
+    for d in range(1, s_n - 1):
+        relay(UP, u_piece, d, is_end)
     lax.fori_loop(n * pairs // 2, n * pairs, att_forward, 0)
-    for d in range(1, s_n):
-        relay(UP, u_piece, d, is_end)
+    relay(UP, u_piece, s_n - 1, is_end)
     relay_done(UP)
 
     def up_block(s, carry):
@@ -726,10 +726,11 @@
         xro[far_b] = (xro[far_b].astype(F32) + zro[2].astype(F32)).astype(BF)
         on.start()
 
+    for d in range(1, s_n - 1):
+        relay(DOWN, d_piece, d, is_end)
     lax.fori_loop(n * pairs - 4, n * pairs - 2, att_backward, 0)
 
-    for d in range(1, s_n):
-        relay(DOWN, d_piece, d, is_end)
+    relay(DOWN, d_piece, s_n - 1, is_end)
     relay_done(DOWN)
 
     def shares(k, send, recv, pre, ss, rr):
@@ -778,15 +779,11 @@
         total = xro[near_b].astype(F32) + zro[0].astype(F32) + zro[1].astype(F32)
         fo[...] = total.astype(BF)
 
-    oq = ohalf // 2
-
     def o_whole(q):
         return gout_o.at[lax.rem(q, 2), c]
 
-    def o_area(q, h):
-        return gout_o.at[lax.rem(q, 2), c, pl.ds(h * oq, oq)]
-
-    plane_send(lambda h: fo.at[pl.ds(h * oq, oq)], o_area, ag_s.at[OUT], sems(ag_r.at[OUT]), at_home)
+    start(rc(fo, o_whole(p), ag_s.at[OUT], ag_r.at[OUT, 0], dev_x), at_home)
+    start(rc(fo, o_whole(p), ag_s.at[OUT], ag_r.at[OUT, 1], dev_y), at_home)
     start(rc(fo, o_whole(p), agc_s.at[OUT], agc_r.at[OUT], partner), at_home)
     cp = pltpu.make_async_copy(fo, o_whole(p), agl.at[OUT])
     pl.when(at_home)(cp.start)
@@ -897,10 +894,8 @@
         def _():
             got(ref, ag_r.at[OUT, k])
 
-    o_got(o_area(xn, 0), 0, at_home)
-    start(rc(o_area(xn, 0), o_area(xn, 0), ag_s.at[OUT], ag_r.at[OUT, 3], dev_y), at_home)
-    o_got(o_area(yn, 1), 1, away)
-    start(rc(o_area(yn, 1), o_area(yn, 1), ag_s.at[OUT], ag_r.at[OUT, 3], dev_x), away)
+    o_got(o_whole(yn), 1, away)
+    start(rc(o_whole(yn), o_whole(yn), ag_s.at[OUT], ag_r.at[OUT, 2], dev_x), away)
     line_sum(UP, xru, zru, fu)
     spread(UP)
 
@@ -938,13 +933,13 @@
     tgrad_out.start()
 
     spread_relay(UP)
-    o_got(o_area(xn, 1), 2, at_home)
+    o_got(o_whole(xn), 0, at_home)
     start(rc(o_whole(xn), o_whole(xn), agc_s.at[OUT], agc_r.at[OUT], partner), at_home)
-    o_got(o_area(yn, 0), 2, away)
     start(rc(o_whole(yn), o_whole(yn), agc_s.at[OUT], agc_r.at[OUT], partner), away)
-    o_got(o_whole(dg), 3, away)
+    o_got(o_whole(dg), 2, away)
     start(rc(o_whole(dg), o_whole(dg), agc_s.at[OUT], agc_r.at[OUT], partner), away)
 
+    spread_near(UP)
     spread_near(IN)
     spread_far(IN)
     got(vr.at[pl.ds(0, 2 * n - 1)], one_r.at[2])
@@ -955,7 +950,6 @@
         vec_v[k] = t
     vec_out = pltpu.make_async_copy(vec_v, vec_o, io.at[11])
     vec_out.start()
-    spread_near(UP)
     spread_far(UP)
     for t in (DOWN, IN, UP):
         spread_end(t)
@@ -993,8 +987,8 @@
         left(outs_of[t][0].at[:, 0], agc_s.at[t])
     left(xro.at[0], zo_s.at[0])
     left(xro.at[0], zo_s.at[1], away)
-    left(wo.at[pl.ds(0, 5 * oq)], ag_s.at[OUT], at_home)
-    left(wo.at[pl.ds(0, oq)], ag_s.at[OUT], away)
+    left(two, ag_s.at[OUT], at_home)
+    left(wo.at[pl.ds(0, ohalf)], ag_s.at[OUT], away)
     left(two, agc_s.at[OUT])
 
 

time: 137 us -> 137 us (level); the launches traced: 137 us -> 136 us
    pallas_call x1, Pallas kernels: 129 us -> 127 us  [fused_call(): pl.pallas_call(functools.partial(fused, z), out_shape=outs, in_specs=[any...]
where the time goes in v7:
time: 137 us; the launch traced here: 136 us
  Pallas kernels  135 us (99%)
    pallas_call x1, Pallas kernels, fused_call(): pl.pallas_call(functools.partial(fused, z), out_shape=outs, in_specs=[any...  127 us
    pallas_call x1, Pallas kernels, finish_call(): pl.pallas_call(functools.partial(finish, z), out_shape=outs, in_specs=[an...  7.67 us

profile of v7, /device:TPU:0, one launch (start us, length us, event | category | flops | bytes accessed | tf_op | source)
XLA Modules:
  0.0 135.6 jit_solution(8757579261014528473)
XLA Ops:
  0.7 127.1 %block_step.1 = (bf16[256,1024]{1,0:T(8,128)(2,1)}, f32[256,1024]{1,0:T(8,128)}, bf16[4,2,128,768]{3,2,1,0:T(8,128)(2,1)}, bf16[4,2,128,1024]{3,2,1,0:T(8,128)(2...) custom-call(bf16[256,1024]{1,0:T(8,128)(2,1)} %refs_0_.1, ...), custom_call_target="tpu_custom_call" | custom-call | tf_op jit(solution)/shard_map/block_step/pallas_call | solution.py:1039
  127.8 7.7 %finish.1 = (bf16[256,1024]{1,0:T(8,128)(2,1)}, f32[256,1024]{1,0:T(8,128)}, f32[256,3072]{1,0:T(8,128)}, f32[256,4096]{1,0:T(8,128)}, f32[1024,1024]{1,0:T(8,12...) custom-call(bf16[256,1024]{1,0:T(8,128)(2,1)} %get-tuple-element.35., ...), custom_call_target="tpu_custom_call" | custom-call | tf_op jit(solution)/shard_map/finish/pallas_call | solution.py:1133
